TPU v7x, 32 devices: a whole 2x2x4 slice. The times are simulated.
32 devices in a mesh: seq: 4 (over y, core), fsdp: 8 (over z, x).
Axes of the slice: x: 2, y: 2, z: 4, core: 2. Of those that a mesh axis runs over, the one named last changes fastest.
Arguments:
- hidden: bfloat16 [16, 384, 1536], P('fsdp', 'seq'), may hold values from -6 to 6
- text: bfloat16 [16, 512, 1536], P('fsdp', 'seq'), may hold values from -6 to 6
- time_emb: bfloat16 [16, 6, 1536], P('fsdp'), may hold values from -3 to 3
- modulation: bfloat16 [6, 1536], P(None, 'fsdp'), may hold values from -3 to 3
- self_in: bfloat16 [3, 1536, 1536], P(None, 'fsdp'), may hold values from -0.15625 to 0.15625
- self_out: bfloat16 [1536, 1536], P('fsdp'), may hold values from -0.625 to 0.625
- cross_in: bfloat16 [3, 1536, 1536], P(None, 'fsdp'), may hold values from -0.15625 to 0.15625
- cross_out: bfloat16 [1536, 1536], P('fsdp'), may hold values from -0.625 to 0.625
- ffn_in: bfloat16 [1536, 8960], P('fsdp'), may hold values from -0.15625 to 0.15625
- ffn_out: bfloat16 [8960, 1536], P('fsdp'), may hold values from -0.0625 to 0.0625
- gains: bfloat16 [5, 1536], P(None, 'fsdp'), may hold values from 0.5 to 1.5
- biases: bfloat16 [10, 1536], P(None, 'fsdp'), may hold values from -2 to 2
- ffn_bias: bfloat16 [8960], P('fsdp'), may hold values from -2 to 2
- positions: int32 [16, 3, 384], P('fsdp', None, 'seq'), may hold values from 0 to 63
- cotangent: bfloat16 [16, 384, 1536], P('fsdp', 'seq'), may hold values from -6 to 6
Outputs:
- mixed: bfloat16 [16, 384, 1536], P('fsdp', 'seq')
- grad_hidden: float32 [16, 384, 1536], P('fsdp', 'seq')
- grad_text: float32 [16, 512, 1536], P('fsdp', 'seq')
- grad_time: float32 [16, 6, 1536], P('fsdp')
- grad_modulation: float32 [6, 1536], P(None, 'fsdp')
- grad_self_in: float32 [3, 1536, 1536], P(None, 'fsdp')
- grad_self_out: float32 [1536, 1536], P('fsdp')
- grad_cross_in: float32 [3, 1536, 1536], P(None, 'fsdp')
- grad_cross_out: float32 [1536, 1536], P('fsdp')
- grad_ffn_in: float32 [1536, 8960], P('fsdp')
- grad_ffn_out: float32 [8960, 1536], P('fsdp')
- grad_gains: float32 [5, 1536], P(None, 'fsdp')
- grad_biases: float32 [10, 1536], P(None, 'fsdp')
- grad_ffn_bias: float32 [8960], P('fsdp')
All inputs are finite; a program needn't handle non-finite values.
Results may differ from a plain program's by a relative error of at most 0.022.
Values may be sent and summed in bfloat16 or wider, within the bound.
A program may use at most 304 MiB of HBM per device.

v0:
```python
import jax
import jax.numpy as jnp
from jax import lax
from jax.sharding import PartitionSpec as P

HEADS = 12
HEAD = 128


EPSILON = 1e-06


def matmul(operand, factor):
    return jnp.dot(operand, factor, preferred_element_type=jnp.float32)


def inner_rows(operand, factor):
    return lax.dot_general(
        operand, factor, (((0,), (0,)), ((), ())), preferred_element_type=jnp.float32
    )


def outer_cols(operand, factor):
    return lax.dot_general(
        operand, factor, (((1,), (1,)), ((), ())), preferred_element_type=jnp.float32
    )


def column_sums(tensor):
    return jnp.sum(tensor.astype(jnp.float32), axis=0)


def layer_norm(tensor):
    centered = tensor - jnp.mean(tensor, axis=-1, keepdims=True)
    return centered * lax.rsqrt(jnp.mean(centered * centered, axis=-1, keepdims=True) + EPSILON)


def rms_norm(tensor, weight):
    return tensor * lax.rsqrt(jnp.mean(tensor * tensor, axis=-1, keepdims=True) + EPSILON) * weight


def modulate_norm(tensor, shift, scale):
    return layer_norm(tensor) * (1.0 + scale) + shift


def affine_norm(tensor, weight, offset):
    return layer_norm(tensor) * weight + offset


def gelu_tanh(tensor):
    return jax.nn.gelu(tensor, approximate=True)


def rotary_tables(places, head_size, head_count):
    one_sixth = head_size // 6
    span_sizes = (head_size - 4 * one_sixth, 2 * one_sixth, 2 * one_sixth)
    angles = []
    for component in range(3):
        exponents = (
            jnp.arange(0, span_sizes[component], 2, dtype=jnp.float32) / span_sizes[component]
        )
        frequency = 1.0 / 10000.0**exponents
        angles.append(places[component].astype(jnp.float32)[:, None] * frequency[None, :])
    joined = jnp.concatenate(angles, axis=1)
    tiled_angles = jnp.tile(jnp.repeat(joined, 2, axis=1), (1, head_count))
    parity = jnp.where(jnp.arange(tiled_angles.shape[1]) % 2 == 0, -1.0, 1.0)
    return (jnp.cos(tiled_angles), jnp.sin(tiled_angles) * parity)


def rotate(tensor, cosine, signed_sine):
    even_lane = jnp.arange(tensor.shape[1]) % 2 == 0
    swapped = jnp.where(even_lane, jnp.roll(tensor, -1, axis=1), jnp.roll(tensor, 1, axis=1))
    return tensor * cosine + swapped * signed_sine


def split_heads(tensor):
    return tensor.reshape(tensor.shape[0], tensor.shape[1] // HEAD, HEAD)


def attend(queries, key_rows, value_rows):
    scores = jnp.einsum(
        "qhd,khd->hqk",
        split_heads(queries),
        split_heads(key_rows),
        preferred_element_type=jnp.float32,
    ) * HEAD ** (-0.5)
    row_max = jnp.max(scores, axis=-1, keepdims=True)
    exponentials = jnp.exp(scores - row_max)
    row_total = jnp.sum(exponentials, axis=-1, keepdims=True)
    probabilities = (exponentials / row_total).astype(jnp.bfloat16)
    result = jnp.einsum(
        "hqk,khd->qhd", probabilities, split_heads(value_rows), preferred_element_type=jnp.float32
    )
    return (result.reshape(queries.shape[0], -1).astype(jnp.bfloat16), row_max + jnp.log(row_total))


def attend_back(queries, key_rows, value_rows, log_total, grad_rows):
    query_split = split_heads(queries)
    key_split = split_heads(key_rows)
    grad_split = split_heads(grad_rows)
    scale_factor = HEAD ** (-0.5)
    scores = (
        jnp.einsum("qhd,khd->hqk", query_split, key_split, preferred_element_type=jnp.float32)
        * scale_factor
    )
    probs_full = jnp.exp(scores - log_total)
    probs_low = probs_full.astype(jnp.bfloat16)
    grad_values = jnp.einsum(
        "hqk,qhd->khd", probs_low, grad_split, preferred_element_type=jnp.float32
    )
    grad_probs = jnp.einsum(
        "qhd,khd->hqk", grad_split, split_heads(value_rows), preferred_element_type=jnp.float32
    )
    grad_scores = (
        probs_full * (grad_probs - jnp.sum(grad_probs * probs_full, axis=-1, keepdims=True))
    ).astype(jnp.bfloat16)
    grad_queries = (
        jnp.einsum("hqk,khd->qhd", grad_scores, key_split, preferred_element_type=jnp.float32)
        * scale_factor
    )
    grad_keys = (
        jnp.einsum("hqk,qhd->khd", grad_scores, query_split, preferred_element_type=jnp.float32)
        * scale_factor
    )
    return (
        grad_queries.reshape(queries.shape[0], -1),
        grad_keys.reshape(key_rows.shape[0], -1),
        grad_values.reshape(value_rows.shape[0], -1),
    )


def fetch_weights(
    modulation, self_in, self_out, cross_in, cross_out, ffn_in, ffn_out, gains, biases, ffn_bias
):
    return (
        lax.all_gather(modulation, "fsdp", axis=1, tiled=True),
        lax.all_gather(self_in, "fsdp", axis=1, tiled=True),
        lax.all_gather(self_out, "fsdp", axis=0, tiled=True),
        lax.all_gather(cross_in, "fsdp", axis=1, tiled=True),
        lax.all_gather(cross_out, "fsdp", axis=0, tiled=True),
        lax.all_gather(ffn_in, "fsdp", axis=0, tiled=True),
        lax.all_gather(ffn_out, "fsdp", axis=0, tiled=True),
        lax.all_gather(gains, "fsdp", axis=1, tiled=True),
        lax.all_gather(biases, "fsdp", axis=1, tiled=True),
        lax.all_gather(ffn_bias, "fsdp", axis=0, tiled=True),
    )


def micro_step(weights, hidden, text, time_emb, places, cotangent):
    modulation, self_in, self_out, cross_in, cross_out, ffn_in, ffn_out, gains, biases, ffn_bias = (
        weights
    )
    gain_rows = gains.astype(jnp.float32)
    bias_rows = biases.astype(jnp.float32)
    modulated = modulation.astype(jnp.float32) + time_emb.astype(jnp.float32)
    cosine, signed_sine = rotary_tables(places, HEAD, HEADS)
    residual_in = hidden.astype(jnp.float32)
    normed_full, pull_first = jax.vjp(modulate_norm, residual_in, modulated[0], modulated[1])
    normed = normed_full.astype(jnp.bfloat16)
    query_pre = matmul(normed, self_in[0]) + bias_rows[0]
    key_pre = matmul(normed, self_in[1]) + bias_rows[1]
    value_low = (matmul(normed, self_in[2]) + bias_rows[2]).astype(jnp.bfloat16)

    def turn_both(query_input, key_input, gain_query, gain_key):
        return (
            rotate(rms_norm(query_input, gain_query), cosine, signed_sine),
            rotate(rms_norm(key_input, gain_key), cosine, signed_sine),
        )

    turned, pull_turn = jax.vjp(turn_both, query_pre, key_pre, gain_rows[0], gain_rows[1])
    query_heads, key_heads, value_heads = (
        lax.all_to_all(
            turned[0].astype(jnp.bfloat16), "seq", split_axis=1, concat_axis=0, tiled=True
        ),
        lax.all_to_all(
            turned[1].astype(jnp.bfloat16), "seq", split_axis=1, concat_axis=0, tiled=True
        ),
        lax.all_to_all(value_low, "seq", split_axis=1, concat_axis=0, tiled=True),
    )
    attn_heads, log_total = attend(query_heads, key_heads, value_heads)
    attended = lax.all_to_all(attn_heads, "seq", split_axis=0, concat_axis=1, tiled=True)
    branch = matmul(attended, self_out) + bias_rows[3]
    after_attn = residual_in + branch * modulated[2]
    crossed_full, pull_cross = jax.vjp(affine_norm, after_attn, gain_rows[4], bias_rows[8])
    crossed = crossed_full.astype(jnp.bfloat16)
    cross_query_pre = matmul(crossed, cross_in[0]) + bias_rows[4]
    cross_query_full, pull_cross_query = jax.vjp(rms_norm, cross_query_pre, gain_rows[2])
    cross_query = cross_query_full.astype(jnp.bfloat16)
    text_key_pre = matmul(text, cross_in[1]) + bias_rows[5]
    text_key_full, pull_text_key = jax.vjp(rms_norm, text_key_pre, gain_rows[3])
    text_value = (matmul(text, cross_in[2]) + bias_rows[6]).astype(jnp.bfloat16)
    key_all, value_all = (
        lax.all_gather(text_key_full.astype(jnp.bfloat16), "seq", axis=0, tiled=True),
        lax.all_gather(text_value, "seq", axis=0, tiled=True),
    )
    cross_rows, cross_total = attend(cross_query, key_all, value_all)
    second = after_attn + matmul(cross_rows, cross_out) + bias_rows[7]
    ffn_normed_full, pull_second = jax.vjp(modulate_norm, second, modulated[3], modulated[4])
    ffn_normed = ffn_normed_full.astype(jnp.bfloat16)
    pre_act = matmul(ffn_normed, ffn_in) + ffn_bias.astype(jnp.float32)
    activation_full, pull_gelu = jax.vjp(gelu_tanh, pre_act)
    activation = activation_full.astype(jnp.bfloat16)
    ffn_branch = matmul(activation, ffn_out) + bias_rows[9]
    mixed = (second + ffn_branch * modulated[5]).astype(jnp.bfloat16)
    grad_output = cotangent.astype(jnp.float32)
    gate_ffn = jnp.sum(grad_output * ffn_branch, axis=0)
    grad_ffn_branch = (grad_output * modulated[5]).astype(jnp.bfloat16)
    weight_ffn_out = inner_rows(activation, grad_ffn_branch)
    grad_pre_full = pull_gelu(outer_cols(grad_ffn_branch, ffn_out))[0]
    grad_pre = grad_pre_full.astype(jnp.bfloat16)
    weight_ffn_in = inner_rows(ffn_normed, grad_pre)
    grad_second_part, shift_ffn, scale_ffn = pull_second(outer_cols(grad_pre, ffn_in))
    grad_second = grad_output + grad_second_part
    grad_cross_branch = grad_second.astype(jnp.bfloat16)
    weight_cross_out = inner_rows(cross_rows, grad_cross_branch)
    grad_cross_rows = outer_cols(grad_cross_branch, cross_out).astype(jnp.bfloat16)
    grad_cross_query, grad_key_all, grad_value_all = attend_back(
        cross_query, key_all, value_all, cross_total, grad_cross_rows
    )
    grad_text_key, grad_text_value_full = (
        lax.psum_scatter(
            grad_key_all.astype(jnp.bfloat16), "seq", scatter_dimension=0, tiled=True
        ).astype(jnp.float32),
        lax.psum_scatter(
            grad_value_all.astype(jnp.bfloat16), "seq", scatter_dimension=0, tiled=True
        ).astype(jnp.float32),
    )
    grad_text_value = grad_text_value_full.astype(jnp.bfloat16)
    grad_text_key_full, gain_cross_key = pull_text_key(grad_text_key)
    grad_text_key_pre = grad_text_key_full.astype(jnp.bfloat16)
    weight_cross_key = inner_rows(text, grad_text_key_pre)
    weight_cross_value = inner_rows(text, grad_text_value)
    grad_words = outer_cols(grad_text_key_pre, cross_in[1]) + outer_cols(
        grad_text_value, cross_in[2]
    )
    grad_cross_query_full, gain_cross_query = pull_cross_query(grad_cross_query)
    grad_cross_query_pre = grad_cross_query_full.astype(jnp.bfloat16)
    weight_cross_query = inner_rows(crossed, grad_cross_query_pre)
    grad_after_part, gain_norm, bias_norm = pull_cross(
        outer_cols(grad_cross_query_pre, cross_in[0])
    )
    grad_after = grad_second + grad_after_part
    gate_attn = jnp.sum(grad_after * branch, axis=0)
    grad_branch = (grad_after * modulated[2]).astype(jnp.bfloat16)
    weight_self_out = inner_rows(attended, grad_branch)
    grad_attended = outer_cols(grad_branch, self_out).astype(jnp.bfloat16)
    grad_attn_heads = lax.all_to_all(grad_attended, "seq", split_axis=1, concat_axis=0, tiled=True)
    grad_query_heads, grad_key_heads, grad_value_heads = attend_back(
        query_heads, key_heads, value_heads, log_total, grad_attn_heads
    )
    grad_query_turned, grad_key_turned, grad_value = (
        lax.all_to_all(
            grad_query_heads.astype(jnp.bfloat16), "seq", split_axis=0, concat_axis=1, tiled=True
        ),
        lax.all_to_all(
            grad_key_heads.astype(jnp.bfloat16), "seq", split_axis=0, concat_axis=1, tiled=True
        ),
        lax.all_to_all(
            grad_value_heads.astype(jnp.bfloat16), "seq", split_axis=0, concat_axis=1, tiled=True
        ),
    )
    grad_query_full, grad_key_full, gain_query, gain_key = pull_turn(
        (grad_query_turned.astype(jnp.float32), grad_key_turned.astype(jnp.float32))
    )
    grad_query_pre = grad_query_full.astype(jnp.bfloat16)
    grad_key_pre = grad_key_full.astype(jnp.bfloat16)
    weight_self_query = inner_rows(normed, grad_query_pre)
    weight_self_key = inner_rows(normed, grad_key_pre)
    weight_self_value = inner_rows(normed, grad_value)
    grad_normed = (
        outer_cols(grad_query_pre, self_in[0])
        + outer_cols(grad_key_pre, self_in[1])
        + outer_cols(grad_value, self_in[2])
    )
    grad_start, shift_attn, scale_attn = pull_first(grad_normed)
    grad_hidden = grad_after + grad_start
    grad_modulated = jnp.stack((shift_attn, scale_attn, gate_attn, shift_ffn, scale_ffn, gate_ffn))
    grad_gains = jnp.stack((gain_query, gain_key, gain_cross_query, gain_cross_key, gain_norm))
    grad_biases = jnp.stack(
        (
            column_sums(grad_query_pre),
            column_sums(grad_key_pre),
            column_sums(grad_value),
            column_sums(grad_branch),
            column_sums(grad_cross_query_pre),
            column_sums(grad_text_key_pre),
            column_sums(grad_text_value),
            column_sums(grad_cross_branch),
            bias_norm,
            column_sums(grad_ffn_branch),
        )
    )
    gradients = (
        grad_modulated,
        jnp.stack((weight_self_query, weight_self_key, weight_self_value)),
        weight_self_out,
        jnp.stack((weight_cross_query, weight_cross_key, weight_cross_value)),
        weight_cross_out,
        weight_ffn_in,
        weight_ffn_out,
        grad_gains,
        grad_biases,
        column_sums(grad_pre),
    )
    return (mixed, grad_hidden, grad_words, grad_modulated, gradients)


def body(
    hidden,
    text,
    time_emb,
    modulation,
    self_in,
    self_out,
    cross_in,
    cross_out,
    ffn_in,
    ffn_out,
    gains,
    biases,
    ffn_bias,
    positions,
    cotangent,
):
    mixed_list = []
    hidden_list = []
    words_list = []
    clock_list = []
    totals = None
    for batch_index in range(hidden.shape[0]):
        weights = fetch_weights(
            modulation,
            self_in,
            self_out,
            cross_in,
            cross_out,
            ffn_in,
            ffn_out,
            gains,
            biases,
            ffn_bias,
        )
        mixed, grad_hidden, grad_words, grad_clock, grads = micro_step(
            weights,
            hidden[batch_index],
            text[batch_index],
            time_emb[batch_index],
            positions[batch_index],
            cotangent[batch_index],
        )
        mixed_list.append(mixed)
        hidden_list.append(grad_hidden)
        words_list.append(grad_words)
        clock_list.append(grad_clock)
        if totals is None:
            totals = tuple(grads)
        else:
            totals = tuple((earlier + later for earlier, later in zip(totals, grads)))
    grad_time = jnp.stack(clock_list)
    owned = (
        lax.psum_scatter(
            totals[0].astype(jnp.bfloat16), "fsdp", scatter_dimension=1, tiled=True
        ).astype(jnp.float32),
        lax.psum_scatter(
            totals[1].astype(jnp.bfloat16), "fsdp", scatter_dimension=1, tiled=True
        ).astype(jnp.float32),
        lax.psum_scatter(
            totals[2].astype(jnp.bfloat16), "fsdp", scatter_dimension=0, tiled=True
        ).astype(jnp.float32),
        lax.psum_scatter(
            totals[3].astype(jnp.bfloat16), "fsdp", scatter_dimension=1, tiled=True
        ).astype(jnp.float32),
        lax.psum_scatter(
            totals[4].astype(jnp.bfloat16), "fsdp", scatter_dimension=0, tiled=True
        ).astype(jnp.float32),
        lax.psum_scatter(
            totals[5].astype(jnp.bfloat16), "fsdp", scatter_dimension=0, tiled=True
        ).astype(jnp.float32),
        lax.psum_scatter(
            totals[6].astype(jnp.bfloat16), "fsdp", scatter_dimension=0, tiled=True
        ).astype(jnp.float32),
        lax.psum_scatter(
            totals[7].astype(jnp.bfloat16), "fsdp", scatter_dimension=1, tiled=True
        ).astype(jnp.float32),
        lax.psum_scatter(
            totals[8].astype(jnp.bfloat16), "fsdp", scatter_dimension=1, tiled=True
        ).astype(jnp.float32),
        lax.psum_scatter(
            totals[9].astype(jnp.bfloat16), "fsdp", scatter_dimension=0, tiled=True
        ).astype(jnp.float32),
    )
    summed = (
        lax.psum(owned[0].astype(jnp.bfloat16), "seq").astype(jnp.float32),
        lax.psum(owned[1].astype(jnp.bfloat16), "seq").astype(jnp.float32),
        lax.psum(owned[2].astype(jnp.bfloat16), "seq").astype(jnp.float32),
        lax.psum(owned[3].astype(jnp.bfloat16), "seq").astype(jnp.float32),
        lax.psum(owned[4].astype(jnp.bfloat16), "seq").astype(jnp.float32),
        lax.psum(owned[5].astype(jnp.bfloat16), "seq").astype(jnp.float32),
        lax.psum(owned[6].astype(jnp.bfloat16), "seq").astype(jnp.float32),
        lax.psum(owned[7].astype(jnp.bfloat16), "seq").astype(jnp.float32),
        lax.psum(owned[8].astype(jnp.bfloat16), "seq").astype(jnp.float32),
        lax.psum(owned[9].astype(jnp.bfloat16), "seq").astype(jnp.float32),
        lax.psum(grad_time.astype(jnp.bfloat16), "seq").astype(jnp.float32),
    )
    finals = summed[:10]
    grad_time = summed[10]
    return (
        jnp.stack(mixed_list),
        jnp.stack(hidden_list),
        jnp.stack(words_list),
        grad_time,
        finals[0],
        finals[1],
        finals[2],
        finals[3],
        finals[4],
        finals[5],
        finals[6],
        finals[7],
        finals[8],
        finals[9],
    )


def solution(mesh):
    return jax.shard_map(
        body,
        mesh=mesh,
        in_specs=(
            P("fsdp", "seq", None),
            P("fsdp", "seq", None),
            P("fsdp", None, None),
            P(None, "fsdp"),
            P(None, "fsdp", None),
            P("fsdp", None),
            P(None, "fsdp", None),
            P("fsdp", None),
            P("fsdp", None),
            P("fsdp", None),
            P(None, "fsdp"),
            P(None, "fsdp"),
            P("fsdp"),
            P("fsdp", None, "seq"),
            P("fsdp", "seq", None),
        ),
        out_specs=(
            P("fsdp", "seq", None),
            P("fsdp", "seq", None),
            P("fsdp", "seq", None),
            P("fsdp", None, None),
            P(None, "fsdp"),
            P(None, "fsdp", None),
            P("fsdp", None),
            P(None, "fsdp", None),
            P("fsdp", None),
            P("fsdp", None),
            P("fsdp", None),
            P(None, "fsdp"),
            P(None, "fsdp"),
            P("fsdp"),
        ),
        check_vma=False,
    )
```

profile of v0, /device:TPU:0, one launch (start us, length us, event | category | flops | bytes accessed | tf_op | source)
XLA Modules:
  0.0 3923.6 jit_solution(2890474537820594167)
XLA Ops:
  9.5 33.2 all-gather.1
  43.5 165.0 %all-gather.18.cloned.1.call-done = bf16[3,1536,1536]{2,1,0:T(8,128)(2,1)} async-done(((bf16[3,192,1536]{2,1,0:T(8,128)(2,1)}), bf16[3,1536,1536]{2,1,0:T(8,128)(2,1)}) %all-gather.18.cloned.1.call-update) | async-done | bytes 14155792 | tf_op jit(solution)/shard_map/all_gather | solution.py:139
  216.4 31.8 all-gather.2
  259.9 31.4 all-gather
  298.0 106.7 %all-gather.14.cloned.1.call-done = bf16[3,1536,1536]{2,1,0:T(8,128)(2,1)} async-done(((bf16[3,192,1536]{2,1,0:T(8,128)(2,1)}), bf16[3,1536,1536]{2,1,0:T(8,128)(2,1)}) %all-gather.14.cloned.1.call-update) | async-done | bytes 14155792 | tf_op jit(solution)/shard_map/all_gather | solution.py:137
  503.9 33.2 all-reduce.16
  579.4 74.3 %all-gather.24.cloned.1.call-done = bf16[1536,1536]{1,0:T(8,128)(2,1)} async-done(((bf16[192,1536]{1,0:T(8,128)(2,1)}), bf16[1536,1536]{1,0:T(8,128)(2,1)}) %all-gather.24.cloned.1.call-update) | async-done | bytes 4718608 | tf_op jit(solution)/shard_map/all_gather | solution.py:140
  665.4 512.9 %all-gather.26.cloned.1.call-done = bf16[1536,8960]{1,0:T(8,128)(2,1)} async-done(((bf16[192,8960]{1,0:T(8,128)(2,1)}), bf16[1536,8960]{1,0:T(8,128)(2,1)}) %all-gather.26.cloned.1.call-update) | async-done | bytes 27525136 | tf_op jit(solution)/shard_map/all_gather | solution.py:141
  1178.2 15.6 convolution_add_fusion
  1193.8 510.4 %all-gather.28.cloned.1.call-done = bf16[8960,1536]{1,0:T(8,128)(2,1)} async-done(((bf16[1120,1536]{1,0:T(8,128)(2,1)}), bf16[8960,1536]{1,0:T(8,128)(2,1)}) %all-gather.28.cloned.1.call-update) | async-done | bytes 27525136 | tf_op jit(solution)/shard_map/all_gather | solution.py:142
  1704.2 16.2 convert_reduce_fusion
  1720.4 15.4 multiply_reduce_fusion.14
  1737.1 15.2 convolution_add_fusion.1
  1752.2 15.8 convert_reduce_fusion.1
  1768.0 15.6 multiply_reduce_fusion.16
  1784.4 15.6 convolution_add_fusion.8
  1800.1 17.1 convert_reduce_fusion.8
  2039.4 23.5 fusion
  2101.2 24.0 fusion.1
  2125.9 23.3 fusion.238
  2149.2 29.6 add_convert_fusion
  2179.9 23.3 fusion.290
  2203.2 30.3 add_convert_fusion.1
  2267.4 116.7 %reduce-scatter.28.cloned.1.call-done = bf16[3,192,1536]{2,1,0:T(8,128)(2,1)} async-done(((bf16[3,1536,1536]{2,1,0:T(8,128)(2,1)}), bf16[3,192,1536]{2,1,0:T(8,128)(2,1)}) %reduce-scatter.28.cloned.1.call-update) | async-done | bytes 1769488 | tf_op jit(solution)/shard_map/reduce_scatter | solution.py:364
  2384.1 232.0 %reduce-scatter.32.cloned.1.call-done = bf16[3,192,1536]{2,1,0:T(8,128)(2,1)} async-done(((bf16[3,1536,1536]{2,1,0:T(8,128)(2,1)}), bf16[3,192,1536]{2,1,0:T(8,128)(2,1)}) %reduce-scatter.32.cloned.1.call-update) | async-done | bytes 1769488 | tf_op jit(solution)/shard_map/reduce_scatter | solution.py:370
  2616.1 440.2 %reduce-scatter.38.cloned.1.call-done = bf16[1120,1536]{1,0:T(8,128)(2,1)} async-done(((bf16[8960,1536]{1,0:T(8,128)(2,1)}), bf16[1120,1536]{1,0:T(8,128)(2,1)}) %reduce-scatter.38.cloned.1.call-update) | async-done | bytes 3440656 | tf_op jit(solution)/shard_map/reduce_scatter | solution.py:379
  3056.3 440.0 %reduce-scatter.36.cloned.1.call-done = bf16[192,8960]{1,0:T(8,128)(2,1)} async-done(((bf16[1536,8960]{1,0:T(8,128)(2,1)}), bf16[192,8960]{1,0:T(8,128)(2,1)}) %reduce-scatter.36.cloned.1.call-update) | async-done | bytes 3440656 | tf_op jit(solution)/shard_map/reduce_scatter | solution.py:376
  3497.1 35.7 all-reduce.17
  3534.9 26.7 reduce-scatter.44.cloned.1.call-done
  3579.8 47.0 %reduce-scatter.46.cloned.1.call-done = bf16[192,5]{1,0:T(8,128)(2,1)} async-done(((bf16[1536,5]{1,0:T(8,128)(2,1)}), bf16[192,5]{1,0:T(8,128)(2,1)}) %reduce-scatter.46.cloned.1.call-update) | async-done | bytes 1936
  3627.7 64.3 %reduce-scatter.48.cloned.1.call-done = bf16[192,10]{1,0:T(8,128)(2,1)} async-done(((bf16[1536,10]{1,0:T(8,128)(2,1)}), bf16[192,10]{1,0:T(8,128)(2,1)}) %reduce-scatter.48.cloned.1.call-update) | async-done | bytes 3856
  3707.9 191.1 %all-reduce.22.cloned.1.call-done = (bf16[3,192,1536]{2,1,0:T(8,128)(2,1)}, bf16[192,1536]{1,0:T(8,128)(2,1)}, bf16[3,192,1536]{2,1,0:T(8,128)(2,1)}, bf16[192,1...) async-done(((bf16[3,192,1536]{2,1,0:T(8,128)(2,1)}, bf16[192,1536]{1,0:T(8,128)(2,1)}, bf16[3,192,1536]{2,1,0:T(8,128)(2,1)}, ...) | async-done | bytes 11599888 | tf_op jit(solution)/shard_map/psum | solution.py:394
  (1075 shorter events, 529.8 us)
Async XLA Ops:
  7.2 201.3 %all-gather.18.cloned.1.call-start = ((), (), s32[]{:S(2)}) async-start(), calls=%async_computation.31 | async-start | bytes 15925248 | tf_op jit(solution)/shard_map/all_gather | solution.py:139
  7.9 396.7 %all-gather.14.cloned.1.call-start = ((), (), s32[]{:S(2)}) async-start(), calls=%async_computation.29 | async-start | bytes 15925248 | tf_op jit(solution)/shard_map/all_gather | solution.py:137
  8.7 529.1 %all-gather.16.cloned.1.call-start = ((), (), s32[]{:S(2)}) async-start(), calls=%async_computation.30 | async-start | bytes 5308416 | tf_op jit(solution)/shard_map/all_gather | solution.py:138
  9.4 543.4 %all-gather.30.cloned.1.call-start = ((), (), s32[]{:S(2)}) async-start(), calls=%async_computation.37 | async-start | bytes 1966080 | tf_op jit(solution)/shard_map/all_gather | solution.py:194
  212.4 343.1 %all-gather.20.cloned.1.call-start = ((), (), s32[]{:S(2)}) async-start(), calls=%async_computation.32 | async-start | bytes 1966080 | tf_op jit(solution)/shard_map/all_gather | solution.py:194
  216.3 341.8 %all-gather.22.cloned.1.call-start = ((), (), s32[]{:S(2)}) async-start(), calls=%async_computation.33 | async-start | bytes 1966080 | tf_op jit(solution)/shard_map/all_gather | solution.py:193
  256.9 315.2 %all-gather.32.cloned.1.call-start = ((), (), s32[]{:S(2)}) async-start(), calls=%async_computation.38 | async-start | bytes 1966080 | tf_op jit(solution)/shard_map/all_gather | solution.py:193
  257.7 396.0 %all-gather.24.cloned.1.call-start = ((), (), s32[]{:S(2)}) async-start(), calls=%async_computation.34 | async-start | bytes 5308416 | tf_op jit(solution)/shard_map/all_gather | solution.py:140
  258.5 919.7 %all-gather.26.cloned.1.call-start = ((), (), s32[]{:S(2)}) async-start(), calls=%async_computation.35 | async-start | bytes 30965760 | tf_op jit(solution)/shard_map/all_gather | solution.py:141
  259.3 1445.0 %all-gather.28.cloned.1.call-start = ((), (), s32[]{:S(2)}) async-start(), calls=%async_computation.36 | async-start | bytes 30965760 | tf_op jit(solution)/shard_map/all_gather | solution.py:142
  408.7 22.3 all-to-all-start.4
  486.4 12.3 all-to-all-start.7
  498.7 39.0 all-to-all-start.3
  502.2 1572.3 %reduce-scatter.26.cloned.1.call-start = ((), (), s32[]{:S(2)}) async-start(), calls=%async_computation.40 | async-start | bytes 1966080 | tf_op jit(solution)/shard_map/reduce_scatter | solution.py:221
  1828.3 246.2 %reduce-scatter.24.cloned.1.call-start = ((), (), s32[]{:S(2)}) async-start(), calls=%async_computation.39 | async-start | bytes 1966080 | tf_op jit(solution)/shard_map/reduce_scatter | solution.py:221
  1839.3 249.8 %reduce-scatter.40.cloned.1.call-start = ((), (), s32[]{:S(2)}) async-start(), calls=%async_computation.47 | async-start | bytes 1966080
  1844.0 251.3 %reduce-scatter.42.cloned.1.call-start = ((), (), s32[]{:S(2)}) async-start(), calls=%async_computation.48 | async-start | bytes 1966080
  1852.6 414.8 %reduce-scatter.30.cloned.1.call-start = ((), (), s32[]{:S(2)}) async-start(), calls=%async_computation.42 | async-start | bytes 5308416 | tf_op jit(solution)/shard_map/reduce_scatter | solution.py:367
  1879.2 13.2 all-to-all-start.12
  1882.7 384.8 %reduce-scatter.34.cloned.1.call-start = ((), (), s32[]{:S(2)}) async-start(), calls=%async_computation.44 | async-start | bytes 5308416 | tf_op jit(solution)/shard_map/reduce_scatter | solution.py:373
  1892.4 10.9 all-to-all-start.8
  1937.5 13.4 all-to-all-start.13
  1961.4 10.5 all-to-all-start.9
  1982.5 13.6 all-to-all-start.15
  1986.5 397.6 %reduce-scatter.28.cloned.1.call-start = ((), (), s32[]{:S(2)}) async-start(), calls=%async_computation.41 | async-start | bytes 15925248 | tf_op jit(solution)/shard_map/reduce_scatter | solution.py:364
  2063.0 553.1 %reduce-scatter.32.cloned.1.call-start = ((), (), s32[]{:S(2)}) async-start(), calls=%async_computation.43 | async-start | bytes 15925248 | tf_op jit(solution)/shard_map/reduce_scatter | solution.py:370
  2125.2 931.1 %reduce-scatter.38.cloned.1.call-start = ((), (), s32[]{:S(2)}) async-start(), calls=%async_computation.46 | async-start | bytes 30965760 | tf_op jit(solution)/shard_map/reduce_scatter | solution.py:379
  2178.9 1317.4 %reduce-scatter.36.cloned.1.call-start = ((), (), s32[]{:S(2)}) async-start(), calls=%async_computation.45 | async-start | bytes 30965760 | tf_op jit(solution)/shard_map/reduce_scatter | solution.py:376
  2233.8 1327.8 %reduce-scatter.44.cloned.1.call-start = ((), (), s32[]{:S(2)}) async-start(), calls=%async_computation.49 | async-start | bytes 442368
  2263.9 1362.9 %reduce-scatter.46.cloned.1.call-start = ((), (), s32[]{:S(2)}) async-start(), calls=%async_computation.50 | async-start | bytes 442368
  2266.0 1425.9 %reduce-scatter.48.cloned.1.call-start = ((), (), s32[]{:S(2)}) async-start(), calls=%async_computation.51 | async-start | bytes 442368
  2267.3 1631.7 %all-reduce.22.cloned.1.call-start = ((), (), s32[]{:S(2)}) async-start(), calls=%async_computation.52 | async-start | bytes 23199744 | tf_op jit(solution)/shard_map/psum | solution.py:394
  (328 other events, 9325.0 us)
Sparse Core Ops, SparseCore 0:
  10.2 198.2 all-gather.17
  210.7 193.9 all-gather.13
  406.8 77.5 all-gather.15
  486.4 19.8 all-gather.29
  508.2 20.4 all-gather.19
  530.7 19.6 all-gather.21
  552.5 19.6 all-gather.31
  574.3 79.3 all-gather.23
  655.2 522.9 all-gather.25
  1179.6 524.5 all-gather.27
  1828.4 27.9 reduce-scatter.25
  1858.8 28.0 reduce-scatter.23
  1889.4 29.3 reduce-scatter.39
  1921.2 31.2 reduce-scatter.41
  1956.5 95.5 reduce-scatter.29
  2056.2 95.2 reduce-scatter.33
  2155.1 229.0 reduce-scatter.27
  2387.6 228.4 reduce-scatter.31
  2620.0 436.2 reduce-scatter.37
  3060.0 436.2 reduce-scatter.35
  3500.2 61.3 reduce-scatter.43
  3565.4 61.3 reduce-scatter.45
  3630.6 61.2 reduce-scatter.47
  3694.9 204.0 all-reduce.21
where the time goes:
time: 3930 us; the launch traced here: 3920 us
  waiting for transfers between devices  2990 us (76%)
  matrix products  447 us (11%)
  blocking collectives  177 us (5%)
  other arithmetic  120 us (3%)
  local copies, waits for them, and re-layouts  102 us (3%)
  starting transfers between devices  64 us (2%)
    all_gather x1, waiting for transfers between devices, fetch_weights(): lax.all_gather(ffn_in, 'fsdp', axis=0, tiled=True)  513 us
    all_gather x1, waiting for transfers between devices, fetch_weights(): lax.all_gather(ffn_out, 'fsdp', axis=0, tiled=True)  510 us
    reduce_scatter x1, waiting for transfers between devices, body(): lax.psum_scatter(totals[6].astype(jnp.bfloat16), 'fsdp', scatter_dimensio...  440 us
    reduce_scatter x1, waiting for transfers between devices, body(): lax.psum_scatter(totals[5].astype(jnp.bfloat16), 'fsdp', scatter_dimensio...  440 us
    reduce_scatter x1, waiting for transfers between devices, body(): lax.psum_scatter(totals[3].astype(jnp.bfloat16), 'fsdp', scatter_dimensio...  232 us
    psum x1, waiting for transfers between devices, body(): lax.psum(owned[1].astype(jnp.bfloat16), 'seq').astype(jnp.float32)  191 us
    dot_general x20, matrix products, inner_rows(): lax.dot_general(operand, factor, (((0,), (0,)), ((), ())), preferred_elem...  180 us
    all_gather x1, waiting for transfers between devices, fetch_weights(): lax.all_gather(cross_in, 'fsdp', axis=1, tiled=True)  165 us
  transfers between devices with their start and end apart: 40, of which 24 were waited for; matrix products, arithmetic and copies ran while one was open for 13% of the time, Pallas kernels for 0%

commit v1 on v0

v1 whole, which is shorter than its diff:
```python
import jax
import jax.numpy as jnp
from jax import lax
from jax.sharding import Mesh, PartitionSpec as P

HEADS = 12
HEAD = 128


EPSILON = 1e-06
SEQ = ("y", "core")
SWAP = [(0, 1), (1, 0)]


def matmul(operand, factor):
    return jnp.dot(operand, factor, preferred_element_type=jnp.float32)


def inner_rows(operand, factor):
    return lax.dot_general(
        operand, factor, (((0,), (0,)), ((), ())), preferred_element_type=jnp.float32
    )


def outer_cols(operand, factor):
    return lax.dot_general(
        operand, factor, (((1,), (1,)), ((), ())), preferred_element_type=jnp.float32
    )


def column_sums(tensor):
    return jnp.sum(tensor.astype(jnp.float32), axis=0)


def layer_norm(tensor):
    centered = tensor - jnp.mean(tensor, axis=-1, keepdims=True)
    return centered * lax.rsqrt(jnp.mean(centered * centered, axis=-1, keepdims=True) + EPSILON)


def rms_norm(tensor, weight):
    return tensor * lax.rsqrt(jnp.mean(tensor * tensor, axis=-1, keepdims=True) + EPSILON) * weight


def modulate_norm(tensor, shift, scale):
    return layer_norm(tensor) * (1.0 + scale) + shift


def affine_norm(tensor, weight, offset):
    return layer_norm(tensor) * weight + offset


def gelu_tanh(tensor):
    return jax.nn.gelu(tensor, approximate=True)


def rotary_tables(places, head_size, head_count):
    one_sixth = head_size // 6
    span_sizes = (head_size - 4 * one_sixth, 2 * one_sixth, 2 * one_sixth)
    angles = []
    for component in range(3):
        exponents = (
            jnp.arange(0, span_sizes[component], 2, dtype=jnp.float32) / span_sizes[component]
        )
        frequency = 1.0 / 10000.0**exponents
        angles.append(places[component].astype(jnp.float32)[:, None] * frequency[None, :])
    joined = jnp.concatenate(angles, axis=1)
    tiled_angles = jnp.tile(jnp.repeat(joined, 2, axis=1), (1, head_count))
    parity = jnp.where(jnp.arange(tiled_angles.shape[1]) % 2 == 0, -1.0, 1.0)
    return (jnp.cos(tiled_angles), jnp.sin(tiled_angles) * parity)


def rotate(tensor, cosine, signed_sine):
    even_lane = jnp.arange(tensor.shape[1]) % 2 == 0
    swapped = jnp.where(even_lane, jnp.roll(tensor, -1, axis=1), jnp.roll(tensor, 1, axis=1))
    return tensor * cosine + swapped * signed_sine


def split_heads(tensor):
    return tensor.reshape(tensor.shape[0], tensor.shape[1] // HEAD, HEAD)


def attend(queries, key_rows, value_rows):
    scores = jnp.einsum(
        "qhd,khd->hqk",
        split_heads(queries),
        split_heads(key_rows),
        preferred_element_type=jnp.float32,
    ) * HEAD ** (-0.5)
    row_max = jnp.max(scores, axis=-1, keepdims=True)
    exponentials = jnp.exp(scores - row_max)
    row_total = jnp.sum(exponentials, axis=-1, keepdims=True)
    probabilities = (exponentials / row_total).astype(jnp.bfloat16)
    result = jnp.einsum(
        "hqk,khd->qhd", probabilities, split_heads(value_rows), preferred_element_type=jnp.float32
    )
    return (result.reshape(queries.shape[0], -1).astype(jnp.bfloat16), row_max + jnp.log(row_total))


def attend_back(queries, key_rows, value_rows, log_total, grad_rows):
    query_split = split_heads(queries)
    key_split = split_heads(key_rows)
    grad_split = split_heads(grad_rows)
    scale_factor = HEAD ** (-0.5)
    scores = (
        jnp.einsum("qhd,khd->hqk", query_split, key_split, preferred_element_type=jnp.float32)
        * scale_factor
    )
    probs_full = jnp.exp(scores - log_total)
    probs_low = probs_full.astype(jnp.bfloat16)
    grad_values = jnp.einsum(
        "hqk,qhd->khd", probs_low, grad_split, preferred_element_type=jnp.float32
    )
    grad_probs = jnp.einsum(
        "qhd,khd->hqk", grad_split, split_heads(value_rows), preferred_element_type=jnp.float32
    )
    grad_scores = (
        probs_full * (grad_probs - jnp.sum(grad_probs * probs_full, axis=-1, keepdims=True))
    ).astype(jnp.bfloat16)
    grad_queries = (
        jnp.einsum("hqk,khd->qhd", grad_scores, key_split, preferred_element_type=jnp.float32)
        * scale_factor
    )
    grad_keys = (
        jnp.einsum("hqk,qhd->khd", grad_scores, query_split, preferred_element_type=jnp.float32)
        * scale_factor
    )
    return (
        grad_queries.reshape(queries.shape[0], -1),
        grad_keys.reshape(key_rows.shape[0], -1),
        grad_values.reshape(value_rows.shape[0], -1),
    )


def swap_core(tensor):
    return lax.ppermute(tensor, "core", SWAP)


def join(mine, other, core):
    width = mine.shape[-1]
    both = jnp.concatenate([other, mine, other], axis=-1)
    return lax.dynamic_slice_in_dim(both, (1 - core) * width, 2 * width, axis=-1)


def halves(tensor, core):
    width = tensor.shape[-1] // 2
    return (
        lax.dynamic_slice_in_dim(tensor, core * width, width, axis=-1),
        lax.dynamic_slice_in_dim(tensor, (1 - core) * width, width, axis=-1),
    )


class Split:
    def __init__(self, mine, other, core):
        self.mine, self.other, self.core = mine, other, core

    def apply(self, rows):
        return join(matmul(rows, self.mine), matmul(rows, self.other), self.core)

    def back(self, grad):
        grad_mine, grad_other = halves(grad, self.core)
        return outer_cols(grad_mine, self.mine) + outer_cols(grad_other, self.other)

    def grad(self, rows, grad):
        grad_mine, grad_other = halves(grad, self.core)
        return (inner_rows(rows, grad_mine), inner_rows(rows, grad_other))


def fetch_split(local, gather_axis, core):
    width = local.shape[-1] // 2
    part = lax.dynamic_slice_in_dim(local, core * width, width, axis=-1)
    mine = lax.all_gather(part, "fsdp", axis=gather_axis, tiled=True)
    return mine, swap_core(mine)


def reduce_split(mine_part, other_part, scatter_axis, core):
    received = swap_core(other_part.astype(jnp.bfloat16)).astype(jnp.float32)
    chip = (mine_part + received).astype(jnp.bfloat16)
    owned = lax.psum_scatter(chip, "fsdp", scatter_dimension=scatter_axis, tiled=True)
    summed = lax.psum(owned, "y").astype(jnp.float32)
    return join(summed, swap_core(summed), core)


def fetch_small(modulation, gains, biases, ffn_bias):
    width = modulation.shape[1]
    length = ffn_bias.shape[0]
    rows = -(-length // width)
    padded = jnp.pad(ffn_bias, (0, rows * width - length)).reshape(rows, width)
    packed = jnp.concatenate([modulation, gains, biases, padded], axis=0)
    full = lax.all_gather(packed, "fsdp", axis=1, tiled=True)
    shards = full.shape[1] // width
    bias_rows = full[21:].reshape(rows, shards, width).transpose(1, 0, 2)
    bias_full = bias_rows.reshape(shards, rows * width)[:, :length].reshape(shards * length)
    return full[:6], full[6:11], full[11:21], bias_full


def reduce_small(grad_mod, grad_gains, grad_biases, grad_ffn_bias, grad_time, width, length):
    rows = -(-length // width)
    shards = grad_mod.shape[1] // width
    bias_rows = jnp.pad(grad_ffn_bias.reshape(shards, length), ((0, 0), (0, rows * width - length)))
    bias_rows = bias_rows.reshape(shards, rows, width).transpose(1, 0, 2).reshape(rows, shards * width)
    packed = jnp.concatenate([grad_mod, grad_gains, grad_biases, bias_rows], axis=0)
    owned = lax.psum_scatter(packed, "fsdp", scatter_dimension=1, tiled=True)
    flat = jnp.concatenate([owned.reshape(-1), grad_time.reshape(-1)])
    summed = lax.psum(flat, SEQ)
    owned = summed[: owned.size].reshape(owned.shape)
    grad_time = summed[owned.size :].reshape(grad_time.shape)
    bias_owned = owned[21:].reshape(-1)[:length]
    return owned[:6], owned[6:11], owned[11:21], bias_owned, grad_time


def micro_step(weights, hidden, text, time_emb, places, cotangent):
    modulation, self_q, self_k, self_v, self_o, cross_q, cross_k, cross_v, cross_o, ffn_in, ffn_out, gains, biases, ffn_bias = (
        weights
    )
    gain_rows = gains.astype(jnp.float32)
    bias_rows = biases.astype(jnp.float32)
    modulated = modulation.astype(jnp.float32) + time_emb.astype(jnp.float32)
    cosine, signed_sine = rotary_tables(places, HEAD, HEADS)
    residual_in = hidden.astype(jnp.float32)
    normed_full, pull_first = jax.vjp(modulate_norm, residual_in, modulated[0], modulated[1])
    normed = normed_full.astype(jnp.bfloat16)
    query_pre = self_q.apply(normed) + bias_rows[0]
    key_pre = self_k.apply(normed) + bias_rows[1]
    value_low = (self_v.apply(normed) + bias_rows[2]).astype(jnp.bfloat16)

    def turn_both(query_input, key_input, gain_query, gain_key):
        return (
            rotate(rms_norm(query_input, gain_query), cosine, signed_sine),
            rotate(rms_norm(key_input, gain_key), cosine, signed_sine),
        )

    turned, pull_turn = jax.vjp(turn_both, query_pre, key_pre, gain_rows[0], gain_rows[1])
    query_heads, key_heads, value_heads = (
        lax.all_to_all(turned[0].astype(jnp.bfloat16), SEQ, split_axis=1, concat_axis=0, tiled=True),
        lax.all_to_all(turned[1].astype(jnp.bfloat16), SEQ, split_axis=1, concat_axis=0, tiled=True),
        lax.all_to_all(value_low, SEQ, split_axis=1, concat_axis=0, tiled=True),
    )
    attn_heads, log_total = attend(query_heads, key_heads, value_heads)
    attended = lax.all_to_all(attn_heads, SEQ, split_axis=0, concat_axis=1, tiled=True)
    branch = self_o.apply(attended) + bias_rows[3]
    after_attn = residual_in + branch * modulated[2]
    crossed_full, pull_cross = jax.vjp(affine_norm, after_attn, gain_rows[4], bias_rows[8])
    crossed = crossed_full.astype(jnp.bfloat16)
    cross_query_pre = cross_q.apply(crossed) + bias_rows[4]
    cross_query_full, pull_cross_query = jax.vjp(rms_norm, cross_query_pre, gain_rows[2])
    cross_query = cross_query_full.astype(jnp.bfloat16)
    text_key_pre = cross_k.apply(text) + bias_rows[5]
    text_key_full, pull_text_key = jax.vjp(rms_norm, text_key_pre, gain_rows[3])
    text_value = (cross_v.apply(text) + bias_rows[6]).astype(jnp.bfloat16)
    key_all, value_all = (
        lax.all_gather(text_key_full.astype(jnp.bfloat16), SEQ, axis=0, tiled=True),
        lax.all_gather(text_value, SEQ, axis=0, tiled=True),
    )
    cross_rows, cross_total = attend(cross_query, key_all, value_all)
    second = after_attn + cross_o.apply(cross_rows) + bias_rows[7]
    ffn_normed_full, pull_second = jax.vjp(modulate_norm, second, modulated[3], modulated[4])
    ffn_normed = ffn_normed_full.astype(jnp.bfloat16)
    pre_act = ffn_in.apply(ffn_normed) + ffn_bias.astype(jnp.float32)
    activation_full, pull_gelu = jax.vjp(gelu_tanh, pre_act)
    activation = activation_full.astype(jnp.bfloat16)
    ffn_branch = ffn_out.apply(activation) + bias_rows[9]
    mixed = (second + ffn_branch * modulated[5]).astype(jnp.bfloat16)
    grad_output = cotangent.astype(jnp.float32)
    gate_ffn = jnp.sum(grad_output * ffn_branch, axis=0)
    grad_ffn_branch = (grad_output * modulated[5]).astype(jnp.bfloat16)
    weight_ffn_out = ffn_out.grad(activation, grad_ffn_branch)
    grad_pre_full = pull_gelu(ffn_out.back(grad_ffn_branch))[0]
    grad_pre = grad_pre_full.astype(jnp.bfloat16)
    weight_ffn_in = ffn_in.grad(ffn_normed, grad_pre)
    grad_second_part, shift_ffn, scale_ffn = pull_second(ffn_in.back(grad_pre))
    grad_second = grad_output + grad_second_part
    grad_cross_branch = grad_second.astype(jnp.bfloat16)
    weight_cross_out = cross_o.grad(cross_rows, grad_cross_branch)
    grad_cross_rows = cross_o.back(grad_cross_branch).astype(jnp.bfloat16)
    grad_cross_query, grad_key_all, grad_value_all = attend_back(
        cross_query, key_all, value_all, cross_total, grad_cross_rows
    )
    grad_text_key, grad_text_value_full = (
        lax.psum_scatter(
            grad_key_all.astype(jnp.bfloat16), SEQ, scatter_dimension=0, tiled=True
        ).astype(jnp.float32),
        lax.psum_scatter(
            grad_value_all.astype(jnp.bfloat16), SEQ, scatter_dimension=0, tiled=True
        ).astype(jnp.float32),
    )
    grad_text_value = grad_text_value_full.astype(jnp.bfloat16)
    grad_text_key_full, gain_cross_key = pull_text_key(grad_text_key)
    grad_text_key_pre = grad_text_key_full.astype(jnp.bfloat16)
    weight_cross_key = cross_k.grad(text, grad_text_key_pre)
    weight_cross_value = cross_v.grad(text, grad_text_value)
    grad_words = cross_k.back(grad_text_key_pre) + cross_v.back(grad_text_value)
    grad_cross_query_full, gain_cross_query = pull_cross_query(grad_cross_query)
    grad_cross_query_pre = grad_cross_query_full.astype(jnp.bfloat16)
    weight_cross_query = cross_q.grad(crossed, grad_cross_query_pre)
    grad_after_part, gain_norm, bias_norm = pull_cross(cross_q.back(grad_cross_query_pre))
    grad_after = grad_second + grad_after_part
    gate_attn = jnp.sum(grad_after * branch, axis=0)
    grad_branch = (grad_after * modulated[2]).astype(jnp.bfloat16)
    weight_self_out = self_o.grad(attended, grad_branch)
    grad_attended = self_o.back(grad_branch).astype(jnp.bfloat16)
    grad_attn_heads = lax.all_to_all(grad_attended, SEQ, split_axis=1, concat_axis=0, tiled=True)
    grad_query_heads, grad_key_heads, grad_value_heads = attend_back(
        query_heads, key_heads, value_heads, log_total, grad_attn_heads
    )
    grad_query_turned, grad_key_turned, grad_value = (
        lax.all_to_all(
            grad_query_heads.astype(jnp.bfloat16), SEQ, split_axis=0, concat_axis=1, tiled=True
        ),
        lax.all_to_all(
            grad_key_heads.astype(jnp.bfloat16), SEQ, split_axis=0, concat_axis=1, tiled=True
        ),
        lax.all_to_all(
            grad_value_heads.astype(jnp.bfloat16), SEQ, split_axis=0, concat_axis=1, tiled=True
        ),
    )
    grad_query_full, grad_key_full, gain_query, gain_key = pull_turn(
        (grad_query_turned.astype(jnp.float32), grad_key_turned.astype(jnp.float32))
    )
    grad_query_pre = grad_query_full.astype(jnp.bfloat16)
    grad_key_pre = grad_key_full.astype(jnp.bfloat16)
    weight_self_query = self_q.grad(normed, grad_query_pre)
    weight_self_key = self_k.grad(normed, grad_key_pre)
    weight_self_value = self_v.grad(normed, grad_value)
    grad_normed = self_q.back(grad_query_pre) + self_k.back(grad_key_pre) + self_v.back(grad_value)
    grad_start, shift_attn, scale_attn = pull_first(grad_normed)
    grad_hidden = grad_after + grad_start
    grad_modulated = jnp.stack((shift_attn, scale_attn, gate_attn, shift_ffn, scale_ffn, gate_ffn))
    grad_gains = jnp.stack((gain_query, gain_key, gain_cross_query, gain_cross_key, gain_norm))
    grad_biases = jnp.stack(
        (
            column_sums(grad_query_pre),
            column_sums(grad_key_pre),
            column_sums(grad_value),
            column_sums(grad_branch),
            column_sums(grad_cross_query_pre),
            column_sums(grad_text_key_pre),
            column_sums(grad_text_value),
            column_sums(grad_cross_branch),
            bias_norm,
            column_sums(grad_ffn_branch),
        )
    )
    small = (grad_modulated, grad_gains, grad_biases, column_sums(grad_pre))
    split = tuple(
        jnp.stack(parts) if len(parts) > 1 else parts[0]
        for parts in (
            tuple(w[0] for w in (weight_self_query, weight_self_key, weight_self_value)),
            tuple(w[1] for w in (weight_self_query, weight_self_key, weight_self_value)),
            (weight_self_out[0],),
            (weight_self_out[1],),
            tuple(w[0] for w in (weight_cross_query, weight_cross_key, weight_cross_value)),
            tuple(w[1] for w in (weight_cross_query, weight_cross_key, weight_cross_value)),
            (weight_cross_out[0],),
            (weight_cross_out[1],),
            (weight_ffn_in[0],),
            (weight_ffn_in[1],),
            (weight_ffn_out[0],),
            (weight_ffn_out[1],),
        )
    )
    return (mixed, grad_hidden, grad_words, grad_modulated, small, split)


def body(
    hidden,
    text,
    time_emb,
    modulation,
    self_in,
    self_out,
    cross_in,
    cross_out,
    ffn_in,
    ffn_out,
    gains,
    biases,
    ffn_bias,
    positions,
    cotangent,
):
    core = lax.axis_index("core")
    width = modulation.shape[1]
    length = ffn_bias.shape[0]
    self_in_mine, self_in_other = fetch_split(self_in, 1, core)
    self_out_mine, self_out_other = fetch_split(self_out, 0, core)
    cross_in_mine, cross_in_other = fetch_split(cross_in, 1, core)
    cross_out_mine, cross_out_other = fetch_split(cross_out, 0, core)
    ffn_in_mine, ffn_in_other = fetch_split(ffn_in, 0, core)
    ffn_out_mine, ffn_out_other = fetch_split(ffn_out, 0, core)
    modulation_full, gains_full, biases_full, ffn_bias_full = fetch_small(modulation, gains, biases, ffn_bias)
    weights = (
        modulation_full,
        Split(self_in_mine[0], self_in_other[0], core),
        Split(self_in_mine[1], self_in_other[1], core),
        Split(self_in_mine[2], self_in_other[2], core),
        Split(self_out_mine, self_out_other, core),
        Split(cross_in_mine[0], cross_in_other[0], core),
        Split(cross_in_mine[1], cross_in_other[1], core),
        Split(cross_in_mine[2], cross_in_other[2], core),
        Split(cross_out_mine, cross_out_other, core),
        Split(ffn_in_mine, ffn_in_other, core),
        Split(ffn_out_mine, ffn_out_other, core),
        gains_full,
        biases_full,
        ffn_bias_full,
    )
    mixed_list = []
    hidden_list = []
    words_list = []
    clock_list = []
    small_totals = None
    split_totals = None
    for batch_index in range(hidden.shape[0]):
        mixed, grad_hidden, grad_words, grad_clock, small, split = micro_step(
            weights,
            hidden[batch_index],
            text[batch_index],
            time_emb[batch_index],
            positions[batch_index],
            cotangent[batch_index],
        )
        mixed_list.append(mixed)
        hidden_list.append(grad_hidden)
        words_list.append(grad_words)
        clock_list.append(grad_clock)
        if small_totals is None:
            small_totals, split_totals = small, split
        else:
            small_totals = tuple(a + b for a, b in zip(small_totals, small))
            split_totals = tuple(a + b for a, b in zip(split_totals, split))
    grad_time = jnp.stack(clock_list)
    finals = [
        reduce_split(split_totals[2 * i], split_totals[2 * i + 1], axis, core)
        for i, axis in enumerate((1, 0, 1, 0, 0, 0))
    ]
    grad_mod, grad_gains, grad_biases, grad_ffn_bias, grad_time = reduce_small(
        *small_totals, grad_time, width, length
    )
    return (
        jnp.stack(mixed_list),
        jnp.stack(hidden_list),
        jnp.stack(words_list),
        grad_time,
        grad_mod,
        finals[0],
        finals[1],
        finals[2],
        finals[3],
        finals[4],
        finals[5],
        grad_gains,
        grad_biases,
        grad_ffn_bias,
    )


def solution(mesh):
    devices = mesh.devices
    split_mesh = Mesh(
        devices.reshape(devices.shape[0] // 2, 2, devices.shape[1]), ("y", "core", "fsdp")
    )
    return jax.shard_map(
        body,
        mesh=split_mesh,
        in_specs=(
            P("fsdp", SEQ, None),
            P("fsdp", SEQ, None),
            P("fsdp", None, None),
            P(None, "fsdp"),
            P(None, "fsdp", None),
            P("fsdp", None),
            P(None, "fsdp", None),
            P("fsdp", None),
            P("fsdp", None),
            P("fsdp", None),
            P(None, "fsdp"),
            P(None, "fsdp"),
            P("fsdp"),
            P("fsdp", None, SEQ),
            P("fsdp", SEQ, None),
        ),
        out_specs=(
            P("fsdp", SEQ, None),
            P("fsdp", SEQ, None),
            P("fsdp", SEQ, None),
            P("fsdp", None, None),
            P(None, "fsdp"),
            P(None, "fsdp", None),
            P("fsdp", None),
            P(None, "fsdp", None),
            P("fsdp", None),
            P("fsdp", None),
            P("fsdp", None),
            P(None, "fsdp"),
            P(None, "fsdp"),
            P("fsdp"),
        ),
        check_vma=False,
    )
```

time: 3930 us -> 2320 us (0.59)
  waiting for transfers between devices: 2990 us -> 1410 us
  blocking collectives: 177 us -> 34.5 us
  matrix products: 447 us -> 487 us
    all_gather x10, waiting for transfers between devices: 1380 us -> 555 us  [the longest x6 489 us: fetch_split(): mine = lax.all_gather(part, 'fsdp', axis=gather_axis, tiled=True)]
    reduce_scatter x8 -> x6, waiting for transfers between devices: 1230 us -> 630 us  [reduce_split(): lax.psum_scatter(chip, 'fsdp', scatter_dimension=scatter_axis, tiled=True)]
    unnamed x29 -> x28, waiting for transfers between devices: 143 us -> 41.2 us
    unnamed x2 -> x0, blocking collectives: 68.8 us -> none
    all_gather x3 -> x1, blocking collectives: 96.4 us -> 34.5 us  [fetch_small(): full = lax.all_gather(packed, 'fsdp', axis=1, tiled=True)]
    psum x1 -> x2, waiting for transfers between devices: 191 us -> 129 us  [the longest x1 101 us: reduce_split(): summed = lax.psum(owned, 'y').astype(jnp.float32)]
    dot_general x20 -> x40, matrix products: 125 us -> 164 us  [outer_cols(): lax.dot_general(operand, factor, (((1,), (1,)), ((), ())), preferred_elem...]
    dot_general x20 -> x40, matrix products: 109 us -> 118 us  [matmul(): return jnp.dot(operand, factor, preferred_element_type=jnp.float32)]
  transfers between devices with their start and end apart: 40 -> 57, of which waited for: 24 -> 28; matrix products, arithmetic and copies ran while one was open for 13% -> 28% of each run, Pallas kernels for 0% -> 0%
where the time goes in v1:
time: 2320 us; the launch traced here: 2300 us
  waiting for transfers between devices  1410 us (61%)
  matrix products  487 us (21%)
  other arithmetic  146 us (6%)
  local copies, waits for them, and re-layouts  125 us (5%)
  starting transfers between devices  78.7 us (3%)
  blocking collectives  34.5 us (1%)
    reduce_scatter x6, waiting for transfers between devices, reduce_split(): lax.psum_scatter(chip, 'fsdp', scatter_dimension=scatter_axis, tiled=True)  630 us
    all_gather x6, waiting for transfers between devices, fetch_split(): mine = lax.all_gather(part, 'fsdp', axis=gather_axis, tiled=True)  489 us
    dot_general x40, matrix products, inner_rows(): lax.dot_general(operand, factor, (((0,), (0,)), ((), ())), preferred_elem...  173 us
    dot_general x40, matrix products, outer_cols(): lax.dot_general(operand, factor, (((1,), (1,)), ((), ())), preferred_elem...  164 us
    dot_general x40, matrix products, matmul(): return jnp.dot(operand, factor, preferred_element_type=jnp.float32)  118 us
    psum x1, waiting for transfers between devices, reduce_split(): summed = lax.psum(owned, 'y').astype(jnp.float32)  101 us
  transfers between devices with their start and end apart: 57, of which 28 were waited for; matrix products, arithmetic and copies ran while one was open for 28% of the time, Pallas kernels for 0%

profile of v1, /device:TPU:0, one launch (start us, length us, event | category | flops | bytes accessed | tf_op | source)
XLA Modules:
  0.0 2304.1 jit_solution(8636096790833700677)
XLA Ops:
  19.8 34.5 %all-gather = bf16[8,192,27]{1,2,0:T(8,128)(2,1)S(1)} all-gather(bf16[1,192,27]{1,2,0:T(8,128)(2,1)S(1)} %maximum_bitcast_fusion), channel_id=1, replica_groups=mesh['y'=2,'core'=2,'fsdp'=8] {'fsdp'}, dimensions={0}, use_global_device_ids=true | all-gather | bytes 93312 | tf_op jit(solution)/shard_map/all_gather | solution.py:189
  58.1 65.0 %all-gather.16.cloned.1.call-done = bf16[3,1536,768]{2,1,0:T(8,128)(2,1)} async-done(((bf16[3,192,768]{2,1,0:T(8,128)(2,1)}), bf16[3,1536,768]{2,1,0:T(8,128)(2,1)}) %all-gather.16.cloned.1.call-update) | async-done | bytes 7077904 | tf_op jit(solution)/shard_map/all_gather | solution.py:171
  125.2 107.2 %all-gather.12.cloned.1.call-done = bf16[3,1536,768]{2,1,0:T(8,128)(2,1)} async-done(((bf16[3,192,768]{2,1,0:T(8,128)(2,1)}), bf16[3,1536,768]{2,1,0:T(8,128)(2,1)}) %all-gather.12.cloned.1.call-update) | async-done | bytes 7077904 | tf_op jit(solution)/shard_map/all_gather | solution.py:171
  235.0 50.1 %all-gather.14.cloned.1.call-done = bf16[1536,768]{1,0:T(8,128)(2,1)} async-done(((bf16[192,768]{1,0:T(8,128)(2,1)}), bf16[1536,768]{1,0:T(8,128)(2,1)}) %all-gather.14.cloned.1.call-update) | async-done | bytes 2359312 | tf_op jit(solution)/shard_map/all_gather | solution.py:171
  308.2 11.1 all-gather.30.cloned.1.call-start
  433.7 95.3 %all-gather.24.cloned.1.call-done = bf16[1536,4480]{1,0:T(8,128)(2,1)} async-done(((bf16[192,4480]{1,0:T(8,128)(2,1)}), bf16[1536,4480]{1,0:T(8,128)(2,1)}) %all-gather.24.cloned.1.call-update) | async-done | bytes 13762576 | tf_op jit(solution)/shard_map/all_gather | solution.py:171
  549.0 171.3 %all-gather.26.cloned.1.call-done = bf16[8960,768]{1,0:T(8,128)(2,1)} async-done(((bf16[1120,768]{1,0:T(8,128)(2,1)}), bf16[8960,768]{1,0:T(8,128)(2,1)}) %all-gather.26.cloned.1.call-update) | async-done | bytes 13762576 | tf_op jit(solution)/shard_map/all_gather | solution.py:171
  724.1 16.1 all-gather.20.cloned.1.call-done
  743.1 18.5 all-gather.30.cloned.1.call-done
  765.8 17.2 all-gather.18.cloned.1.call-done
  789.5 14.7 all-gather.28.cloned.1.call-done
  811.0 11.2 fusion.430
  856.4 10.5 convert_reduce_fusion.1
  876.6 9.9 multiply_reduce_fusion.16
  933.1 10.6 multiply_reduce_fusion.14
  1154.2 13.1 fusion.2
  1170.5 11.8 collective-permute-done.12
  1226.2 11.2 fusion.159
  1237.5 16.6 add_convert_fusion.3
  1269.3 11.3 fusion.162
  1280.6 19.9 add_convert_fusion.2
  1302.0 12.3 fusion.425
  1314.4 16.3 add_convert_fusion.1
  1330.9 12.4 fusion.428
  1351.9 20.4 add_convert_fusion
  1385.1 45.1 %reduce-scatter.22.cloned.1.call-done = bf16[3,192,768]{2,1,0:T(8,128)(2,1)} async-done(((bf16[3,1536,768]{2,1,0:T(8,128)(2,1)}), bf16[3,192,768]{2,1,0:T(8,128)(2,1)}) %reduce-scatter.22.cloned.1.call-update) | async-done | bytes 884752 | tf_op jit(solution)/shard_map/reduce_scatter | solution.py:178
  1430.3 131.8 %reduce-scatter.26.cloned.1.call-done = bf16[3,192,768]{2,1,0:T(8,128)(2,1)} async-done(((bf16[3,1536,768]{2,1,0:T(8,128)(2,1)}), bf16[3,192,768]{2,1,0:T(8,128)(2,1)}) %reduce-scatter.26.cloned.1.call-update) | async-done | bytes 884752 | tf_op jit(solution)/shard_map/reduce_scatter | solution.py:178
  1562.1 226.7 %reduce-scatter.30.cloned.1.call-done = bf16[192,4480]{1,0:T(8,128)(2,1)} async-done(((bf16[1536,4480]{1,0:T(8,128)(2,1)}), bf16[192,4480]{1,0:T(8,128)(2,1)}) %reduce-scatter.30.cloned.1.call-update) | async-done | bytes 1720336 | tf_op jit(solution)/shard_map/reduce_scatter | solution.py:178
  1788.8 226.5 %reduce-scatter.32.cloned.1.call-done = bf16[1120,768]{1,0:T(8,128)(2,1)} async-done(((bf16[8960,768]{1,0:T(8,128)(2,1)}), bf16[1120,768]{1,0:T(8,128)(2,1)}) %reduce-scatter.32.cloned.1.call-update) | async-done | bytes 1720336 | tf_op jit(solution)/shard_map/reduce_scatter | solution.py:178
  2059.0 101.1 %all-reduce.24.cloned.1.call-done = (bf16[3,192,768]{2,1,0:T(8,128)(2,1)}, bf16[192,768]{1,0:T(8,128)(2,1)}, bf16[3,192,768]{2,1,0:T(8,128)(2,1)}, bf16[192,768]...) async-done(((bf16[3,192,768]{2,1,0:T(8,128)(2,1)}, bf16[192,768]{1,0:T(8,128)(2,1)}, bf16[3,192,768]{2,1,0:T(8,128)(2,1)}, ...) | async-done | bytes 5799952 | tf_op jit(solution)/shard_map/psum | solution.py:179
  2186.5 40.8 %reduce-scatter.42.cloned.1.call-done = f32[192,27]{1,0:T(8,128)} async-done(((f32[1536,27]{1,0:T(8,128)}), f32[192,27]{1,0:T(8,128)}) %reduce-scatter.42.cloned.1.call-update) | async-done | bytes 20752
  2234.9 28.4 %all-reduce.22.cloned.1.call-done = f32[23616]{0:T(1024)} async-done(((f32[23616]{0:T(1024)}), f32[23616]{0:T(1024)}) %all-reduce.22.cloned.1.call-update) | async-done | bytes 94480 | tf_op jit(solution)/shard_map/psum | solution.py:204
  (1297 shorter events, 695.1 us)
Async XLA Ops:
  7.2 115.9 %all-gather.16.cloned.1.call-start = ((), (), s32[]{:S(2)}) async-start(), calls=%async_computation.29 | async-start | bytes 7962624 | tf_op jit(solution)/shard_map/all_gather | solution.py:171
  9.6 222.8 %all-gather.12.cloned.1.call-start = ((), (), s32[]{:S(2)}) async-start(), calls=%async_computation.27 | async-start | bytes 7962624 | tf_op jit(solution)/shard_map/all_gather | solution.py:171
  11.8 273.3 %all-gather.14.cloned.1.call-start = ((), (), s32[]{:S(2)}) async-start(), calls=%async_computation.28 | async-start | bytes 2654208 | tf_op jit(solution)/shard_map/all_gather | solution.py:171
  13.6 378.2 %all-gather.22.cloned.1.call-start = ((), (), s32[]{:S(2)}) async-start(), calls=%async_computation.32 | async-start | bytes 2654208 | tf_op jit(solution)/shard_map/all_gather | solution.py:171
  15.3 513.7 %all-gather.24.cloned.1.call-start = ((), (), s32[]{:S(2)}) async-start(), calls=%async_computation.33 | async-start | bytes 15482880 | tf_op jit(solution)/shard_map/all_gather | solution.py:171
  16.8 703.6 %all-gather.26.cloned.1.call-start = ((), (), s32[]{:S(2)}) async-start(), calls=%async_computation.34 | async-start | bytes 15482880 | tf_op jit(solution)/shard_map/all_gather | solution.py:171
  19.6 720.6 %all-gather.20.cloned.1.call-start = ((), (), s32[]{:S(2)}) async-start(), calls=%async_computation.31 | async-start | bytes 1966080 | tf_op jit(solution)/shard_map/all_gather | solution.py:251
  123.1 178.0 %collective-permute-start.2 = (bf16[3,1536,768]{2,1,0:T(8,128)(2,1)}, bf16[3,1536,768]{2,1,0:T(8,128)(2,1)}, u32[]{:S(2)}, u32[]{:S(2)}) collective-permute-start(bf16[3,1536,768]{2,1,0:T(8,128)(2,1)} %all-gather.16.cloned.1.call-done), channel_id=1, source_target_pairs={{0,8},{8,0},{1,9},{9,1},{2,10},{10,2},{3,11},{11,3},{4,12},{12,4},... | collective-permute-start | bytes 21233672 | tf_op jit(solution)/shard_map/ppermute | solution.py:135
  285.1 248.7 %collective-permute-start.1 = (bf16[1536,768]{1,0:T(8,128)(2,1)}, bf16[1536,768]{1,0:T(8,128)(2,1)}, u32[]{:S(2)}, u32[]{:S(2)}) collective-permute-start(bf16[1536,768]{1,0:T(8,128)(2,1)} %all-gather.14.cloned.1.call-done), channel_id=1, source_target_pairs={{0,8},{8,0},{1,9},{9,1},{2,10},{10,2},{3,11},{11,3},{4,12},{12,4},... | collective-permute-start | bytes 7077896 | tf_op jit(solution)/shard_map/ppermute | solution.py:135
  308.2 453.4 %all-gather.30.cloned.1.call-start = ((), (), s32[]{:S(2)}) async-start(), calls=%async_computation.36 | async-start | bytes 1966080 | tf_op jit(solution)/shard_map/all_gather | solution.py:251
  336.7 446.3 %all-gather.18.cloned.1.call-start = ((), (), s32[]{:S(2)}) async-start(), calls=%async_computation.30 | async-start | bytes 1966080 | tf_op jit(solution)/shard_map/all_gather | solution.py:252
  389.4 414.8 %all-gather.28.cloned.1.call-start = ((), (), s32[]{:S(2)}) async-start(), calls=%async_computation.35 | async-start | bytes 1966080 | tf_op jit(solution)/shard_map/all_gather | solution.py:252
  391.8 394.8 %collective-permute-start.3 = (bf16[1536,768]{1,0:T(8,128)(2,1)}, bf16[1536,768]{1,0:T(8,128)(2,1)}, u32[]{:S(2)}, u32[]{:S(2)}) collective-permute-start(bf16[1536,768]{1,0:T(8,128)(2,1)} %all-gather.22.cloned.1.call-done), channel_id=1, source_target_pairs={{0,8},{8,0},{1,9},{9,1},{2,10},{10,2},{3,11},{11,3},{4,12},{12,4},... | collective-permute-start | bytes 7077896 | tf_op jit(solution)/shard_map/ppermute | solution.py:135
  432.3 773.6 %reduce-scatter.34.cloned.1.call-start = ((), (), s32[]{:S(2)}) async-start(), calls=%async_computation.44 | async-start | bytes 1966080
  529.0 307.7 %collective-permute-start.4 = (bf16[1536,4480]{1,0:T(8,128)(2,1)}, bf16[1536,4480]{1,0:T(8,128)(2,1)}, u32[]{:S(2)}, u32[]{:S(2)}) collective-permute-start(bf16[1536,4480]{1,0:T(8,128)(2,1)} %all-gather.24.cloned.1.call-done), channel_id=1, source_target_pairs={{0,8},{8,0},{1,9},{9,1},{2,10},{10,2},{3,11},{11,3},{4,12},{12,4},... | collective-permute-start | bytes 41287688 | tf_op jit(solution)/shard_map/ppermute | solution.py:135
  720.3 136.0 %collective-permute-start.5 = (bf16[8960,768]{1,0:T(8,128)(2,1)}, bf16[8960,768]{1,0:T(8,128)(2,1)}, u32[]{:S(2)}, u32[]{:S(2)}) collective-permute-start(bf16[8960,768]{1,0:T(8,128)(2,1)} %all-gather.26.cloned.1.call-done), channel_id=1, source_target_pairs={{0,8},{8,0},{1,9},{9,1},{2,10},{10,2},{3,11},{11,3},{4,12},{12,4},... | collective-permute-start | bytes 41287688 | tf_op jit(solution)/shard_map/ppermute | solution.py:135
  946.3 261.4 %reduce-scatter.38.cloned.1.call-start = ((), (), s32[]{:S(2)}) async-start(), calls=%async_computation.46 | async-start | bytes 1966080
  988.3 221.4 %reduce-scatter.40.cloned.1.call-start = ((), (), s32[]{:S(2)}) async-start(), calls=%async_computation.47 | async-start | bytes 1966080
  1011.9 199.0 %reduce-scatter.36.cloned.1.call-start = ((), (), s32[]{:S(2)}) async-start(), calls=%async_computation.45 | async-start | bytes 1966080
  1025.7 124.5 %collective-permute-start.8 = (bf16[1536,768]{1,0:T(8,128)(2,1)}, bf16[1536,768]{1,0:T(8,128)(2,1)}, u32[]{:S(2)}, u32[]{:S(2)}) collective-permute-start(bf16[1536,768]{1,0:T(8,128)(2,1)} %add_convert_fusion.7), channel_id=1, source_target_pairs={{0,8},{8,0},{1,9},{9,1},{2,10},{10,2},{3,11},{11,3},{4,12},{12,4},... | collective-permute-start | bytes 7077896 | tf_op jit(solution)/shard_map/ppermute | solution.py:135
  1117.6 267.5 %reduce-scatter.24.cloned.1.call-start = ((), (), s32[]{:S(2)}) async-start(), calls=%async_computation.39 | async-start | bytes 2654208 | tf_op jit(solution)/shard_map/reduce_scatter | solution.py:178
  1154.2 230.9 %reduce-scatter.28.cloned.1.call-start = ((), (), s32[]{:S(2)}) async-start(), calls=%async_computation.41 | async-start | bytes 2654208 | tf_op jit(solution)/shard_map/reduce_scatter | solution.py:178
  1184.6 245.7 %reduce-scatter.22.cloned.1.call-start = ((), (), s32[]{:S(2)}) async-start(), calls=%async_computation.38 | async-start | bytes 7962624 | tf_op jit(solution)/shard_map/reduce_scatter | solution.py:178
  1198.8 363.3 %reduce-scatter.26.cloned.1.call-start = ((), (), s32[]{:S(2)}) async-start(), calls=%async_computation.40 | async-start | bytes 7962624 | tf_op jit(solution)/shard_map/reduce_scatter | solution.py:178
  1267.9 521.0 %reduce-scatter.30.cloned.1.call-start = ((), (), s32[]{:S(2)}) async-start(), calls=%async_computation.42 | async-start | bytes 15482880 | tf_op jit(solution)/shard_map/reduce_scatter | solution.py:178
  1300.6 714.8 %reduce-scatter.32.cloned.1.call-start = ((), (), s32[]{:S(2)}) async-start(), calls=%async_computation.43 | async-start | bytes 15482880 | tf_op jit(solution)/shard_map/reduce_scatter | solution.py:178
  1372.6 787.5 %all-reduce.24.cloned.1.call-start = ((), (), s32[]{:S(2)}) async-start(), calls=%async_computation.49 | async-start | bytes 11599872 | tf_op jit(solution)/shard_map/psum | solution.py:179
  2015.4 211.9 %reduce-scatter.42.cloned.1.call-start = ((), (), s32[]{:S(2)}) async-start(), calls=%async_computation.48 | async-start | bytes 884736
  2051.9 211.4 %all-reduce.22.cloned.1.call-start = ((), (), s32[]{:S(2)}) async-start(), calls=%async_computation.37 | async-start | bytes 196608 | tf_op jit(solution)/shard_map/psum | solution.py:204
  2161.9 124.5 %collective-permute-start.15 = (f32[192,4480]{1,0:T(8,128)S(1)}, f32[192,4480]{1,0:T(8,128)}, u32[]{:S(2)}, u32[]{:S(2)}) collective-permute-start(f32[192,4480]{1,0:T(8,128)S(1)} %convert_element_type.813), channel_id=1, source_target_pairs={{0,8},{8,0},{1,9},{9,1},{2,10},{10,2},{3,11},{11,3},{4,12},{12,4},... | collective-permute-start | bytes 10321928 | tf_op jit(solution)/shard_map/ppermute | solution.py:135
  2171.5 105.5 %collective-permute-start.7 = (f32[3,192,768]{2,1,0:T(8,128)}, f32[3,192,768]{2,1,0:T(8,128)}, u32[]{:S(2)}, u32[]{:S(2)}) collective-permute-start(f32[3,192,768]{2,1,0:T(8,128)} %convert_element_type.797), channel_id=1, source_target_pairs={{0,8},{8,0},{1,9},{9,1},{2,10},{10,2},{3,11},{11,3},{4,12},{12,4},... | collective-permute-start | bytes 5308424 | tf_op jit(solution)/shard_map/ppermute | solution.py:135
  2178.5 112.9 %collective-permute-start.17 = (f32[1120,768]{1,0:T(8,128)}, f32[1120,768]{1,0:T(8,128)}, u32[]{:S(2)}, u32[]{:S(2)}) collective-permute-start(f32[1120,768]{1,0:T(8,128)} %convert_element_type.817), channel_id=1, source_target_pairs={{0,8},{8,0},{1,9},{9,1},{2,10},{10,2},{3,11},{11,3},{4,12},{12,4},... | collective-permute-start | bytes 10321928 | tf_op jit(solution)/shard_map/ppermute | solution.py:135
  (388 other events, 6519.2 us)
Sparse Core Ops, SparseCore 0:
  10.8 112.2 all-gather.15
  125.8 106.4 all-gather.11
  235.1 49.9 all-gather.13
  287.2 50.1 all-gather.21
  340.0 189.0 all-gather.23
  531.6 188.6 all-gather.25
  721.9 18.2 all-gather.19
  741.8 19.7 all-gather.29
  763.2 19.8 all-gather.17
  784.4 19.8 all-gather.27
  946.5 28.0 reduce-scatter.33
  988.4 28.2 reduce-scatter.37
  1019.2 29.9 reduce-scatter.39
  1051.7 31.3 reduce-scatter.35
  1154.3 71.2 reduce-scatter.23
  1229.6 68.6 reduce-scatter.27
  1301.8 128.3 reduce-scatter.21
  1433.8 128.2 reduce-scatter.25
  1565.7 223.0 reduce-scatter.29
  1792.3 223.0 reduce-scatter.31
  2018.3 141.7 all-reduce.23
  2164.0 63.2 reduce-scatter.41
  2232.4 30.8 all-reduce.21

commit v2 on v1

--- a/solution.py
+++ b/solution.py
@@ -149,35 +149,53 @@
     )
 
 
+def swap_y(tensor):
+    return lax.ppermute(tensor, "y", SWAP)
+
+
 class Split:
-    def __init__(self, mine, other, core):
-        self.mine, self.other, self.core = mine, other, core
+    def __init__(self, parts, spot):
+        self.parts, self.spot = parts, spot
 
     def apply(self, rows):
-        return join(matmul(rows, self.mine), matmul(rows, self.other), self.core)
+        y, core = self.spot
+        own, y_part, core_part, cross_part = (matmul(rows, part) for part in self.parts)
+        return join(join(own, y_part, y), join(core_part, cross_part, y), core)
+
+    def quarters(self, grad):
+        y, core = self.spot
+        grad_mine, grad_other = halves(grad, core)
+        return halves(grad_mine, y) + halves(grad_other, y)
 
     def back(self, grad):
-        grad_mine, grad_other = halves(grad, self.core)
-        return outer_cols(grad_mine, self.mine) + outer_cols(grad_other, self.other)
+        pieces = [outer_cols(g, part) for g, part in zip(self.quarters(grad), self.parts)]
+        return (pieces[0] + pieces[1]) + (pieces[2] + pieces[3])
 
     def grad(self, rows, grad):
-        grad_mine, grad_other = halves(grad, self.core)
-        return (inner_rows(rows, grad_mine), inner_rows(rows, grad_other))
-
-
-def fetch_split(local, gather_axis, core):
-    width = local.shape[-1] // 2
-    part = lax.dynamic_slice_in_dim(local, core * width, width, axis=-1)
-    mine = lax.all_gather(part, "fsdp", axis=gather_axis, tiled=True)
-    return mine, swap_core(mine)
-
-
-def reduce_split(mine_part, other_part, scatter_axis, core):
-    received = swap_core(other_part.astype(jnp.bfloat16)).astype(jnp.float32)
-    chip = (mine_part + received).astype(jnp.bfloat16)
-    owned = lax.psum_scatter(chip, "fsdp", scatter_dimension=scatter_axis, tiled=True)
-    summed = lax.psum(owned, "y").astype(jnp.float32)
-    return join(summed, swap_core(summed), core)
+        return tuple(inner_rows(rows, g) for g in self.quarters(grad))
+
+
+def fetch_split(local, gather_axis, spot):
+    y, core = spot
+    width = local.shape[-1] // 4
+    part = lax.dynamic_slice_in_dim(local, (2 * core + y) * width, width, axis=-1)
+    own = lax.all_gather(part, "fsdp", axis=gather_axis, tiled=True)
+    y_part = swap_y(own)
+    return (own, y_part, swap_core(own), swap_core(y_part))
+
+
+def reduce_split(parts, scatter_axis, spot):
+    y, core = spot
+    own, y_part, core_part, cross_part = parts
+    from_core = swap_core(core_part.astype(jnp.bfloat16)).astype(jnp.float32)
+    from_cross = swap_core(cross_part.astype(jnp.bfloat16)).astype(jnp.float32)
+    chip_own = own + from_core
+    chip_y = (y_part + from_cross).astype(jnp.bfloat16)
+    total = (chip_own + swap_y(chip_y).astype(jnp.float32)).astype(jnp.bfloat16)
+    owned = lax.psum_scatter(total, "fsdp", scatter_dimension=scatter_axis, tiled=True)
+    owned_y = swap_y(owned)
+    mine = join(owned, owned_y, y)
+    return join(mine, swap_core(mine), core).astype(jnp.float32)
 
 
 def fetch_small(modulation, gains, biases, ffn_bias):
@@ -341,23 +359,19 @@
         )
     )
     small = (grad_modulated, grad_gains, grad_biases, column_sums(grad_pre))
-    split = tuple(
-        jnp.stack(parts) if len(parts) > 1 else parts[0]
-        for parts in (
-            tuple(w[0] for w in (weight_self_query, weight_self_key, weight_self_value)),
-            tuple(w[1] for w in (weight_self_query, weight_self_key, weight_self_value)),
-            (weight_self_out[0],),
-            (weight_self_out[1],),
-            tuple(w[0] for w in (weight_cross_query, weight_cross_key, weight_cross_value)),
-            tuple(w[1] for w in (weight_cross_query, weight_cross_key, weight_cross_value)),
-            (weight_cross_out[0],),
-            (weight_cross_out[1],),
-            (weight_ffn_in[0],),
-            (weight_ffn_in[1],),
-            (weight_ffn_out[0],),
-            (weight_ffn_out[1],),
-        )
-    )
+    stacked = []
+    for group in (
+        (weight_self_query, weight_self_key, weight_self_value),
+        (weight_self_out,),
+        (weight_cross_query, weight_cross_key, weight_cross_value),
+        (weight_cross_out,),
+        (weight_ffn_in,),
+        (weight_ffn_out,),
+    ):
+        for quarter in range(4):
+            parts = tuple(w[quarter] for w in group)
+            stacked.append(jnp.stack(parts) if len(parts) > 1 else parts[0])
+    split = tuple(stacked)
     return (mixed, grad_hidden, grad_words, grad_modulated, small, split)
 
 
@@ -378,28 +392,28 @@
     positions,
     cotangent,
 ):
-    core = lax.axis_index("core")
+    spot = (lax.axis_index("y"), lax.axis_index("core"))
     width = modulation.shape[1]
     length = ffn_bias.shape[0]
-    self_in_mine, self_in_other = fetch_split(self_in, 1, core)
-    self_out_mine, self_out_other = fetch_split(self_out, 0, core)
-    cross_in_mine, cross_in_other = fetch_split(cross_in, 1, core)
-    cross_out_mine, cross_out_other = fetch_split(cross_out, 0, core)
-    ffn_in_mine, ffn_in_other = fetch_split(ffn_in, 0, core)
-    ffn_out_mine, ffn_out_other = fetch_split(ffn_out, 0, core)
+    self_in_parts = fetch_split(self_in, 1, spot)
+    self_out_parts = fetch_split(self_out, 0, spot)
+    cross_in_parts = fetch_split(cross_in, 1, spot)
+    cross_out_parts = fetch_split(cross_out, 0, spot)
+    ffn_in_parts = fetch_split(ffn_in, 0, spot)
+    ffn_out_parts = fetch_split(ffn_out, 0, spot)
     modulation_full, gains_full, biases_full, ffn_bias_full = fetch_small(modulation, gains, biases, ffn_bias)
     weights = (
         modulation_full,
-        Split(self_in_mine[0], self_in_other[0], core),
-        Split(self_in_mine[1], self_in_other[1], core),
-        Split(self_in_mine[2], self_in_other[2], core),
-        Split(self_out_mine, self_out_other, core),
-        Split(cross_in_mine[0], cross_in_other[0], core),
-        Split(cross_in_mine[1], cross_in_other[1], core),
-        Split(cross_in_mine[2], cross_in_other[2], core),
-        Split(cross_out_mine, cross_out_other, core),
-        Split(ffn_in_mine, ffn_in_other, core),
-        Split(ffn_out_mine, ffn_out_other, core),
+        Split(tuple(part[0] for part in self_in_parts), spot),
+        Split(tuple(part[1] for part in self_in_parts), spot),
+        Split(tuple(part[2] for part in self_in_parts), spot),
+        Split(self_out_parts, spot),
+        Split(tuple(part[0] for part in cross_in_parts), spot),
+        Split(tuple(part[1] for part in cross_in_parts), spot),
+        Split(tuple(part[2] for part in cross_in_parts), spot),
+        Split(cross_out_parts, spot),
+        Split(ffn_in_parts, spot),
+        Split(ffn_out_parts, spot),
         gains_full,
         biases_full,
         ffn_bias_full,
@@ -430,7 +444,7 @@
             split_totals = tuple(a + b for a, b in zip(split_totals, split))
     grad_time = jnp.stack(clock_list)
     finals = [
-        reduce_split(split_totals[2 * i], split_totals[2 * i + 1], axis, core)
+        reduce_split(split_totals[4 * i : 4 * i + 4], axis, spot)
         for i, axis in enumerate((1, 0, 1, 0, 0, 0))
     ]
     grad_mod, grad_gains, grad_biases, grad_ffn_bias, grad_time = reduce_small(

time: 2320 us -> 2040 us (0.88)
  waiting for transfers between devices: 1410 us -> 954 us
  matrix products: 487 us -> 576 us
  local copies, waits for them, and re-layouts: 125 us -> 174 us
  other arithmetic: 146 us -> 171 us
    reduce_scatter x6, waiting for transfers between devices: 630 us -> 70.7 us  [reduce_split(): lax.psum_scatter(total, 'fsdp', scatter_dimension=scatter_axis, tiled=True)]
    ppermute x0 -> x18, waiting for transfers between devices: none -> 467 us  [swap_y(): return lax.ppermute(tensor, 'y', SWAP)]
    all_gather x6, waiting for transfers between devices: 489 us -> 231 us  [fetch_split(): own = lax.all_gather(part, 'fsdp', axis=gather_axis, tiled=True)]
    all_to_all x2, waiting for transfers between devices: 1.41 us -> 143 us  [micro_step(): lax.all_to_all(turned[0].astype(jnp.bfloat16), SEQ, split_axis=1, concat_...]
    psum x1 -> x0, waiting for transfers between devices: 101 us -> none  [reduce_split(): summed = lax.psum(owned, 'y').astype(jnp.float32)]
    convert_element_type x10 -> x18, other arithmetic: 42.3 us -> 84.6 us  [the longest x6 45.4 us: reduce_split(): total = (chip_own + swap_y(chip_y).astype(jnp.float32)).astype(jnp.bfloat16)]
    unnamed x28 -> x27, waiting for transfers between devices: 41.2 us -> 0.43 us
    all_gather x2, waiting for transfers between devices: 34.7 us -> 0.02 us  [micro_step(): lax.all_gather(text_key_full.astype(jnp.bfloat16), SEQ, axis=0, tiled=True)]
  transfers between devices with their start and end apart: 57 -> 86, of which waited for: 28 -> 28; matrix products, arithmetic and copies ran while one was open for 28% -> 37% of each run, Pallas kernels for 0% -> 0%
where the time goes in v2:
time: 2040 us; the launch traced here: 2020 us
  waiting for transfers between devices  954 us (47%)
  matrix products  576 us (28%)
  local copies, waits for them, and re-layouts  174 us (9%)
  other arithmetic  171 us (8%)
  starting transfers between devices  91.6 us (4%)
  blocking collectives  33.2 us (2%)
  between operations  21.5 us (1%)
    ppermute x18, waiting for transfers between devices, swap_y(): return lax.ppermute(tensor, 'y', SWAP)  467 us
    all_gather x6, waiting for transfers between devices, fetch_split(): own = lax.all_gather(part, 'fsdp', axis=gather_axis, tiled=True)  231 us
    dot_general x80, matrix products, inner_rows(): lax.dot_general(operand, factor, (((0,), (0,)), ((), ())), preferred_elem...  205 us
    dot_general x80, matrix products, outer_cols(): lax.dot_general(operand, factor, (((1,), (1,)), ((), ())), preferred_elem...  188 us
    dot_general x80, matrix products, matmul(): return jnp.dot(operand, factor, preferred_element_type=jnp.float32)  152 us
    all_to_all x2, waiting for transfers between devices, micro_step(): lax.all_to_all(turned[0].astype(jnp.bfloat16), SEQ, split_axis=1, concat_...  143 us
    reduce_scatter x6, waiting for transfers between devices, reduce_split(): lax.psum_scatter(total, 'fsdp', scatter_dimension=scatter_axis, tiled=True)  70.7 us
    convert_element_type x6, other arithmetic, reduce_split(): total = (chip_own + swap_y(chip_y).astype(jnp.float32)).astype(jnp.bfloat16)  45.4 us
  transfers between devices with their start and end apart: 86, of which 28 were waited for; matrix products, arithmetic and copies ran while one was open for 37% of the time, Pallas kernels for 0%

profile of v2, /device:TPU:0, one launch (start us, length us, event | category | flops | bytes accessed | tf_op | source)
XLA Modules:
  0.0 2022.2 jit_solution(12766569407485843037)
XLA Ops:
  18.4 33.2 %all-gather = bf16[8,192,27]{1,2,0:T(8,128)(2,1)S(1)} all-gather(bf16[1,192,27]{1,2,0:T(8,128)(2,1)S(1)} %maximum_bitcast_fusion), channel_id=1, replica_groups=mesh['y'=2,'core'=2,'fsdp'=8] {'fsdp'}, dimensions={0}, use_global_device_ids=true | all-gather | bytes 93312 | tf_op jit(solution)/shard_map/all_gather | solution.py:207
  56.4 22.5 %all-gather.12.cloned.1.call-done = bf16[3,1536,384]{2,1,0:T(8,128)(2,1)} async-done(((bf16[3,192,384]{2,1,0:T(8,128)(2,1)}), bf16[3,1536,384]{2,1,0:T(8,128)(2,1)}) %all-gather.12.cloned.1.call-update) | async-done | bytes 3538960 | tf_op jit(solution)/shard_map/all_gather | solution.py:182
  85.6 59.6 %all-gather.16.cloned.1.call-done = bf16[3,1536,384]{2,1,0:T(8,128)(2,1)} async-done(((bf16[3,192,384]{2,1,0:T(8,128)(2,1)}), bf16[3,1536,384]{2,1,0:T(8,128)(2,1)}) %all-gather.16.cloned.1.call-update) | async-done | bytes 3538960 | tf_op jit(solution)/shard_map/all_gather | solution.py:182
  146.7 41.0 %all-gather.14.cloned.1.call-done = bf16[1536,384]{1,0:T(8,128)(2,1)} async-done(((bf16[192,384]{1,0:T(8,128)(2,1)}), bf16[1536,384]{1,0:T(8,128)(2,1)}) %all-gather.14.cloned.1.call-update) | async-done | bytes 1179664 | tf_op jit(solution)/shard_map/all_gather | solution.py:182
  189.2 40.8 %all-gather.22.cloned.1.call-done = bf16[1536,384]{1,0:T(8,128)(2,1)} async-done(((bf16[192,384]{1,0:T(8,128)(2,1)}), bf16[1536,384]{1,0:T(8,128)(2,1)}) %all-gather.22.cloned.1.call-update) | async-done | bytes 1179664 | tf_op jit(solution)/shard_map/all_gather | solution.py:182
  272.6 67.0 %all-gather.24.cloned.1.call-done = bf16[1536,2240]{1,0:T(8,128)(2,1)} async-done(((bf16[192,2240]{1,0:T(8,128)(2,1)}), bf16[1536,2240]{1,0:T(8,128)(2,1)}) %all-gather.24.cloned.1.call-update) | async-done | bytes 6881296 | tf_op jit(solution)/shard_map/all_gather | solution.py:182
  339.6 10.3 copy.405
  396.5 143.0 %all-to-all-done.1 = bf16[96,4,384]{2,0,1:T(8,128)(2,1)S(1)} async-done(((bf16[96,4,384]{2,0,1:T(8,128)(2,1)}), bf16[96,4,384]{2,0,1:T(8,128)(2,1)S(1)}, u32[]{:S(2)}, u32[]{:S(2)}) %all-to-all-start.1) | async-done | bytes 294944 | tf_op jit(solution)/shard_map/all_to_all | solution.py:252
  580.0 7.4 all-to-all-done.6
  681.1 90.2 %collective-permute-done.15 = bf16[8960,384]{1,0:T(8,128)(2,1)} collective-permute-done((bf16[8960,384]{1,0:T(8,128)(2,1)}, bf16[8960,384]{1,0:T(8,128)(2,1)}, u32[]{:S(2)}, u32[]{:S(2)}) %collective-permute-start.15) | collective-permute-done | bytes 6881312 | tf_op jit(solution)/shard_map/ppermute | solution.py:153
  842.9 9.3 convert_reduce_fusion.1
  910.6 10.4 convert_reduce_fusion
  1033.8 8.0 fusion.391
  1045.2 8.7 fusion.394
  1058.9 12.4 convolution_add_fusion.3
  1186.9 11.7 add_convert_fusion.5
  1237.7 9.7 copy.483
  1247.4 102.0 %collective-permute-done.40 = bf16[1536,2240]{0,1:T(8,128)(2,1)} collective-permute-done((bf16[1536,2240]{0,1:T(8,128)(2,1)}, bf16[1536,2240]{0,1:T(8,128)(2,1)}, u32[]{:S(2)}, u32[]{:S(2)}) %collective-permute-start.40) | collective-permute-done | bytes 6881312 | tf_op jit(solution)/shard_map/ppermute | solution.py:153
  1349.4 10.0 copy.484
  1359.4 13.0 add_convert_fusion
  1413.4 9.9 add_convert_fusion.3
  1456.9 21.9 %collective-permute-done.25 = bf16[1536,384]{1,0:T(8,128)(2,1)S(1)} collective-permute-done((bf16[1536,384]{1,0:T(8,128)(2,1)S(1)}, bf16[1536,384]{1,0:T(8,128)(2,1)S(1)}, u32[]{:S(2)}, u32[]{:S(2)}) %collective-permute-start.25) | collective-permute-done | bytes 1179680 | tf_op jit(solution)/shard_map/ppermute | solution.py:153
  1501.1 12.5 collective-permute-done.35
  1546.9 42.2 %collective-permute-done.20 = bf16[3,1536,384]{2,1,0:T(8,128)(2,1)} collective-permute-done((bf16[3,1536,384]{2,1,0:T(8,128)(2,1)}, bf16[3,1536,384]{2,1,0:T(8,128)(2,1)}, u32[]{:S(2)}, u32[]{:S(2)}) %collective-permute-start.20) | collective-permute-done | bytes 3538976 | tf_op jit(solution)/shard_map/ppermute | solution.py:153
  1589.1 9.8 fusion.6
  1616.2 7.8 fusion.604
  1624.0 11.9 add_convert_fusion.2
  1641.2 54.6 %collective-permute-done.30 = bf16[3,1536,384]{2,1,0:T(8,128)(2,1)} collective-permute-done((bf16[3,1536,384]{2,1,0:T(8,128)(2,1)}, bf16[3,1536,384]{2,1,0:T(8,128)(2,1)}, u32[]{:S(2)}, u32[]{:S(2)}) %collective-permute-start.30) | collective-permute-done | bytes 3538976 | tf_op jit(solution)/shard_map/ppermute | solution.py:153
  1703.7 7.8 fusion.616
  1711.5 130.8 %collective-permute-done.45 = bf16[8960,384]{1,0:T(8,128)(2,1)} collective-permute-done((bf16[8960,384]{1,0:T(8,128)(2,1)}, bf16[8960,384]{1,0:T(8,128)(2,1)}, u32[]{:S(2)}, u32[]{:S(2)}) %collective-permute-start.45) | collective-permute-done | bytes 6881312 | tf_op jit(solution)/shard_map/ppermute | solution.py:153
  1842.3 12.4 add_convert_fusion.1
  1908.7 70.7 %reduce-scatter.32.cloned.1.call-done = bf16[1120,384]{1,0:T(8,128)(2,1)} async-done(((bf16[8960,384]{1,0:T(8,128)(2,1)}), bf16[1120,384]{1,0:T(8,128)(2,1)}) %reduce-scatter.32.cloned.1.call-update) | async-done | bytes 860176 | tf_op jit(solution)/shard_map/reduce_scatter | solution.py:195
  (1610 shorter events, 898.1 us)
Async XLA Ops:
  11.2 176.5 %all-gather.14.cloned.1.call-start = ((), (), s32[]{:S(2)}) async-start(), calls=%async_computation.28 | async-start | bytes 1327104 | tf_op jit(solution)/shard_map/all_gather | solution.py:182
  12.8 217.1 %all-gather.22.cloned.1.call-start = ((), (), s32[]{:S(2)}) async-start(), calls=%async_computation.32 | async-start | bytes 1327104 | tf_op jit(solution)/shard_map/all_gather | solution.py:182
  14.5 325.1 %all-gather.24.cloned.1.call-start = ((), (), s32[]{:S(2)}) async-start(), calls=%async_computation.33 | async-start | bytes 7962624 | tf_op jit(solution)/shard_map/all_gather | solution.py:182
  15.9 547.4 %all-gather.26.cloned.1.call-start = ((), (), s32[]{:S(2)}) async-start(), calls=%async_computation.34 | async-start | bytes 7741440 | tf_op jit(solution)/shard_map/all_gather | solution.py:182
  18.2 628.0 %all-gather.20.cloned.1.call-start = ((), (), s32[]{:S(2)}) async-start(), calls=%async_computation.31 | async-start | bytes 1966080 | tf_op jit(solution)/shard_map/all_gather | solution.py:269
  78.9 161.1 %collective-permute-start = (bf16[3,1536,384]{2,1,0:T(8,128)(2,1)}, bf16[3,1536,384]{2,1,0:T(8,128)(2,1)}, u32[]{:S(2)}, u32[]{:S(2)}) collective-permute-start(bf16[3,1536,384]{2,1,0:T(8,128)(2,1)} %all-gather.12.cloned.1.call-done), channel_id=1, source_target_pairs={{0,16},{16,0},{1,17},{17,1},{2,18},{18,2},{3,19},{19,3},{4,20},{20... | collective-permute-start | bytes 10616840 | tf_op jit(solution)/shard_map/ppermute | solution.py:153
  187.7 162.2 %collective-permute-start.3 = (bf16[1536,384]{1,0:T(8,128)(2,1)}, bf16[1536,384]{1,0:T(8,128)(2,1)}, u32[]{:S(2)}, u32[]{:S(2)}) collective-permute-start(bf16[1536,384]{1,0:T(8,128)(2,1)} %all-gather.14.cloned.1.call-done), channel_id=1, source_target_pairs={{0,16},{16,0},{1,17},{17,1},{2,18},{18,2},{3,19},{19,3},{4,20},{20... | collective-permute-start | bytes 3538952 | tf_op jit(solution)/shard_map/ppermute | solution.py:153
  270.3 350.1 %collective-permute-start.5 = (bf16[1536,384]{1,0:T(8,128)(2,1)}, bf16[1536,384]{1,0:T(8,128)(2,1)}, u32[]{:S(2)}, u32[]{:S(2)}) collective-permute-start(bf16[1536,384]{1,0:T(8,128)(2,1)} %all-gather.14.cloned.1.call-done), channel_id=1, source_target_pairs={{0,8},{8,0},{1,9},{9,1},{2,10},{10,2},{3,11},{11,3},{4,12},{12,4},... | collective-permute-start | bytes 3538952 | tf_op jit(solution)/shard_map/ppermute | solution.py:135
  349.8 311.8 %collective-permute-start.11 = (bf16[1536,384]{1,0:T(8,128)(2,1)}, bf16[1536,384]{1,0:T(8,128)(2,1)}, u32[]{:S(2)}, u32[]{:S(2)}) collective-permute-start(bf16[1536,384]{1,0:T(8,128)(2,1)} %all-gather.22.cloned.1.call-done), channel_id=1, source_target_pairs={{0,8},{8,0},{1,9},{9,1},{2,10},{10,2},{3,11},{11,3},{4,12},{12,4},... | collective-permute-start | bytes 3538952 | tf_op jit(solution)/shard_map/ppermute | solution.py:135
  349.9 268.7 %collective-permute-start.4 = (bf16[1536,384]{1,0:T(8,128)(2,1)}, bf16[1536,384]{1,0:T(8,128)(2,1)}, u32[]{:S(2)}, u32[]{:S(2)}) collective-permute-start(bf16[1536,384]{1,0:T(8,128)(2,1)} %collective-permute-done.3), channel_id=1, source_target_pairs={{0,8},{8,0},{1,9},{9,1},{2,10},{10,2},{3,11},{11,3},{4,12},{12,4},... | collective-permute-start | bytes 3538952 | tf_op jit(solution)/shard_map/ppermute | solution.py:135
  350.4 308.7 %collective-permute-start.10 = (bf16[1536,384]{1,0:T(8,128)(2,1)}, bf16[1536,384]{1,0:T(8,128)(2,1)}, u32[]{:S(2)}, u32[]{:S(2)}) collective-permute-start(bf16[1536,384]{1,0:T(8,128)(2,1)} %collective-permute-done.9), channel_id=1, source_target_pairs={{0,8},{8,0},{1,9},{9,1},{2,10},{10,2},{3,11},{11,3},{4,12},{12,4},... | collective-permute-start | bytes 3538952 | tf_op jit(solution)/shard_map/ppermute | solution.py:135
  360.3 314.3 %collective-permute-start.12 = (bf16[1536,2240]{0,1:T(8,128)(2,1)}, bf16[1536,2240]{0,1:T(8,128)(2,1)}, u32[]{:S(2)}, u32[]{:S(2)}) collective-permute-start(bf16[1536,2240]{0,1:T(8,128)(2,1)} %copy.405), channel_id=1, source_target_pairs={{0,16},{16,0},{1,17},{17,1},{2,18},{18,2},{3,19},{19,3},{4,20},{20... | collective-permute-start | bytes 20643848 | tf_op jit(solution)/shard_map/ppermute | solution.py:153
  373.2 275.9 %all-gather.18.cloned.1.call-start = ((), (), s32[]{:S(2)}) async-start(), calls=%async_computation.30 | async-start | bytes 1966080 | tf_op jit(solution)/shard_map/all_gather | solution.py:270
  388.0 151.5 %all-to-all-start.1 = ((bf16[96,4,384]{2,0,1:T(8,128)(2,1)}), bf16[96,4,384]{2,0,1:T(8,128)(2,1)S(1)}, u32[]{:S(2)}, u32[]{:S(2)}) async-start(bf16[96,4,384]{2,0,1:T(8,128)(2,1)} %bitcast.1032), calls=%async_computation.1 | async-start | bytes 589824 | tf_op jit(solution)/shard_map/all_to_all | solution.py:252
  391.5 261.7 %all-gather.30.cloned.1.call-start = ((), (), s32[]{:S(2)}) async-start(), calls=%async_computation.36 | async-start | bytes 1966080 | tf_op jit(solution)/shard_map/all_gather | solution.py:269
  612.3 615.7 %reduce-scatter.34.cloned.1.call-start = ((), (), s32[]{:S(2)}) async-start(), calls=%async_computation.44 | async-start | bytes 1966080
  618.6 157.8 %collective-permute-start.14 = (bf16[1536,2240]{0,1:T(8,128)(2,1)}, bf16[1536,2240]{0,1:T(8,128)(2,1)}, u32[]{:S(2)}, u32[]{:S(2)}) collective-permute-start(bf16[1536,2240]{0,1:T(8,128)(2,1)} %copy.405), channel_id=1, source_target_pairs={{0,8},{8,0},{1,9},{9,1},{2,10},{10,2},{3,11},{11,3},{4,12},{12,4},... | collective-permute-start | bytes 20643848 | tf_op jit(solution)/shard_map/ppermute | solution.py:135
  1005.5 223.7 %reduce-scatter.38.cloned.1.call-start = ((), (), s32[]{:S(2)}) async-start(), calls=%async_computation.46 | async-start | bytes 1966080
  1011.3 221.5 %reduce-scatter.36.cloned.1.call-start = ((), (), s32[]{:S(2)}) async-start(), calls=%async_computation.45 | async-start | bytes 1966080
  1033.4 153.5 %collective-permute-start.39 = (bf16[1536,2240]{0,1:T(8,128)(2,1)}, bf16[1536,2240]{0,1:T(8,128)(2,1)}, u32[]{:S(2)}, u32[]{:S(2)}) collective-permute-start(bf16[1536,2240]{0,1:T(8,128)(2,1)} %fusion.1), channel_id=1, source_target_pairs={{0,8},{8,0},{1,9},{9,1},{2,10},{10,2},{3,11},{11,3},{4,12},{12,4},... | collective-permute-start | bytes 20643848 | tf_op jit(solution)/shard_map/ppermute | solution.py:135
  1041.8 192.5 %reduce-scatter.40.cloned.1.call-start = ((), (), s32[]{:S(2)}) async-start(), calls=%async_computation.47 | async-start | bytes 1966080
  1162.9 380.7 %reduce-scatter.42.cloned.1.call-start = ((), (), s32[]{:S(2)}) async-start(), calls=%async_computation.48 | async-start | bytes 884736
  1237.6 642.0 %reduce-scatter.30.cloned.1.call-start = ((), (), s32[]{:S(2)}) async-start(), calls=%async_computation.42 | async-start | bytes 7962624 | tf_op jit(solution)/shard_map/reduce_scatter | solution.py:195
  1372.4 515.0 %reduce-scatter.24.cloned.1.call-start = ((), (), s32[]{:S(2)}) async-start(), calls=%async_computation.39 | async-start | bytes 1327104 | tf_op jit(solution)/shard_map/reduce_scatter | solution.py:195
  1456.8 167.2 %collective-permute-start.44 = (bf16[8960,384]{1,0:T(8,128)(2,1)}, bf16[8960,384]{1,0:T(8,128)(2,1)}, u32[]{:S(2)}, u32[]{:S(2)}) collective-permute-start(bf16[8960,384]{1,0:T(8,128)(2,1)} %add_convert_fusion.3), channel_id=1, source_target_pairs={{0,8},{8,0},{1,9},{9,1},{2,10},{10,2},{3,11},{11,3},{4,12},{12,4},... | collective-permute-start | bytes 20643848 | tf_op jit(solution)/shard_map/ppermute | solution.py:135
  1481.7 406.0 %reduce-scatter.28.cloned.1.call-start = ((), (), s32[]{:S(2)}) async-start(), calls=%async_computation.41 | async-start | bytes 1327104 | tf_op jit(solution)/shard_map/reduce_scatter | solution.py:195
  1501.0 210.5 %collective-permute-start.43 = (bf16[8960,384]{1,0:T(8,128)(2,1)}, bf16[8960,384]{1,0:T(8,128)(2,1)}, u32[]{:S(2)}, u32[]{:S(2)}) collective-permute-start(bf16[8960,384]{1,0:T(8,128)(2,1)} %add_convert_fusion.4), channel_id=1, source_target_pairs={{0,8},{8,0},{1,9},{9,1},{2,10},{10,2},{3,11},{11,3},{4,12},{12,4},... | collective-permute-start | bytes 20643848 | tf_op jit(solution)/shard_map/ppermute | solution.py:135
  1516.4 375.5 %all-reduce.20.cloned.1.call-start = ((), (), s32[]{:S(2)}) async-start(), calls=%async_computation.37 | async-start | bytes 196608 | tf_op jit(solution)/shard_map/psum | solution.py:222
  1546.8 359.8 %reduce-scatter.22.cloned.1.call-start = ((), (), s32[]{:S(2)}) async-start(), calls=%async_computation.38 | async-start | bytes 3981312 | tf_op jit(solution)/shard_map/reduce_scatter | solution.py:195
  1598.9 309.5 %reduce-scatter.26.cloned.1.call-start = ((), (), s32[]{:S(2)}) async-start(), calls=%async_computation.40 | async-start | bytes 3981312 | tf_op jit(solution)/shard_map/reduce_scatter | solution.py:195
  1635.9 206.4 %collective-permute-start.45 = (bf16[8960,384]{1,0:T(8,128)(2,1)}, bf16[8960,384]{1,0:T(8,128)(2,1)}, u32[]{:S(2)}, u32[]{:S(2)}) collective-permute-start(bf16[8960,384]{1,0:T(8,128)(2,1)} %add_convert_fusion.2), channel_id=1, source_target_pairs={{0,16},{16,0},{1,17},{17,1},{2,18},{18,2},{3,19},{19,3},{4,20},{20... | collective-permute-start | bytes 20643848 | tf_op jit(solution)/shard_map/ppermute | solution.py:153
  1700.5 278.9 %reduce-scatter.32.cloned.1.call-start = ((), (), s32[]{:S(2)}) async-start(), calls=%async_computation.43 | async-start | bytes 7741440 | tf_op jit(solution)/shard_map/reduce_scatter | solution.py:195
  (460 other events, 10191.5 us)
Sparse Core Ops, SparseCore 0:
  10.8 68.1 all-gather.11
  81.7 63.4 all-gather.15
  148.0 39.6 all-gather.13
  190.3 39.6 all-gather.21
  232.6 106.9 all-gather.23
  342.2 104.0 all-gather.25
  447.8 26.5 all-gather.19
  475.9 28.3 all-gather.17
  505.9 28.3 all-gather.29
  572.1 21.6 all-gather.27
  983.7 25.4 reduce-scatter.33
  1011.6 31.1 reduce-scatter.37
  1045.3 27.9 reduce-scatter.35
  1087.8 26.1 reduce-scatter.39
  1237.7 59.4 reduce-scatter.41
  1372.5 126.5 reduce-scatter.29
  1503.0 63.8 reduce-scatter.23
  1570.7 63.8 reduce-scatter.27
  1636.9 30.9 all-reduce.19
  1672.0 79.3 reduce-scatter.21
  1755.1 79.0 reduce-scatter.25
  1854.9 124.4 reduce-scatter.31

commit v3 on v2

--- a/solution.py
+++ b/solution.py
@@ -159,8 +159,10 @@
 
     def apply(self, rows):
         y, core = self.spot
-        own, y_part, core_part, cross_part = (matmul(rows, part) for part in self.parts)
-        return join(join(own, y_part, y), join(core_part, cross_part, y), core)
+        outs = [matmul(rows, part) for part in self.parts]
+        if len(outs) == 2:
+            return join(outs[0], outs[1], core)
+        return join(join(outs[0], outs[1], y), join(outs[2], outs[3], y), core)
 
     def quarters(self, grad):
         y, core = self.spot
@@ -168,6 +170,9 @@
         return halves(grad_mine, y) + halves(grad_other, y)
 
     def back(self, grad):
+        if len(self.parts) == 2:
+            grad_mine, grad_other = halves(grad, self.spot[1])
+            return outer_cols(grad_mine, self.parts[0]) + outer_cols(grad_other, self.parts[1])
         pieces = [outer_cols(g, part) for g, part in zip(self.quarters(grad), self.parts)]
         return (pieces[0] + pieces[1]) + (pieces[2] + pieces[3])
 
@@ -175,8 +180,13 @@
         return tuple(inner_rows(rows, g) for g in self.quarters(grad))
 
 
-def fetch_split(local, gather_axis, spot):
+def fetch_split(local, gather_axis, spot, quarters=True):
     y, core = spot
+    if not quarters:
+        width = local.shape[-1] // 2
+        part = lax.dynamic_slice_in_dim(local, core * width, width, axis=-1)
+        mine = lax.all_gather(part, "fsdp", axis=gather_axis, tiled=True)
+        return (mine, swap_core(mine))
     width = local.shape[-1] // 4
     part = lax.dynamic_slice_in_dim(local, (2 * core + y) * width, width, axis=-1)
     own = lax.all_gather(part, "fsdp", axis=gather_axis, tiled=True)
@@ -399,8 +409,8 @@
     self_out_parts = fetch_split(self_out, 0, spot)
     cross_in_parts = fetch_split(cross_in, 1, spot)
     cross_out_parts = fetch_split(cross_out, 0, spot)
-    ffn_in_parts = fetch_split(ffn_in, 0, spot)
-    ffn_out_parts = fetch_split(ffn_out, 0, spot)
+    ffn_in_parts = fetch_split(ffn_in, 0, spot, quarters=False)
+    ffn_out_parts = fetch_split(ffn_out, 0, spot, quarters=False)
     modulation_full, gains_full, biases_full, ffn_bias_full = fetch_small(modulation, gains, biases, ffn_bias)
     weights = (
         modulation_full,

time: 2040 us -> 1950 us (0.956)
  matrix products: 576 us -> 544 us
  local copies, waits for them, and re-layouts: 174 us -> 145 us
  waiting for transfers between devices: 954 us -> 933 us
    all_to_all x2, waiting for transfers between devices: 143 us -> 1.38 us  [micro_step(): lax.all_to_all(turned[0].astype(jnp.bfloat16), SEQ, split_axis=1, concat_...]
    all_gather x0 -> x2, waiting for transfers between devices: none -> 140 us  [fetch_split(): mine = lax.all_gather(part, 'fsdp', axis=gather_axis, tiled=True)]
    all_gather x6 -> x4, waiting for transfers between devices: 231 us -> 166 us  [fetch_split(): own = lax.all_gather(part, 'fsdp', axis=gather_axis, tiled=True)]
    all_gather x2, waiting for transfers between devices: 0.17 us -> 36.9 us  [micro_step(): lax.all_gather(text_value, SEQ, axis=0, tiled=True)]
    all_gather x2, waiting for transfers between devices: 0.02 us -> 30.8 us  [micro_step(): lax.all_gather(text_key_full.astype(jnp.bfloat16), SEQ, axis=0, tiled=True)]
    ppermute x18 -> x16, waiting for transfers between devices: 467 us -> 438 us  [swap_y(): return lax.ppermute(tensor, 'y', SWAP)]
    dot_general x80 -> x72, matrix products: 152 us -> 131 us  [matmul(): return jnp.dot(operand, factor, preferred_element_type=jnp.float32)]
    dot_general x80 -> x72, matrix products: 188 us -> 177 us  [outer_cols(): lax.dot_general(operand, factor, (((1,), (1,)), ((), ())), preferred_elem...]
  transfers between devices with their start and end apart: 86 -> 82, of which waited for: 28 -> 32; matrix products, arithmetic and copies ran while one was open for 37% -> 36% of each run, Pallas kernels for 0% -> 0%
where the time goes in v3:
time: 1950 us; the launch traced here: 1930 us
  waiting for transfers between devices  933 us (48%)
  matrix products  544 us (28%)
  other arithmetic  166 us (9%)
  local copies, waits for them, and re-layouts  145 us (7%)
  starting transfers between devices  88.8 us (5%)
  blocking collectives  33 us (2%)
  between operations  20.9 us (1%)
    ppermute x16, waiting for transfers between devices, swap_y(): return lax.ppermute(tensor, 'y', SWAP)  438 us
    dot_general x80, matrix products, inner_rows(): lax.dot_general(operand, factor, (((0,), (0,)), ((), ())), preferred_elem...  205 us
    dot_general x72, matrix products, outer_cols(): lax.dot_general(operand, factor, (((1,), (1,)), ((), ())), preferred_elem...  177 us
    all_gather x4, waiting for transfers between devices, fetch_split(): own = lax.all_gather(part, 'fsdp', axis=gather_axis, tiled=True)  166 us
    all_gather x2, waiting for transfers between devices, fetch_split(): mine = lax.all_gather(part, 'fsdp', axis=gather_axis, tiled=True)  140 us
    dot_general x72, matrix products, matmul(): return jnp.dot(operand, factor, preferred_element_type=jnp.float32)  131 us
    reduce_scatter x6, waiting for transfers between devices, reduce_split(): lax.psum_scatter(total, 'fsdp', scatter_dimension=scatter_axis, tiled=True)  80.4 us
    convert_element_type x6, other arithmetic, reduce_split(): total = (chip_own + swap_y(chip_y).astype(jnp.float32)).astype(jnp.bfloat16)  45.5 us
  transfers between devices with their start and end apart: 82, of which 32 were waited for; matrix products, arithmetic and copies ran while one was open for 36% of the time, Pallas kernels for 0%

profile of v3, /device:TPU:0, one launch (start us, length us, event | category | flops | bytes accessed | tf_op | source)
XLA Modules:
  0.0 1931.8 jit_solution(1022058168821942538)
XLA Ops:
  19.0 33.0 %all-gather = bf16[8,192,27]{1,2,0:T(8,128)(2,1)S(1)} all-gather(bf16[1,192,27]{1,2,0:T(8,128)(2,1)S(1)} %maximum_bitcast_fusion), channel_id=1, replica_groups=mesh['y'=2,'core'=2,'fsdp'=8] {'fsdp'}, dimensions={0}, use_global_device_ids=true | all-gather | bytes 93312 | tf_op jit(solution)/shard_map/all_gather | solution.py:217
  55.5 23.5 %all-gather.12.cloned.1.call-done = bf16[3,1536,384]{2,1,0:T(8,128)(2,1)} async-done(((bf16[3,192,384]{2,1,0:T(8,128)(2,1)}), bf16[3,1536,384]{2,1,0:T(8,128)(2,1)}) %all-gather.12.cloned.1.call-update) | async-done | bytes 3538960 | tf_op jit(solution)/shard_map/all_gather | solution.py:192
  84.5 37.1 %all-gather.14.cloned.1.call-done = bf16[1536,384]{1,0:T(8,128)(2,1)} async-done(((bf16[192,384]{1,0:T(8,128)(2,1)}), bf16[1536,384]{1,0:T(8,128)(2,1)}) %all-gather.14.cloned.1.call-update) | async-done | bytes 1179664 | tf_op jit(solution)/shard_map/all_gather | solution.py:192
  123.1 40.9 %all-gather.22.cloned.1.call-done = bf16[1536,384]{1,0:T(8,128)(2,1)} async-done(((bf16[192,384]{1,0:T(8,128)(2,1)}), bf16[1536,384]{1,0:T(8,128)(2,1)}) %all-gather.22.cloned.1.call-update) | async-done | bytes 1179664 | tf_op jit(solution)/shard_map/all_gather | solution.py:192
  165.5 64.5 %all-gather.16.cloned.1.call-done = bf16[3,1536,384]{2,1,0:T(8,128)(2,1)} async-done(((bf16[3,192,384]{2,1,0:T(8,128)(2,1)}), bf16[3,1536,384]{2,1,0:T(8,128)(2,1)}) %all-gather.16.cloned.1.call-update) | async-done | bytes 3538960 | tf_op jit(solution)/shard_map/all_gather | solution.py:192
  249.5 57.3 %collective-permute-done.6 = bf16[3,1536,384]{2,1,0:T(8,128)(2,1)S(1)} collective-permute-done((bf16[3,1536,384]{2,1,0:T(8,128)(2,1)}, bf16[3,1536,384]{2,1,0:T(8,128)(2,1)S(1)}, u32[]{:S(2)}, u32[]{:S(2)}) %collective-permute-start.6) | collective-permute-done | bytes 3538976 | tf_op jit(solution)/shard_map/ppermute | solution.py:153
  473.7 139.5 %all-gather.26.cloned.1.call-done = bf16[8960,768]{1,0:T(8,128)(2,1)} async-done(((bf16[1120,768]{1,0:T(8,128)(2,1)}), bf16[8960,768]{1,0:T(8,128)(2,1)}) %all-gather.26.cloned.1.call-update) | async-done | bytes 13762576 | tf_op jit(solution)/shard_map/all_gather | solution.py:188
  613.2 19.9 %all-gather.20.cloned.1.call-done = bf16[512,1536]{0,1:T(8,128)(2,1)} async-done(((bf16[128,1536]{0,1:T(8,128)(2,1)}), bf16[512,1536]{0,1:T(8,128)(2,1)}) %all-gather.20.cloned.1.call-update) | async-done | bytes 1572880 | tf_op jit(solution)/shard_map/all_gather | solution.py:279
  635.8 18.6 all-gather.18.cloned.1.call-done
  665.0 10.9 all-gather.30.cloned.1.call-done
  678.9 18.2 all-gather.28.cloned.1.call-done
  708.1 11.0 fusion.508
  753.6 10.1 convert_reduce_fusion.1
  763.7 9.8 fusion.130
  773.5 9.9 multiply_reduce_fusion.16
  824.4 10.6 fusion.127
  835.0 10.8 multiply_reduce_fusion.14
  958.2 12.1 convolution_add_fusion.3
  1091.9 11.7 add_convert_fusion.5
  1143.3 10.2 copy.384
  1153.5 100.8 %collective-permute-done.36 = bf16[1536,2240]{0,1:T(8,128)(2,1)} collective-permute-done((bf16[1536,2240]{0,1:T(8,128)(2,1)}, bf16[1536,2240]{0,1:T(8,128)(2,1)}, u32[]{:S(2)}, u32[]{:S(2)}) %collective-permute-start.36) | collective-permute-done | bytes 6881312 | tf_op jit(solution)/shard_map/ppermute | solution.py:153
  1263.8 13.0 add_convert_fusion
  1318.4 10.1 add_convert_fusion.3
  1363.2 21.9 %collective-permute-done.21 = bf16[1536,384]{1,0:T(8,128)(2,1)S(1)} collective-permute-done((bf16[1536,384]{1,0:T(8,128)(2,1)S(1)}, bf16[1536,384]{1,0:T(8,128)(2,1)S(1)}, u32[]{:S(2)}, u32[]{:S(2)}) %collective-permute-start.21) | collective-permute-done | bytes 1179680 | tf_op jit(solution)/shard_map/ppermute | solution.py:153
  1406.7 12.9 collective-permute-done.31
  1450.2 44.9 %collective-permute-done.16 = bf16[3,1536,384]{2,1,0:T(8,128)(2,1)} collective-permute-done((bf16[3,1536,384]{2,1,0:T(8,128)(2,1)}, bf16[3,1536,384]{2,1,0:T(8,128)(2,1)}, u32[]{:S(2)}, u32[]{:S(2)}) %collective-permute-start.16) | collective-permute-done | bytes 3538976 | tf_op jit(solution)/shard_map/ppermute | solution.py:153
  1495.2 9.9 fusion.4
  1529.2 11.9 add_convert_fusion.2
  1547.5 54.5 %collective-permute-done.26 = bf16[3,1536,384]{2,1,0:T(8,128)(2,1)} collective-permute-done((bf16[3,1536,384]{2,1,0:T(8,128)(2,1)}, bf16[3,1536,384]{2,1,0:T(8,128)(2,1)}, u32[]{:S(2)}, u32[]{:S(2)}) %collective-permute-start.26) | collective-permute-done | bytes 3538976 | tf_op jit(solution)/shard_map/ppermute | solution.py:153
  1616.8 131.7 %collective-permute-done.41 = bf16[8960,384]{1,0:T(8,128)(2,1)} collective-permute-done((bf16[8960,384]{1,0:T(8,128)(2,1)}, bf16[8960,384]{1,0:T(8,128)(2,1)}, u32[]{:S(2)}, u32[]{:S(2)}) %collective-permute-start.41) | collective-permute-done | bytes 6881312 | tf_op jit(solution)/shard_map/ppermute | solution.py:153
  1748.5 12.4 add_convert_fusion.1
  1808.6 80.4 %reduce-scatter.32.cloned.1.call-done = bf16[1120,384]{1,0:T(8,128)(2,1)} async-done(((bf16[8960,384]{1,0:T(8,128)(2,1)}), bf16[1120,384]{1,0:T(8,128)(2,1)}) %reduce-scatter.32.cloned.1.call-update) | async-done | bytes 860176 | tf_op jit(solution)/shard_map/reduce_scatter | solution.py:205
  (1463 shorter events, 846.8 us)
Async XLA Ops:
  10.9 153.1 %all-gather.22.cloned.1.call-start = ((), (), s32[]{:S(2)}) async-start(), calls=%async_computation.32 | async-start | bytes 1327104 | tf_op jit(solution)/shard_map/all_gather | solution.py:192
  12.6 217.4 %all-gather.16.cloned.1.call-start = ((), (), s32[]{:S(2)}) async-start(), calls=%async_computation.29 | async-start | bytes 3981312 | tf_op jit(solution)/shard_map/all_gather | solution.py:192
  14.5 447.7 %all-gather.24.cloned.1.call-start = ((), (), s32[]{:S(2)}) async-start(), calls=%async_computation.33 | async-start | bytes 15482880 | tf_op jit(solution)/shard_map/all_gather | solution.py:188
  15.9 597.3 %all-gather.26.cloned.1.call-start = ((), (), s32[]{:S(2)}) async-start(), calls=%async_computation.34 | async-start | bytes 15482880 | tf_op jit(solution)/shard_map/all_gather | solution.py:188
  18.8 614.3 %all-gather.20.cloned.1.call-start = ((), (), s32[]{:S(2)}) async-start(), calls=%async_computation.31 | async-start | bytes 1966080 | tf_op jit(solution)/shard_map/all_gather | solution.py:279
  78.9 161.1 %collective-permute-start = (bf16[3,1536,384]{2,1,0:T(8,128)(2,1)}, bf16[3,1536,384]{2,1,0:T(8,128)(2,1)}, u32[]{:S(2)}, u32[]{:S(2)}) collective-permute-start(bf16[3,1536,384]{2,1,0:T(8,128)(2,1)} %all-gather.12.cloned.1.call-done), channel_id=1, source_target_pairs={{0,16},{16,0},{1,17},{17,1},{2,18},{18,2},{3,19},{19,3},{4,20},{20... | collective-permute-start | bytes 10616840 | tf_op jit(solution)/shard_map/ppermute | solution.py:153
  121.6 278.6 %collective-permute-start.3 = (bf16[1536,384]{1,0:T(8,128)(2,1)}, bf16[1536,384]{1,0:T(8,128)(2,1)}, u32[]{:S(2)}, u32[]{:S(2)}) collective-permute-start(bf16[1536,384]{1,0:T(8,128)(2,1)} %all-gather.14.cloned.1.call-done), channel_id=1, source_target_pairs={{0,16},{16,0},{1,17},{17,1},{2,18},{18,2},{3,19},{19,3},{4,20},{20... | collective-permute-start | bytes 3538952 | tf_op jit(solution)/shard_map/ppermute | solution.py:153
  164.0 236.6 %collective-permute-start.9 = (bf16[1536,384]{1,0:T(8,128)(2,1)}, bf16[1536,384]{1,0:T(8,128)(2,1)}, u32[]{:S(2)}, u32[]{:S(2)}) collective-permute-start(bf16[1536,384]{1,0:T(8,128)(2,1)} %all-gather.22.cloned.1.call-done), channel_id=1, source_target_pairs={{0,16},{16,0},{1,17},{17,1},{2,18},{18,2},{3,19},{19,3},{4,20},{20... | collective-permute-start | bytes 3538952 | tf_op jit(solution)/shard_map/ppermute | solution.py:153
  339.6 314.8 %all-gather.18.cloned.1.call-start = ((), (), s32[]{:S(2)}) async-start(), calls=%async_computation.30 | async-start | bytes 1966080 | tf_op jit(solution)/shard_map/all_gather | solution.py:280
  350.5 325.4 %all-gather.30.cloned.1.call-start = ((), (), s32[]{:S(2)}) async-start(), calls=%async_computation.36 | async-start | bytes 1966080 | tf_op jit(solution)/shard_map/all_gather | solution.py:279
  397.2 299.9 %all-gather.28.cloned.1.call-start = ((), (), s32[]{:S(2)}) async-start(), calls=%async_computation.35 | async-start | bytes 1966080 | tf_op jit(solution)/shard_map/all_gather | solution.py:280
  400.1 258.3 %collective-permute-start.11 = (bf16[1536,384]{1,0:T(8,128)(2,1)}, bf16[1536,384]{1,0:T(8,128)(2,1)}, u32[]{:S(2)}, u32[]{:S(2)}) collective-permute-start(bf16[1536,384]{1,0:T(8,128)(2,1)} %all-gather.22.cloned.1.call-done), channel_id=1, source_target_pairs={{0,8},{8,0},{1,9},{9,1},{2,10},{10,2},{3,11},{11,3},{4,12},{12,4},... | collective-permute-start | bytes 3538952 | tf_op jit(solution)/shard_map/ppermute | solution.py:135
  400.6 256.0 %collective-permute-start.10 = (bf16[1536,384]{1,0:T(8,128)(2,1)}, bf16[1536,384]{1,0:T(8,128)(2,1)}, u32[]{:S(2)}, u32[]{:S(2)}) collective-permute-start(bf16[1536,384]{1,0:T(8,128)(2,1)} %collective-permute-done.9), channel_id=1, source_target_pairs={{0,8},{8,0},{1,9},{9,1},{2,10},{10,2},{3,11},{11,3},{4,12},{12,4},... | collective-permute-start | bytes 3538952 | tf_op jit(solution)/shard_map/ppermute | solution.py:135
  440.1 693.5 %reduce-scatter.34.cloned.1.call-start = ((), (), s32[]{:S(2)}) async-start(), calls=%async_computation.44 | async-start | bytes 1966080
  462.2 271.3 %collective-permute-start.12 = (bf16[1536,4480]{1,0:T(8,128)(2,1)}, bf16[1536,4480]{1,0:T(8,128)(2,1)}, u32[]{:S(2)}, u32[]{:S(2)}) collective-permute-start(bf16[1536,4480]{1,0:T(8,128)(2,1)} %all-gather.24.cloned.1.call-done), channel_id=1, source_target_pairs={{0,8},{8,0},{1,9},{9,1},{2,10},{10,2},{3,11},{11,3},{4,12},{12,4},... | collective-permute-start | bytes 41287688 | tf_op jit(solution)/shard_map/ppermute | solution.py:135
  905.5 229.4 %reduce-scatter.38.cloned.1.call-start = ((), (), s32[]{:S(2)}) async-start(), calls=%async_computation.46 | async-start | bytes 1966080
  911.3 227.3 %reduce-scatter.36.cloned.1.call-start = ((), (), s32[]{:S(2)}) async-start(), calls=%async_computation.45 | async-start | bytes 1966080
  933.1 158.8 %collective-permute-start.35 = (bf16[1536,2240]{0,1:T(8,128)(2,1)}, bf16[1536,2240]{0,1:T(8,128)(2,1)}, u32[]{:S(2)}, u32[]{:S(2)}) collective-permute-start(bf16[1536,2240]{0,1:T(8,128)(2,1)} %fusion.1), channel_id=1, source_target_pairs={{0,8},{8,0},{1,9},{9,1},{2,10},{10,2},{3,11},{11,3},{4,12},{12,4},... | collective-permute-start | bytes 20643848 | tf_op jit(solution)/shard_map/ppermute | solution.py:135
  941.6 198.4 %reduce-scatter.40.cloned.1.call-start = ((), (), s32[]{:S(2)}) async-start(), calls=%async_computation.47 | async-start | bytes 1966080
  985.9 157.4 %collective-permute-start.34 = (bf16[1536,2240]{0,1:T(8,128)(2,1)}, bf16[1536,2240]{0,1:T(8,128)(2,1)}, u32[]{:S(2)}, u32[]{:S(2)}) collective-permute-start(bf16[1536,2240]{0,1:T(8,128)(2,1)} %fusion), channel_id=1, source_target_pairs={{0,8},{8,0},{1,9},{9,1},{2,10},{10,2},{3,11},{11,3},{4,12},{12,4},... | collective-permute-start | bytes 20643848 | tf_op jit(solution)/shard_map/ppermute | solution.py:135
  1062.2 386.2 %reduce-scatter.42.cloned.1.call-start = ((), (), s32[]{:S(2)}) async-start(), calls=%async_computation.48 | async-start | bytes 884736
  1103.6 150.7 %collective-permute-start.36 = (bf16[1536,2240]{0,1:T(8,128)(2,1)}, bf16[1536,2240]{0,1:T(8,128)(2,1)}, u32[]{:S(2)}, u32[]{:S(2)}) collective-permute-start(bf16[1536,2240]{0,1:T(8,128)(2,1)} %add_convert_fusion.5), channel_id=1, source_target_pairs={{0,16},{16,0},{1,17},{17,1},{2,18},{18,2},{3,19},{19,3},{4,20},{20... | collective-permute-start | bytes 20643848 | tf_op jit(solution)/shard_map/ppermute | solution.py:153
  1143.3 635.3 %reduce-scatter.30.cloned.1.call-start = ((), (), s32[]{:S(2)}) async-start(), calls=%async_computation.42 | async-start | bytes 7962624 | tf_op jit(solution)/shard_map/reduce_scatter | solution.py:205
  1276.9 509.3 %reduce-scatter.24.cloned.1.call-start = ((), (), s32[]{:S(2)}) async-start(), calls=%async_computation.39 | async-start | bytes 1327104 | tf_op jit(solution)/shard_map/reduce_scatter | solution.py:205
  1363.0 166.2 %collective-permute-start.40 = (bf16[8960,384]{1,0:T(8,128)(2,1)}, bf16[8960,384]{1,0:T(8,128)(2,1)}, u32[]{:S(2)}, u32[]{:S(2)}) collective-permute-start(bf16[8960,384]{1,0:T(8,128)(2,1)} %add_convert_fusion.3), channel_id=1, source_target_pairs={{0,8},{8,0},{1,9},{9,1},{2,10},{10,2},{3,11},{11,3},{4,12},{12,4},... | collective-permute-start | bytes 20643848 | tf_op jit(solution)/shard_map/ppermute | solution.py:135
  1387.9 398.8 %reduce-scatter.28.cloned.1.call-start = ((), (), s32[]{:S(2)}) async-start(), calls=%async_computation.41 | async-start | bytes 1327104 | tf_op jit(solution)/shard_map/reduce_scatter | solution.py:205
  1406.5 210.3 %collective-permute-start.39 = (bf16[8960,384]{1,0:T(8,128)(2,1)}, bf16[8960,384]{1,0:T(8,128)(2,1)}, u32[]{:S(2)}, u32[]{:S(2)}) collective-permute-start(bf16[8960,384]{1,0:T(8,128)(2,1)} %add_convert_fusion.4), channel_id=1, source_target_pairs={{0,8},{8,0},{1,9},{9,1},{2,10},{10,2},{3,11},{11,3},{4,12},{12,4},... | collective-permute-start | bytes 20643848 | tf_op jit(solution)/shard_map/ppermute | solution.py:135
  1422.4 368.2 %all-reduce.20.cloned.1.call-start = ((), (), s32[]{:S(2)}) async-start(), calls=%async_computation.37 | async-start | bytes 196608 | tf_op jit(solution)/shard_map/psum | solution.py:232
  1450.2 356.4 %reduce-scatter.22.cloned.1.call-start = ((), (), s32[]{:S(2)}) async-start(), calls=%async_computation.38 | async-start | bytes 3981312 | tf_op jit(solution)/shard_map/reduce_scatter | solution.py:205
  1505.0 303.3 %reduce-scatter.26.cloned.1.call-start = ((), (), s32[]{:S(2)}) async-start(), calls=%async_computation.40 | async-start | bytes 3981312 | tf_op jit(solution)/shard_map/reduce_scatter | solution.py:205
  1541.1 207.4 %collective-permute-start.41 = (bf16[8960,384]{1,0:T(8,128)(2,1)}, bf16[8960,384]{1,0:T(8,128)(2,1)}, u32[]{:S(2)}, u32[]{:S(2)}) collective-permute-start(bf16[8960,384]{1,0:T(8,128)(2,1)} %add_convert_fusion.2), channel_id=1, source_target_pairs={{0,16},{16,0},{1,17},{17,1},{2,18},{18,2},{3,19},{19,3},{4,20},{20... | collective-permute-start | bytes 20643848 | tf_op jit(solution)/shard_map/ppermute | solution.py:153
  1606.7 282.3 %reduce-scatter.32.cloned.1.call-start = ((), (), s32[]{:S(2)}) async-start(), calls=%async_computation.43 | async-start | bytes 7741440 | tf_op jit(solution)/shard_map/reduce_scatter | solution.py:205
  (402 other events, 9616.6 us)
Sparse Core Ops, SparseCore 0:
  10.8 68.1 all-gather.11
  81.7 39.8 all-gather.13
  124.4 39.6 all-gather.21
  166.7 63.2 all-gather.15
  232.6 189.1 all-gather.23
  424.5 188.7 all-gather.25
  614.8 18.2 all-gather.19
  634.6 19.7 all-gather.17
  656.0 19.8 all-gather.29
  677.3 19.8 all-gather.27
  884.2 30.5 reduce-scatter.33
  917.2 28.2 reduce-scatter.37
  948.0 27.9 reduce-scatter.35
  986.2 32.7 reduce-scatter.39
  1143.4 63.2 reduce-scatter.41
  1277.0 130.2 reduce-scatter.29
  1411.1 63.8 reduce-scatter.23
  1478.8 63.7 reduce-scatter.27
  1544.9 31.0 all-reduce.19
  1579.5 79.3 reduce-scatter.21
  1662.6 79.0 reduce-scatter.25
  1761.1 127.8 reduce-scatter.31

commit v4 on v3

--- a/solution.py
+++ b/solution.py
@@ -236,7 +236,7 @@
     return owned[:6], owned[6:11], owned[11:21], bias_owned, grad_time
 
 
-def micro_step(weights, hidden, text, time_emb, places, cotangent):
+def micro_step(weights, hidden, key_all, value_all, time_emb, places, cotangent):
     modulation, self_q, self_k, self_v, self_o, cross_q, cross_k, cross_v, cross_o, ffn_in, ffn_out, gains, biases, ffn_bias = (
         weights
     )
@@ -272,13 +272,6 @@
     cross_query_pre = cross_q.apply(crossed) + bias_rows[4]
     cross_query_full, pull_cross_query = jax.vjp(rms_norm, cross_query_pre, gain_rows[2])
     cross_query = cross_query_full.astype(jnp.bfloat16)
-    text_key_pre = cross_k.apply(text) + bias_rows[5]
-    text_key_full, pull_text_key = jax.vjp(rms_norm, text_key_pre, gain_rows[3])
-    text_value = (cross_v.apply(text) + bias_rows[6]).astype(jnp.bfloat16)
-    key_all, value_all = (
-        lax.all_gather(text_key_full.astype(jnp.bfloat16), SEQ, axis=0, tiled=True),
-        lax.all_gather(text_value, SEQ, axis=0, tiled=True),
-    )
     cross_rows, cross_total = attend(cross_query, key_all, value_all)
     second = after_attn + cross_o.apply(cross_rows) + bias_rows[7]
     ffn_normed_full, pull_second = jax.vjp(modulate_norm, second, modulated[3], modulated[4])
@@ -291,40 +284,21 @@
     grad_output = cotangent.astype(jnp.float32)
     gate_ffn = jnp.sum(grad_output * ffn_branch, axis=0)
     grad_ffn_branch = (grad_output * modulated[5]).astype(jnp.bfloat16)
-    weight_ffn_out = ffn_out.grad(activation, grad_ffn_branch)
     grad_pre_full = pull_gelu(ffn_out.back(grad_ffn_branch))[0]
     grad_pre = grad_pre_full.astype(jnp.bfloat16)
-    weight_ffn_in = ffn_in.grad(ffn_normed, grad_pre)
     grad_second_part, shift_ffn, scale_ffn = pull_second(ffn_in.back(grad_pre))
     grad_second = grad_output + grad_second_part
     grad_cross_branch = grad_second.astype(jnp.bfloat16)
-    weight_cross_out = cross_o.grad(cross_rows, grad_cross_branch)
     grad_cross_rows = cross_o.back(grad_cross_branch).astype(jnp.bfloat16)
     grad_cross_query, grad_key_all, grad_value_all = attend_back(
         cross_query, key_all, value_all, cross_total, grad_cross_rows
     )
-    grad_text_key, grad_text_value_full = (
-        lax.psum_scatter(
-            grad_key_all.astype(jnp.bfloat16), SEQ, scatter_dimension=0, tiled=True
-        ).astype(jnp.float32),
-        lax.psum_scatter(
-            grad_value_all.astype(jnp.bfloat16), SEQ, scatter_dimension=0, tiled=True
-        ).astype(jnp.float32),
-    )
-    grad_text_value = grad_text_value_full.astype(jnp.bfloat16)
-    grad_text_key_full, gain_cross_key = pull_text_key(grad_text_key)
-    grad_text_key_pre = grad_text_key_full.astype(jnp.bfloat16)
-    weight_cross_key = cross_k.grad(text, grad_text_key_pre)
-    weight_cross_value = cross_v.grad(text, grad_text_value)
-    grad_words = cross_k.back(grad_text_key_pre) + cross_v.back(grad_text_value)
     grad_cross_query_full, gain_cross_query = pull_cross_query(grad_cross_query)
     grad_cross_query_pre = grad_cross_query_full.astype(jnp.bfloat16)
-    weight_cross_query = cross_q.grad(crossed, grad_cross_query_pre)
     grad_after_part, gain_norm, bias_norm = pull_cross(cross_q.back(grad_cross_query_pre))
     grad_after = grad_second + grad_after_part
     gate_attn = jnp.sum(grad_after * branch, axis=0)
     grad_branch = (grad_after * modulated[2]).astype(jnp.bfloat16)
-    weight_self_out = self_o.grad(attended, grad_branch)
     grad_attended = self_o.back(grad_branch).astype(jnp.bfloat16)
     grad_attn_heads = lax.all_to_all(grad_attended, SEQ, split_axis=1, concat_axis=0, tiled=True)
     grad_query_heads, grad_key_heads, grad_value_heads = attend_back(
@@ -346,14 +320,11 @@
     )
     grad_query_pre = grad_query_full.astype(jnp.bfloat16)
     grad_key_pre = grad_key_full.astype(jnp.bfloat16)
-    weight_self_query = self_q.grad(normed, grad_query_pre)
-    weight_self_key = self_k.grad(normed, grad_key_pre)
-    weight_self_value = self_v.grad(normed, grad_value)
     grad_normed = self_q.back(grad_query_pre) + self_k.back(grad_key_pre) + self_v.back(grad_value)
     grad_start, shift_attn, scale_attn = pull_first(grad_normed)
     grad_hidden = grad_after + grad_start
     grad_modulated = jnp.stack((shift_attn, scale_attn, gate_attn, shift_ffn, scale_ffn, gate_ffn))
-    grad_gains = jnp.stack((gain_query, gain_key, gain_cross_query, gain_cross_key, gain_norm))
+    grad_gains = jnp.stack((gain_query, gain_key, gain_cross_query, jnp.zeros_like(gain_query), gain_norm))
     grad_biases = jnp.stack(
         (
             column_sums(grad_query_pre),
@@ -361,28 +332,25 @@
             column_sums(grad_value),
             column_sums(grad_branch),
             column_sums(grad_cross_query_pre),
-            column_sums(grad_text_key_pre),
-            column_sums(grad_text_value),
+            jnp.zeros_like(bias_norm),
+            jnp.zeros_like(bias_norm),
             column_sums(grad_cross_branch),
             bias_norm,
             column_sums(grad_ffn_branch),
         )
     )
     small = (grad_modulated, grad_gains, grad_biases, column_sums(grad_pre))
-    stacked = []
-    for group in (
-        (weight_self_query, weight_self_key, weight_self_value),
-        (weight_self_out,),
-        (weight_cross_query, weight_cross_key, weight_cross_value),
-        (weight_cross_out,),
-        (weight_ffn_in,),
-        (weight_ffn_out,),
-    ):
-        for quarter in range(4):
-            parts = tuple(w[quarter] for w in group)
-            stacked.append(jnp.stack(parts) if len(parts) > 1 else parts[0])
-    split = tuple(stacked)
-    return (mixed, grad_hidden, grad_words, grad_modulated, small, split)
+    split = (
+        (normed, grad_query_pre),
+        (normed, grad_key_pre),
+        (normed, grad_value),
+        (attended, grad_branch),
+        (crossed, grad_cross_query_pre),
+        (cross_rows, grad_cross_branch),
+        (ffn_normed, grad_pre),
+        (activation, grad_ffn_branch),
+    )
+    return (mixed, grad_hidden, (grad_key_all, grad_value_all), grad_modulated, small, split)
 
 
 def body(
@@ -405,73 +373,123 @@
     spot = (lax.axis_index("y"), lax.axis_index("core"))
     width = modulation.shape[1]
     length = ffn_bias.shape[0]
-    self_in_parts = fetch_split(self_in, 1, spot)
-    self_out_parts = fetch_split(self_out, 0, spot)
-    cross_in_parts = fetch_split(cross_in, 1, spot)
-    cross_out_parts = fetch_split(cross_out, 0, spot)
+    heads_in = self_in.shape[0]
+    attn_in_parts = fetch_split(jnp.concatenate([self_in, cross_in], axis=0), 1, spot)
+    attn_out_parts = fetch_split(jnp.stack([self_out, cross_out]), 1, spot)
     ffn_in_parts = fetch_split(ffn_in, 0, spot, quarters=False)
     ffn_out_parts = fetch_split(ffn_out, 0, spot, quarters=False)
     modulation_full, gains_full, biases_full, ffn_bias_full = fetch_small(modulation, gains, biases, ffn_bias)
+    in_split = [Split(tuple(part[i] for part in attn_in_parts), spot) for i in range(2 * heads_in)]
+    out_split = [Split(tuple(part[i] for part in attn_out_parts), spot) for i in range(2)]
     weights = (
         modulation_full,
-        Split(tuple(part[0] for part in self_in_parts), spot),
-        Split(tuple(part[1] for part in self_in_parts), spot),
-        Split(tuple(part[2] for part in self_in_parts), spot),
-        Split(self_out_parts, spot),
-        Split(tuple(part[0] for part in cross_in_parts), spot),
-        Split(tuple(part[1] for part in cross_in_parts), spot),
-        Split(tuple(part[2] for part in cross_in_parts), spot),
-        Split(cross_out_parts, spot),
+        in_split[0],
+        in_split[1],
+        in_split[2],
+        out_split[0],
+        in_split[3],
+        in_split[4],
+        in_split[5],
+        out_split[1],
         Split(ffn_in_parts, spot),
         Split(ffn_out_parts, spot),
         gains_full,
         biases_full,
         ffn_bias_full,
     )
+    cross_k, cross_v = in_split[4], in_split[5]
+    gain_rows = gains_full.astype(jnp.float32)
+    bias_rows = biases_full.astype(jnp.float32)
+    clips, words, model = text.shape
+    text_flat = text.reshape(clips * words, model)
+    text_key_pre = cross_k.apply(text_flat) + bias_rows[5]
+    text_key_full, pull_text_key = jax.vjp(rms_norm, text_key_pre, gain_rows[3])
+    text_value = (cross_v.apply(text_flat) + bias_rows[6]).astype(jnp.bfloat16)
+    text_key_low = text_key_full.astype(jnp.bfloat16)
+    local_kv = jnp.concatenate(
+        [part[i * words : (i + 1) * words] for part in (text_key_low, text_value) for i in range(clips)], axis=1
+    )
+    all_kv = lax.all_gather(local_kv, SEQ, axis=0, tiled=True)
     mixed_list = []
     hidden_list = []
-    words_list = []
+    key_grads = []
+    value_grads = []
     clock_list = []
     small_totals = None
-    split_totals = None
-    for batch_index in range(hidden.shape[0]):
-        mixed, grad_hidden, grad_words, grad_clock, small, split = micro_step(
+    pair_lists = None
+    for batch_index in range(clips):
+        mixed, grad_hidden, text_grads, grad_clock, small, split = micro_step(
             weights,
             hidden[batch_index],
-            text[batch_index],
+            all_kv[:, batch_index * model : (batch_index + 1) * model],
+            all_kv[:, (clips + batch_index) * model : (clips + batch_index + 1) * model],
             time_emb[batch_index],
             positions[batch_index],
             cotangent[batch_index],
         )
         mixed_list.append(mixed)
         hidden_list.append(grad_hidden)
-        words_list.append(grad_words)
+        key_grads.append(text_grads[0])
+        value_grads.append(text_grads[1])
         clock_list.append(grad_clock)
         if small_totals is None:
-            small_totals, split_totals = small, split
+            small_totals, pair_lists = small, [[pair] for pair in split]
         else:
             small_totals = tuple(a + b for a, b in zip(small_totals, small))
-            split_totals = tuple(a + b for a, b in zip(split_totals, split))
+            for found, pair in zip(pair_lists, split):
+                found.append(pair)
+    pairs = [
+        (jnp.concatenate([p[0] for p in found]), jnp.concatenate([p[1] for p in found]))
+        for found in pair_lists
+    ]
+    split_grads = [
+        split_weight.grad(rows, grad)
+        for split_weight, (rows, grad) in zip(
+            (in_split[0], in_split[1], in_split[2], out_split[0], in_split[3], out_split[1], weights[9], weights[10]),
+            pairs,
+        )
+    ]
+    grad_kv = jnp.concatenate(key_grads + value_grads, axis=1).astype(jnp.bfloat16)
+    owned_kv = lax.psum_scatter(grad_kv, SEQ, scatter_dimension=0, tiled=True).astype(jnp.float32)
+    owned_parts = [owned_kv[:, i * model : (i + 1) * model] for i in range(2 * clips)]
+    grad_text_key = jnp.concatenate(owned_parts[:clips], axis=0)
+    grad_text_value = jnp.concatenate(owned_parts[clips:], axis=0).astype(jnp.bfloat16)
+    grad_text_key_full, gain_cross_key = pull_text_key(grad_text_key)
+    grad_text_key_pre = grad_text_key_full.astype(jnp.bfloat16)
+    weight_cross_key = cross_k.grad(text_flat, grad_text_key_pre)
+    weight_cross_value = cross_v.grad(text_flat, grad_text_value)
+    grad_words = cross_k.back(grad_text_key_pre) + cross_v.back(grad_text_value)
+    grad_mod, grad_gains, grad_biases, grad_ffn_bias_local = small_totals
+    grad_gains = grad_gains.at[3].add(gain_cross_key)
+    grad_biases = grad_biases.at[5].add(column_sums(grad_text_key_pre))
+    grad_biases = grad_biases.at[6].add(column_sums(grad_text_value))
+    attn_in_grads = tuple(
+        jnp.stack(
+            [split_grads[0][q], split_grads[1][q], split_grads[2][q], split_grads[4][q], weight_cross_key[q], weight_cross_value[q]]
+        )
+        for q in range(4)
+    )
+    attn_out_grads = tuple(jnp.stack([split_grads[3][q], split_grads[5][q]]) for q in range(4))
+    attn_in_final = reduce_split(attn_in_grads, 1, spot)
+    attn_out_final = reduce_split(attn_out_grads, 1, spot)
+    ffn_in_final = reduce_split(split_grads[6], 0, spot)
+    ffn_out_final = reduce_split(split_grads[7], 0, spot)
     grad_time = jnp.stack(clock_list)
-    finals = [
-        reduce_split(split_totals[4 * i : 4 * i + 4], axis, spot)
-        for i, axis in enumerate((1, 0, 1, 0, 0, 0))
-    ]
     grad_mod, grad_gains, grad_biases, grad_ffn_bias, grad_time = reduce_small(
-        *small_totals, grad_time, width, length
+        grad_mod, grad_gains, grad_biases, grad_ffn_bias_local, grad_time, width, length
     )
     return (
         jnp.stack(mixed_list),
         jnp.stack(hidden_list),
-        jnp.stack(words_list),
+        grad_words.reshape(clips, words, model),
         grad_time,
         grad_mod,
-        finals[0],
-        finals[1],
-        finals[2],
-        finals[3],
-        finals[4],
-        finals[5],
+        attn_in_final[:heads_in],
+        attn_out_final[0],
+        attn_in_final[heads_in:],
+        attn_out_final[1],
+        ffn_in_final,
+        ffn_out_final,
         grad_gains,
         grad_biases,
         grad_ffn_bias,

time: 1950 us -> 1920 us (0.985)
  matrix products: 544 us -> 433 us
  waiting for transfers between devices: 933 us -> 1020 us
    all_to_all x2, waiting for transfers between devices: 10.7 us -> 145 us  [micro_step(): lax.all_to_all(grad_key_heads.astype(jnp.bfloat16), SEQ, split_axis=0, co...]
    dot_general x80 -> x40, matrix products: 205 us -> 102 us  [inner_rows(): lax.dot_general(operand, factor, (((0,), (0,)), ((), ())), preferred_elem...]
    all_gather x4 -> x1, waiting for transfers between devices: 67.6 us -> 0.01 us  [body(): all_kv = lax.all_gather(local_kv, SEQ, axis=0, tiled=True)]
    all_gather x2, waiting for transfers between devices: 140 us -> 200 us  [fetch_split(): mine = lax.all_gather(part, 'fsdp', axis=gather_axis, tiled=True)]
    all_gather x4 -> x2, waiting for transfers between devices: 166 us -> 121 us  [fetch_split(): own = lax.all_gather(part, 'fsdp', axis=gather_axis, tiled=True)]
    psum x1, waiting for transfers between devices: 0.01 us -> 26.3 us  [reduce_small(): summed = lax.psum(flat, SEQ)]
    ppermute x16 -> x10, waiting for transfers between devices: 438 us -> 415 us  [swap_y(): return lax.ppermute(tensor, 'y', SWAP)]
    reduce_scatter x6 -> x4, waiting for transfers between devices: 80.4 us -> 61.4 us  [reduce_split(): lax.psum_scatter(total, 'fsdp', scatter_dimension=scatter_axis, tiled=True)]
  transfers between devices with their start and end apart: 82 -> 56, of which waited for: 32 -> 23; matrix products, arithmetic and copies ran while one was open for 36% -> 30% of each run, Pallas kernels for 0% -> 0%
where the time goes in v4:
time: 1920 us; the launch traced here: 1910 us
  waiting for transfers between devices  1020 us (53%)
  matrix products  433 us (23%)
  other arithmetic  165 us (9%)
  local copies, waits for them, and re-layouts  160 us (8%)
  starting transfers between devices  82.1 us (4%)
  blocking collectives  30.8 us (2%)
  between operations  20.2 us (1%)
    ppermute x10, waiting for transfers between devices, swap_y(): return lax.ppermute(tensor, 'y', SWAP)  415 us
    all_gather x2, waiting for transfers between devices, fetch_split(): mine = lax.all_gather(part, 'fsdp', axis=gather_axis, tiled=True)  200 us
    dot_general x64, matrix products, outer_cols(): lax.dot_general(operand, factor, (((1,), (1,)), ((), ())), preferred_elem...  192 us
    all_to_all x2, waiting for transfers between devices, micro_step(): lax.all_to_all(grad_key_heads.astype(jnp.bfloat16), SEQ, split_axis=0, co...  145 us
    all_gather x2, waiting for transfers between devices, fetch_split(): own = lax.all_gather(part, 'fsdp', axis=gather_axis, tiled=True)  121 us
    dot_general x64, matrix products, matmul(): return jnp.dot(operand, factor, preferred_element_type=jnp.float32)  114 us
    dot_general x40, matrix products, inner_rows(): lax.dot_general(operand, factor, (((0,), (0,)), ((), ())), preferred_elem...  102 us
    reduce_scatter x4, waiting for transfers between devices, reduce_split(): lax.psum_scatter(total, 'fsdp', scatter_dimension=scatter_axis, tiled=True)  61.4 us
  transfers between devices with their start and end apart: 56, of which 23 were waited for; matrix products, arithmetic and copies ran while one was open for 30% of the time, Pallas kernels for 0%

profile of v4, /device:TPU:0, one launch (start us, length us, event | category | flops | bytes accessed | tf_op | source)
XLA Modules:
  0.0 1906.6 jit_solution(491706760823347476)
XLA Ops:
  15.7 106.1 %all-gather.7.cloned.1.call-done = bf16[6,1536,384]{2,1,0:T(8,128)(2,1)} async-done(((bf16[6,192,384]{2,1,0:T(8,128)(2,1)}), bf16[6,1536,384]{2,1,0:T(8,128)(2,1)}) %all-gather.7.cloned.1.call-update) | async-done | bytes 7077904 | tf_op jit(solution)/shard_map/all_gather | solution.py:192
  123.4 30.8 %all-gather = bf16[8,192,27]{1,2,0:T(8,128)(2,1)S(1)} all-gather(bf16[1,192,27]{1,2,0:T(8,128)(2,1)S(1)} %maximum_bitcast_fusion), channel_id=1, replica_groups=mesh['y'=2,'core'=2,'fsdp'=8] {'fsdp'}, dimensions={0}, use_global_device_ids=true | all-gather | bytes 93312 | tf_op jit(solution)/shard_map/all_gather | solution.py:217
  159.6 15.2 all-gather.9.cloned.1.call-done
  180.2 145.5 %collective-permute-done.3 = bf16[2,1536,384]{2,1,0:T(8,128)(2,1)} collective-permute-done((bf16[2,1536,384]{2,1,0:T(8,128)(2,1)}, bf16[2,1536,384]{2,1,0:T(8,128)(2,1)}, u32[]{:S(2)}, u32[]{:S(2)}) %collective-permute-start.3) | collective-permute-done | bytes 2359328 | tf_op jit(solution)/shard_map/ppermute | solution.py:153
  357.7 8.9 all-gather.13.cloned.1.call-done
  366.6 191.3 %all-gather.15.cloned.1.call-done = bf16[8960,768]{1,0:T(8,128)(2,1)} async-done(((bf16[1120,768]{1,0:T(8,128)(2,1)}), bf16[8960,768]{1,0:T(8,128)(2,1)}) %all-gather.15.cloned.1.call-update) | async-done | bytes 13762576 | tf_op jit(solution)/shard_map/all_gather | solution.py:188
  558.0 10.9 fusion.534
  680.7 9.1 all-to-all-done.7
  766.5 9.0 convert_reduce_fusion.1
  775.5 9.8 fusion.167
  785.3 10.7 multiply_reduce_fusion.17
  818.2 9.2 fusion.531
  827.4 9.3 convert_reduce_fusion
  837.9 10.0 fusion.164
  847.9 11.1 multiply_reduce_fusion.15
  932.9 8.9 copy.378
  975.6 8.1 fusion.477
  1007.7 9.9 all-to-all-done.8
  1054.6 140.1 %all-to-all-done.14 = bf16[4,96,384]{2,1,0:T(8,128)(2,1)S(1)} async-done(((bf16[4,96,384]{2,1,0:T(8,128)(2,1)}), bf16[4,96,384]{2,1,0:T(8,128)(2,1)S(1)}, u32[]{:S(2)}, u32[]{:S(2)}) %all-to-all-start.14) | async-done | bytes 294944 | tf_op jit(solution)/shard_map/all_to_all | solution.py:311
  1253.6 25.0 %collective-permute-done.15 = bf16[2,1536,384]{2,1,0:T(8,128)(2,1)} collective-permute-done((bf16[2,1536,384]{2,1,0:T(8,128)(2,1)}, bf16[2,1536,384]{2,1,0:T(8,128)(2,1)}, u32[]{:S(2)}, u32[]{:S(2)}) %collective-permute-start.15) | collective-permute-done | bytes 2359328 | tf_op jit(solution)/shard_map/ppermute | solution.py:153
  1297.3 13.0 add_convert_fusion.3
  1332.6 8.6 add_convert_fusion.5
  1367.0 10.5 copy.343
  1387.7 102.9 %collective-permute-done.20 = bf16[1536,2240]{0,1:T(8,128)(2,1)} collective-permute-done((bf16[1536,2240]{0,1:T(8,128)(2,1)}, bf16[1536,2240]{0,1:T(8,128)(2,1)}, u32[]{:S(2)}, u32[]{:S(2)}) %collective-permute-start.20) | collective-permute-done | bytes 6881312 | tf_op jit(solution)/shard_map/ppermute | solution.py:153
  1490.6 9.7 copy.344
  1500.3 13.0 add_convert_fusion
  1581.3 111.8 %collective-permute-done.10 = bf16[6,1536,384]{2,1,0:T(8,128)(2,1)} collective-permute-done((bf16[6,1536,384]{2,1,0:T(8,128)(2,1)}, bf16[6,1536,384]{2,1,0:T(8,128)(2,1)}, u32[]{:S(2)}, u32[]{:S(2)}) %collective-permute-start.10) | collective-permute-done | bytes 7077920 | tf_op jit(solution)/shard_map/ppermute | solution.py:153
  1693.2 13.1 add_convert_fusion.1
  1741.5 11.5 collective-permute-done.26
  1760.3 11.2 collective-permute-done.21
  1777.0 61.4 %reduce-scatter.11.cloned.1.call-done = bf16[6,192,384]{2,1,0:T(8,128)(2,1)} async-done(((bf16[6,1536,384]{2,1,0:T(8,128)(2,1)}), bf16[6,192,384]{2,1,0:T(8,128)(2,1)}) %reduce-scatter.11.cloned.1.call-update) | async-done | bytes 884752 | tf_op jit(solution)/shard_map/reduce_scatter | solution.py:205
  1847.9 26.3 %all-reduce.20.cloned.1.call-done = f32[23616]{0:T(1024)} async-done(((f32[23616]{0:T(1024)}), f32[23616]{0:T(1024)}) %all-reduce.20.cloned.1.call-update) | async-done | bytes 94480 | tf_op jit(solution)/shard_map/psum | solution.py:232
  (1345 shorter events, 714.6 us)
Async XLA Ops:
  7.2 114.6 %all-gather.7.cloned.1.call-start = ((), (), s32[]{:S(2)}) async-start(), calls=%async_computation.22 | async-start | bytes 7962624 | tf_op jit(solution)/shard_map/all_gather | solution.py:192
  9.6 165.2 %all-gather.9.cloned.1.call-start = ((), (), s32[]{:S(2)}) async-start(), calls=%async_computation.23 | async-start | bytes 2654208 | tf_op jit(solution)/shard_map/all_gather | solution.py:192
  11.4 355.2 %all-gather.13.cloned.1.call-start = ((), (), s32[]{:S(2)}) async-start(), calls=%async_computation.25 | async-start | bytes 15482880 | tf_op jit(solution)/shard_map/all_gather | solution.py:188
  12.8 545.2 %all-gather.15.cloned.1.call-start = ((), (), s32[]{:S(2)}) async-start(), calls=%async_computation.26 | async-start | bytes 15482880 | tf_op jit(solution)/shard_map/all_gather | solution.py:188
  121.8 208.2 %collective-permute-start = (bf16[6,1536,384]{2,1,0:T(8,128)(2,1)}, bf16[6,1536,384]{2,1,0:T(8,128)(2,1)}, u32[]{:S(2)}, u32[]{:S(2)}) collective-permute-start(bf16[6,1536,384]{2,1,0:T(8,128)(2,1)} %all-gather.7.cloned.1.call-done), channel_id=1, source_target_pairs={{0,16},{16,0},{1,17},{17,1},{2,18},{18,2},{3,19},{19,3},{4,20},{20... | collective-permute-start | bytes 21233672 | tf_op jit(solution)/shard_map/ppermute | solution.py:153
  174.8 150.9 %collective-permute-start.3 = (bf16[2,1536,384]{2,1,0:T(8,128)(2,1)}, bf16[2,1536,384]{2,1,0:T(8,128)(2,1)}, u32[]{:S(2)}, u32[]{:S(2)}) collective-permute-start(bf16[2,1536,384]{2,1,0:T(8,128)(2,1)} %all-gather.9.cloned.1.call-done), channel_id=1, source_target_pairs={{0,16},{16,0},{1,17},{17,1},{2,18},{18,2},{3,19},{19,3},{4,20},{20... | collective-permute-start | bytes 7077896 | tf_op jit(solution)/shard_map/ppermute | solution.py:153
  177.7 173.2 %collective-permute-start.2 = (bf16[6,1536,384]{2,1,0:T(8,128)(2,1)}, bf16[6,1536,384]{2,1,0:T(8,128)(2,1)S(1)}, u32[]{:S(2)}, u32[]{:S(2)}) collective-permute-start(bf16[6,1536,384]{2,1,0:T(8,128)(2,1)} %all-gather.7.cloned.1.call-done), channel_id=1, source_target_pairs={{0,8},{8,0},{1,9},{9,1},{2,10},{10,2},{3,11},{11,3},{4,12},{12,4},... | collective-permute-start | bytes 21233672 | tf_op jit(solution)/shard_map/ppermute | solution.py:135
  179.7 511.8 %collective-permute-start.5 = (bf16[2,1536,384]{2,1,0:T(8,128)(2,1)}, bf16[2,1536,384]{2,1,0:T(8,128)(2,1)}, u32[]{:S(2)}, u32[]{:S(2)}) collective-permute-start(bf16[2,1536,384]{2,1,0:T(8,128)(2,1)} %all-gather.9.cloned.1.call-done), channel_id=1, source_target_pairs={{0,8},{8,0},{1,9},{9,1},{2,10},{10,2},{3,11},{11,3},{4,12},{12,4},... | collective-permute-start | bytes 7077896 | tf_op jit(solution)/shard_map/ppermute | solution.py:135
  325.7 364.1 %collective-permute-start.4 = (bf16[2,1536,384]{2,1,0:T(8,128)(2,1)}, bf16[2,1536,384]{2,1,0:T(8,128)(2,1)}, u32[]{:S(2)}, u32[]{:S(2)}) collective-permute-start(bf16[2,1536,384]{2,1,0:T(8,128)(2,1)} %collective-permute-done.3), channel_id=1, source_target_pairs={{0,8},{8,0},{1,9},{9,1},{2,10},{10,2},{3,11},{11,3},{4,12},{12,4},... | collective-permute-start | bytes 7077896 | tf_op jit(solution)/shard_map/ppermute | solution.py:135
  330.1 238.8 %collective-permute-start.1 = (bf16[6,1536,384]{2,1,0:T(8,128)(2,1)}, bf16[6,1536,384]{2,1,0:T(8,128)(2,1)}, u32[]{:S(2)}, u32[]{:S(2)}) collective-permute-start(bf16[6,1536,384]{2,1,0:T(8,128)(2,1)} %collective-permute-done), channel_id=1, source_target_pairs={{0,8},{8,0},{1,9},{9,1},{2,10},{10,2},{3,11},{11,3},{4,12},{12,4},... | collective-permute-start | bytes 21233672 | tf_op jit(solution)/shard_map/ppermute | solution.py:135
  366.6 379.6 %collective-permute-start.6 = (bf16[1536,4480]{1,0:T(8,128)(2,1)}, bf16[1536,4480]{1,0:T(8,128)(2,1)}, u32[]{:S(2)}, u32[]{:S(2)}) collective-permute-start(bf16[1536,4480]{1,0:T(8,128)(2,1)} %all-gather.13.cloned.1.call-done), channel_id=1, source_target_pairs={{0,8},{8,0},{1,9},{9,1},{2,10},{10,2},{3,11},{11,3},{4,12},{12,4},... | collective-permute-start | bytes 41287688 | tf_op jit(solution)/shard_map/ppermute | solution.py:135
  557.9 208.5 %collective-permute-start.7 = (bf16[8960,768]{1,0:T(8,128)(2,1)}, bf16[8960,768]{1,0:T(8,128)(2,1)}, u32[]{:S(2)}, u32[]{:S(2)}) collective-permute-start(bf16[8960,768]{1,0:T(8,128)(2,1)} %all-gather.15.cloned.1.call-done), channel_id=1, source_target_pairs={{0,8},{8,0},{1,9},{9,1},{2,10},{10,2},{3,11},{11,3},{4,12},{12,4},... | collective-permute-start | bytes 41287688 | tf_op jit(solution)/shard_map/ppermute | solution.py:135
  639.8 79.6 %all-gather.11.cloned.1.call-start = ((), (), s32[]{:S(2)}) async-start(), calls=%async_computation.24 | async-start | bytes 7864320 | tf_op jit(solution)/shard_map/all_gather | solution.py:412
  927.3 450.2 %reduce-scatter.19.cloned.1.call-start = ((), (), s32[]{:S(2)}) async-start(), calls=%async_computation.32 | async-start | bytes 7864320
  941.8 91.9 %collective-permute-start.24 = (bf16[8960,384]{1,0:T(8,128)(2,1)}, bf16[8960,384]{1,0:T(8,128)(2,1)}, u32[]{:S(2)}, u32[]{:S(2)}) collective-permute-start(bf16[8960,384]{1,0:T(8,128)(2,1)} %convolution_convert_fusion), channel_id=1, source_target_pairs={{0,8},{8,0},{1,9},{9,1},{2,10},{10,2},{3,11},{11,3},{4,12},{12,4},... | collective-permute-start | bytes 20643848 | tf_op jit(solution)/shard_map/ppermute | solution.py:135
  953.7 265.9 %collective-permute-start.14 = (bf16[2,1536,384]{2,1,0:T(8,128)(2,1)}, bf16[2,1536,384]{2,1,0:T(8,128)(2,1)}, u32[]{:S(2)}, u32[]{:S(2)}) collective-permute-start(bf16[2,1536,384]{2,1,0:T(8,128)(2,1)} %pad_maximum_fusion.3), channel_id=1, source_target_pairs={{0,8},{8,0},{1,9},{9,1},{2,10},{10,2},{3,11},{11,3},{4,12},{12,4},... | collective-permute-start | bytes 7077896 | tf_op jit(solution)/shard_map/ppermute | solution.py:135
  957.2 296.0 %collective-permute-start.13 = (bf16[2,1536,384]{2,1,0:T(8,128)(2,1)}, bf16[2,1536,384]{2,1,0:T(8,128)(2,1)}, u32[]{:S(2)}, u32[]{:S(2)}) collective-permute-start(bf16[2,1536,384]{2,1,0:T(8,128)(2,1)} %pad_maximum_fusion.2), channel_id=1, source_target_pairs={{0,8},{8,0},{1,9},{9,1},{2,10},{10,2},{3,11},{11,3},{4,12},{12,4},... | collective-permute-start | bytes 7077896 | tf_op jit(solution)/shard_map/ppermute | solution.py:135
  996.3 336.2 %collective-permute-start.19 = (bf16[1536,2240]{0,1:T(8,128)(2,1)}, bf16[1536,2240]{0,1:T(8,128)(2,1)}, u32[]{:S(2)}, u32[]{:S(2)}) collective-permute-start(bf16[1536,2240]{0,1:T(8,128)(2,1)} %convolution_convert_fusion.2), channel_id=1, source_target_pairs={{0,8},{8,0},{1,9},{9,1},{2,10},{10,2},{3,11},{11,3},{4,12},{12,4},... | collective-permute-start | bytes 20643848 | tf_op jit(solution)/shard_map/ppermute | solution.py:135
  996.7 300.5 %collective-permute-start.23 = (bf16[8960,384]{1,0:T(8,128)(2,1)}, bf16[8960,384]{1,0:T(8,128)(2,1)}, u32[]{:S(2)}, u32[]{:S(2)}) collective-permute-start(bf16[8960,384]{1,0:T(8,128)(2,1)} %convolution_convert_fusion.1), channel_id=1, source_target_pairs={{0,8},{8,0},{1,9},{9,1},{2,10},{10,2},{3,11},{11,3},{4,12},{12,4},... | collective-permute-start | bytes 20643848 | tf_op jit(solution)/shard_map/ppermute | solution.py:135
  1040.7 256.5 %collective-permute-start.25 = (bf16[8960,384]{1,0:T(8,128)(2,1)}, bf16[8960,384]{1,0:T(8,128)(2,1)}, u32[]{:S(2)}, u32[]{:S(2)}) collective-permute-start(bf16[8960,384]{1,0:T(8,128)(2,1)} %add_convert_fusion.4), channel_id=1, source_target_pairs={{0,16},{16,0},{1,17},{17,1},{2,18},{18,2},{3,19},{19,3},{4,20},{20... | collective-permute-start | bytes 20643848 | tf_op jit(solution)/shard_map/ppermute | solution.py:153
  1049.2 145.4 %all-to-all-start.14 = ((bf16[4,96,384]{2,1,0:T(8,128)(2,1)}), bf16[4,96,384]{2,1,0:T(8,128)(2,1)S(1)}, u32[]{:S(2)}, u32[]{:S(2)}) async-start(bf16[4,96,384]{2,1,0:T(8,128)(2,1)} %copy.376), calls=%async_computation.14 | async-start | bytes 589824 | tf_op jit(solution)/shard_map/all_to_all | solution.py:311
  1237.7 470.6 %reduce-scatter.13.cloned.1.call-start = ((), (), s32[]{:S(2)}) async-start(), calls=%async_computation.29 | async-start | bytes 2654208 | tf_op jit(solution)/shard_map/reduce_scatter | solution.py:205
  1253.2 113.8 %collective-permute-start.18 = (bf16[1536,2240]{0,1:T(8,128)(2,1)}, bf16[1536,2240]{0,1:T(8,128)(2,1)}, u32[]{:S(2)}, u32[]{:S(2)}) collective-permute-start(bf16[1536,2240]{0,1:T(8,128)(2,1)} %convolution_convert_fusion.3), channel_id=1, source_target_pairs={{0,8},{8,0},{1,9},{9,1},{2,10},{10,2},{3,11},{11,3},{4,12},{12,4},... | collective-permute-start | bytes 20643848 | tf_op jit(solution)/shard_map/ppermute | solution.py:135
  1283.3 447.4 %reduce-scatter.17.cloned.1.call-start = ((), (), s32[]{:S(2)}) async-start(), calls=%async_computation.31 | async-start | bytes 7741440 | tf_op jit(solution)/shard_map/reduce_scatter | solution.py:205
  1310.3 426.6 %reduce-scatter.15.cloned.1.call-start = ((), (), s32[]{:S(2)}) async-start(), calls=%async_computation.30 | async-start | bytes 7962624 | tf_op jit(solution)/shard_map/reduce_scatter | solution.py:205
  1341.2 149.4 %collective-permute-start.20 = (bf16[1536,2240]{0,1:T(8,128)(2,1)}, bf16[1536,2240]{0,1:T(8,128)(2,1)}, u32[]{:S(2)}, u32[]{:S(2)}) collective-permute-start(bf16[1536,2240]{0,1:T(8,128)(2,1)} %add_convert_fusion.5), channel_id=1, source_target_pairs={{0,16},{16,0},{1,17},{17,1},{2,18},{18,2},{3,19},{19,3},{4,20},{20... | collective-permute-start | bytes 20643848 | tf_op jit(solution)/shard_map/ppermute | solution.py:153
  1387.7 142.6 %collective-permute-start.9 = (bf16[6,1536,384]{2,1,0:T(8,128)(2,1)}, bf16[6,1536,384]{2,1,0:T(8,128)(2,1)}, u32[]{:S(2)}, u32[]{:S(2)}) collective-permute-start(bf16[6,1536,384]{2,1,0:T(8,128)(2,1)} %fusion.54), channel_id=1, source_target_pairs={{0,8},{8,0},{1,9},{9,1},{2,10},{10,2},{3,11},{11,3},{4,12},{12,4},... | collective-permute-start | bytes 21233672 | tf_op jit(solution)/shard_map/ppermute | solution.py:135
  1513.3 245.9 %reduce-scatter.21.cloned.1.call-start = ((), (), s32[]{:S(2)}) async-start(), calls=%async_computation.33 | async-start | bytes 884736
  1538.0 155.1 %collective-permute-start.10 = (bf16[6,1536,384]{2,1,0:T(8,128)(2,1)}, bf16[6,1536,384]{2,1,0:T(8,128)(2,1)}, u32[]{:S(2)}, u32[]{:S(2)}) collective-permute-start(bf16[6,1536,384]{2,1,0:T(8,128)(2,1)} %add_convert_fusion.2), channel_id=1, source_target_pairs={{0,16},{16,0},{1,17},{17,1},{2,18},{18,2},{3,19},{19,3},{4,20},{20... | collective-permute-start | bytes 21233672 | tf_op jit(solution)/shard_map/ppermute | solution.py:153
  1577.2 261.2 %reduce-scatter.11.cloned.1.call-start = ((), (), s32[]{:S(2)}) async-start(), calls=%async_computation.28 | async-start | bytes 7962624 | tf_op jit(solution)/shard_map/reduce_scatter | solution.py:205
  1706.4 167.9 %all-reduce.20.cloned.1.call-start = ((), (), s32[]{:S(2)}) async-start(), calls=%async_computation.27 | async-start | bytes 196608 | tf_op jit(solution)/shard_map/psum | solution.py:232
  1756.1 127.7 %collective-permute-start.27 = (bf16[1120,768]{1,0:T(8,128)(2,1)}, bf16[1120,768]{1,0:T(8,128)(2,1)}, u32[]{:S(2)}, u32[]{:S(2)}) collective-permute-start(bf16[1120,768]{1,0:T(8,128)(2,1)} %fusion.100), channel_id=1, source_target_pairs={{0,8},{8,0},{1,9},{9,1},{2,10},{10,2},{3,11},{11,3},{4,12},{12,4},... | collective-permute-start | bytes 5160968 | tf_op jit(solution)/shard_map/ppermute | solution.py:135
  (377 other events, 9786.4 us)
Sparse Core Ops, SparseCore 0:
  10.8 110.9 all-gather.6
  124.6 50.1 all-gather.8
  177.6 188.9 all-gather.12
  369.2 188.6 all-gather.14
  642.4 55.3 all-gather.10
  942.0 59.3 reduce-scatter.18
  1283.4 68.5 reduce-scatter.12
  1355.7 126.0 reduce-scatter.16
  1513.4 127.3 reduce-scatter.14
  1644.0 62.4 reduce-scatter.20
  1710.1 128.2 reduce-scatter.10
  1844.0 30.2 all-reduce.19

commit v5 on v4

--- a/solution.py
+++ b/solution.py
@@ -176,8 +176,9 @@
         pieces = [outer_cols(g, part) for g, part in zip(self.quarters(grad), self.parts)]
         return (pieces[0] + pieces[1]) + (pieces[2] + pieces[3])
 
-    def grad(self, rows, grad):
-        return tuple(inner_rows(rows, g) for g in self.quarters(grad))
+    def grad(self, rows, grad, quarters=True):
+        pieces = self.quarters(grad) if quarters else halves(grad, self.spot[1])
+        return tuple(inner_rows(rows, g) for g in pieces)
 
 
 def fetch_split(local, gather_axis, spot, quarters=True):
@@ -206,6 +207,16 @@
     owned_y = swap_y(owned)
     mine = join(owned, owned_y, y)
     return join(mine, swap_core(mine), core).astype(jnp.float32)
+
+
+def reduce_half(parts, scatter_axis, spot):
+    y, core = spot
+    mine, other = parts
+    received = swap_core(other.astype(jnp.bfloat16)).astype(jnp.float32)
+    chip = (mine + received).astype(jnp.bfloat16)
+    owned = lax.psum_scatter(chip, "fsdp", scatter_dimension=scatter_axis, tiled=True)
+    summed = owned.astype(jnp.float32) + swap_y(owned).astype(jnp.float32)
+    return join(summed, swap_core(summed), core)
 
 
 def fetch_small(modulation, gains, biases, ffn_bias):
@@ -443,10 +454,12 @@
         for found in pair_lists
     ]
     split_grads = [
-        split_weight.grad(rows, grad)
-        for split_weight, (rows, grad) in zip(
-            (in_split[0], in_split[1], in_split[2], out_split[0], in_split[3], out_split[1], weights[9], weights[10]),
-            pairs,
+        split_weight.grad(rows, grad, quarters=index < 6)
+        for index, (split_weight, (rows, grad)) in enumerate(
+            zip(
+                (in_split[0], in_split[1], in_split[2], out_split[0], in_split[3], out_split[1], weights[9], weights[10]),
+                pairs,
+            )
         )
     ]
     grad_kv = jnp.concatenate(key_grads + value_grads, axis=1).astype(jnp.bfloat16)
@@ -472,8 +485,8 @@
     attn_out_grads = tuple(jnp.stack([split_grads[3][q], split_grads[5][q]]) for q in range(4))
     attn_in_final = reduce_split(attn_in_grads, 1, spot)
     attn_out_final = reduce_split(attn_out_grads, 1, spot)
-    ffn_in_final = reduce_split(split_grads[6], 0, spot)
-    ffn_out_final = reduce_split(split_grads[7], 0, spot)
+    ffn_in_final = reduce_half(split_grads[6], 0, spot)
+    ffn_out_final = reduce_half(split_grads[7], 0, spot)
     grad_time = jnp.stack(clock_list)
     grad_mod, grad_gains, grad_biases, grad_ffn_bias, grad_time = reduce_small(
         grad_mod, grad_gains, grad_biases, grad_ffn_bias_local, grad_time, width, length

time: 1920 us -> 1890 us (0.984)
  waiting for transfers between devices: 1020 us -> 1080 us
  local copies, waits for them, and re-layouts: 160 us -> 120 us
  other arithmetic: 165 us -> 138 us
  matrix products: 433 us -> 408 us
    reduce_scatter x0 -> x2, waiting for transfers between devices: none -> 225 us  [reduce_half(): lax.psum_scatter(chip, 'fsdp', scatter_dimension=scatter_axis, tiled=True)]
    all_to_all x2, waiting for transfers between devices: 145 us -> 42 us  [micro_step(): lax.all_to_all(grad_key_heads.astype(jnp.bfloat16), SEQ, split_axis=0, co...]
    ppermute x10 -> x8, waiting for transfers between devices: 415 us -> 314 us  [swap_y(): return lax.ppermute(tensor, 'y', SWAP)]
    reduce_scatter x4 -> x2, waiting for transfers between devices: 61.4 us -> 91.6 us  [reduce_split(): lax.psum_scatter(total, 'fsdp', scatter_dimension=scatter_axis, tiled=True)]
    convert_element_type x4 -> x2, other arithmetic: 43.8 us -> 13.8 us  [reduce_split(): total = (chip_own + swap_y(chip_y).astype(jnp.float32)).astype(jnp.bfloat16)]
    dot_general x40 -> x36, matrix products: 102 us -> 79.6 us  [inner_rows(): lax.dot_general(operand, factor, (((0,), (0,)), ((), ())), preferred_elem...]
    unnamed x14, waiting for transfers between devices: 0.2 us -> 21.8 us
    ppermute x2 -> x0, local copies, waits for them, and re-layouts: 20.1 us -> none  [the longest x1 10.5 us: swap_core(): return lax.ppermute(tensor, 'core', SWAP)]
  transfers between devices with their start and end apart: 56 -> 52, of which waited for: 23 -> 22; matrix products, arithmetic and copies ran while one was open for 30% -> 26% of each run, Pallas kernels for 0% -> 0%
where the time goes in v5:
time: 1890 us; the launch traced here: 1880 us
  waiting for transfers between devices  1080 us (57%)
  matrix products  408 us (22%)
  other arithmetic  138 us (7%)
  local copies, waits for them, and re-layouts  120 us (6%)
  starting transfers between devices  80 us (4%)
  blocking collectives  30.8 us (2%)
  between operations  20.3 us (1%)
    ppermute x8, waiting for transfers between devices, swap_y(): return lax.ppermute(tensor, 'y', SWAP)  314 us
    reduce_scatter x2, waiting for transfers between devices, reduce_half(): lax.psum_scatter(chip, 'fsdp', scatter_dimension=scatter_axis, tiled=True)  225 us
    all_gather x2, waiting for transfers between devices, fetch_split(): mine = lax.all_gather(part, 'fsdp', axis=gather_axis, tiled=True)  200 us
    dot_general x64, matrix products, outer_cols(): lax.dot_general(operand, factor, (((1,), (1,)), ((), ())), preferred_elem...  193 us
    all_gather x2, waiting for transfers between devices, fetch_split(): own = lax.all_gather(part, 'fsdp', axis=gather_axis, tiled=True)  121 us
    dot_general x64, matrix products, matmul(): return jnp.dot(operand, factor, preferred_element_type=jnp.float32)  114 us
    reduce_scatter x2, waiting for transfers between devices, reduce_split(): lax.psum_scatter(total, 'fsdp', scatter_dimension=scatter_axis, tiled=True)  91.6 us
    dot_general x36, matrix products, inner_rows(): lax.dot_general(operand, factor, (((0,), (0,)), ((), ())), preferred_elem...  79.6 us
  transfers between devices with their start and end apart: 52, of which 22 were waited for; matrix products, arithmetic and copies ran while one was open for 26% of the time, Pallas kernels for 0%

profile of v5, /device:TPU:0, one launch (start us, length us, event | category | flops | bytes accessed | tf_op | source)
XLA Modules:
  0.0 1876.6 jit_solution(14345437092412042048)
XLA Ops:
  15.7 106.1 %all-gather.7.cloned.1.call-done = bf16[6,1536,384]{2,1,0:T(8,128)(2,1)} async-done(((bf16[6,192,384]{2,1,0:T(8,128)(2,1)}), bf16[6,1536,384]{2,1,0:T(8,128)(2,1)}) %all-gather.7.cloned.1.call-update) | async-done | bytes 7077904 | tf_op jit(solution)/shard_map/all_gather | solution.py:193
  123.4 30.8 %all-gather = bf16[8,192,27]{1,2,0:T(8,128)(2,1)S(1)} all-gather(bf16[1,192,27]{1,2,0:T(8,128)(2,1)S(1)} %maximum_bitcast_fusion), channel_id=1, replica_groups=mesh['y'=2,'core'=2,'fsdp'=8] {'fsdp'}, dimensions={0}, use_global_device_ids=true | all-gather | bytes 93312 | tf_op jit(solution)/shard_map/all_gather | solution.py:228
  159.6 15.2 all-gather.9.cloned.1.call-done
  180.2 145.6 %collective-permute-done.3 = bf16[2,1536,384]{2,1,0:T(8,128)(2,1)} collective-permute-done((bf16[2,1536,384]{2,1,0:T(8,128)(2,1)}, bf16[2,1536,384]{2,1,0:T(8,128)(2,1)}, u32[]{:S(2)}, u32[]{:S(2)}) %collective-permute-start.3) | collective-permute-done | bytes 2359328 | tf_op jit(solution)/shard_map/ppermute | solution.py:153
  357.7 9.0 all-gather.13.cloned.1.call-done
  366.6 191.3 %all-gather.15.cloned.1.call-done = bf16[8960,768]{1,0:T(8,128)(2,1)} async-done(((bf16[1120,768]{1,0:T(8,128)(2,1)}), bf16[8960,768]{1,0:T(8,128)(2,1)}) %all-gather.15.cloned.1.call-update) | async-done | bytes 13762576 | tf_op jit(solution)/shard_map/all_gather | solution.py:189
  558.0 10.9 fusion.518
  680.9 8.7 all-to-all-done.7
  745.6 7.3 fusion.808
  752.9 7.2 fusion.804
  765.8 9.3 convert_reduce_fusion.1
  775.2 9.8 fusion.159
  785.0 10.7 multiply_reduce_fusion.17
  818.6 9.2 fusion.515
  827.8 9.1 convert_reduce_fusion
  838.2 10.0 fusion.156
  848.2 11.1 multiply_reduce_fusion.15
  860.9 7.4 fusion.810
  870.7 7.3 fusion.806
  898.2 7.0 convolution_convert_fusion
  911.8 8.6 copy.367
  1017.3 36.6 %all-to-all-done.14 = bf16[4,96,384]{2,1,0:T(8,128)(2,1)S(1)} async-done(((bf16[4,96,384]{2,1,0:T(8,128)(2,1)}), bf16[4,96,384]{2,1,0:T(8,128)(2,1)S(1)}, u32[]{:S(2)}, u32[]{:S(2)}) %all-to-all-start.14) | async-done | bytes 294944 | tf_op jit(solution)/shard_map/all_to_all | solution.py:322
  1129.6 10.3 add_convert_fusion.1
  1216.3 8.1 convolution_convert_fusion.1
  1230.7 138.7 %collective-permute-done.10 = bf16[6,1536,384]{2,1,0:T(8,128)(2,1)} collective-permute-done((bf16[6,1536,384]{2,1,0:T(8,128)(2,1)}, bf16[6,1536,384]{2,1,0:T(8,128)(2,1)}, u32[]{:S(2)}, u32[]{:S(2)}) %collective-permute-start.10) | collective-permute-done | bytes 7077920 | tf_op jit(solution)/shard_map/ppermute | solution.py:153
  1369.4 9.1 add_convert_fusion.2
  1379.6 11.8 add_convert_fusion
  1426.7 91.6 %reduce-scatter.11.cloned.1.call-done = bf16[6,192,384]{2,1,0:T(8,128)(2,1)} async-done(((bf16[6,1536,384]{2,1,0:T(8,128)(2,1)}), bf16[6,192,384]{2,1,0:T(8,128)(2,1)}) %reduce-scatter.11.cloned.1.call-update) | async-done | bytes 884752 | tf_op jit(solution)/shard_map/reduce_scatter | solution.py:206
  1519.7 225.1 %reduce-scatter.17.cloned.1.call-done = bf16[1120,768]{1,0:T(8,128)(2,1)} async-done(((bf16[8960,768]{1,0:T(8,128)(2,1)}), bf16[1120,768]{1,0:T(8,128)(2,1)}) %reduce-scatter.17.cloned.1.call-update) | async-done | bytes 1720336 | tf_op jit(solution)/shard_map/reduce_scatter | solution.py:217
  1756.0 28.1 %collective-permute-done.22 = bf16[1120,768]{1,0:T(8,128)(2,1)S(1)} collective-permute-done((bf16[1120,768]{1,0:T(8,128)(2,1)}, bf16[1120,768]{1,0:T(8,128)(2,1)S(1)}, u32[]{:S(2)}, u32[]{:S(2)}) %collective-permute-start.22) | collective-permute-done | bytes 1720352 | tf_op jit(solution)/shard_map/ppermute | solution.py:153
  1789.3 21.6 %reduce-scatter.21.cloned.1.call-done = f32[192,27]{1,0:T(8,128)} async-done(((f32[1536,27]{1,0:T(8,128)}), f32[192,27]{1,0:T(8,128)}) %reduce-scatter.21.cloned.1.call-update) | async-done | bytes 20752
  1817.3 27.2 %all-reduce.20.cloned.1.call-done = f32[23616]{0:T(1024)} async-done(((f32[23616]{0:T(1024)}), f32[23616]{0:T(1024)}) %all-reduce.20.cloned.1.call-update) | async-done | bytes 94480 | tf_op jit(solution)/shard_map/psum | solution.py:243
  (1326 shorter events, 616.5 us)
Async XLA Ops:
  7.2 114.6 %all-gather.7.cloned.1.call-start = ((), (), s32[]{:S(2)}) async-start(), calls=%async_computation.22 | async-start | bytes 7962624 | tf_op jit(solution)/shard_map/all_gather | solution.py:193
  9.6 165.2 %all-gather.9.cloned.1.call-start = ((), (), s32[]{:S(2)}) async-start(), calls=%async_computation.23 | async-start | bytes 2654208 | tf_op jit(solution)/shard_map/all_gather | solution.py:193
  11.4 355.2 %all-gather.13.cloned.1.call-start = ((), (), s32[]{:S(2)}) async-start(), calls=%async_computation.25 | async-start | bytes 15482880 | tf_op jit(solution)/shard_map/all_gather | solution.py:189
  12.8 545.2 %all-gather.15.cloned.1.call-start = ((), (), s32[]{:S(2)}) async-start(), calls=%async_computation.26 | async-start | bytes 15482880 | tf_op jit(solution)/shard_map/all_gather | solution.py:189
  121.8 208.2 %collective-permute-start = (bf16[6,1536,384]{2,1,0:T(8,128)(2,1)}, bf16[6,1536,384]{2,1,0:T(8,128)(2,1)}, u32[]{:S(2)}, u32[]{:S(2)}) collective-permute-start(bf16[6,1536,384]{2,1,0:T(8,128)(2,1)} %all-gather.7.cloned.1.call-done), channel_id=1, source_target_pairs={{0,16},{16,0},{1,17},{17,1},{2,18},{18,2},{3,19},{19,3},{4,20},{20... | collective-permute-start | bytes 21233672 | tf_op jit(solution)/shard_map/ppermute | solution.py:153
  174.8 150.9 %collective-permute-start.3 = (bf16[2,1536,384]{2,1,0:T(8,128)(2,1)}, bf16[2,1536,384]{2,1,0:T(8,128)(2,1)}, u32[]{:S(2)}, u32[]{:S(2)}) collective-permute-start(bf16[2,1536,384]{2,1,0:T(8,128)(2,1)} %all-gather.9.cloned.1.call-done), channel_id=1, source_target_pairs={{0,16},{16,0},{1,17},{17,1},{2,18},{18,2},{3,19},{19,3},{4,20},{20... | collective-permute-start | bytes 7077896 | tf_op jit(solution)/shard_map/ppermute | solution.py:153
  177.6 173.2 %collective-permute-start.2 = (bf16[6,1536,384]{2,1,0:T(8,128)(2,1)}, bf16[6,1536,384]{2,1,0:T(8,128)(2,1)S(1)}, u32[]{:S(2)}, u32[]{:S(2)}) collective-permute-start(bf16[6,1536,384]{2,1,0:T(8,128)(2,1)} %all-gather.7.cloned.1.call-done), channel_id=1, source_target_pairs={{0,8},{8,0},{1,9},{9,1},{2,10},{10,2},{3,11},{11,3},{4,12},{12,4},... | collective-permute-start | bytes 21233672 | tf_op jit(solution)/shard_map/ppermute | solution.py:135
  179.7 511.7 %collective-permute-start.5 = (bf16[2,1536,384]{2,1,0:T(8,128)(2,1)}, bf16[2,1536,384]{2,1,0:T(8,128)(2,1)}, u32[]{:S(2)}, u32[]{:S(2)}) collective-permute-start(bf16[2,1536,384]{2,1,0:T(8,128)(2,1)} %all-gather.9.cloned.1.call-done), channel_id=1, source_target_pairs={{0,8},{8,0},{1,9},{9,1},{2,10},{10,2},{3,11},{11,3},{4,12},{12,4},... | collective-permute-start | bytes 7077896 | tf_op jit(solution)/shard_map/ppermute | solution.py:135
  325.7 364.0 %collective-permute-start.4 = (bf16[2,1536,384]{2,1,0:T(8,128)(2,1)}, bf16[2,1536,384]{2,1,0:T(8,128)(2,1)}, u32[]{:S(2)}, u32[]{:S(2)}) collective-permute-start(bf16[2,1536,384]{2,1,0:T(8,128)(2,1)} %collective-permute-done.3), channel_id=1, source_target_pairs={{0,8},{8,0},{1,9},{9,1},{2,10},{10,2},{3,11},{11,3},{4,12},{12,4},... | collective-permute-start | bytes 7077896 | tf_op jit(solution)/shard_map/ppermute | solution.py:135
  330.1 238.8 %collective-permute-start.1 = (bf16[6,1536,384]{2,1,0:T(8,128)(2,1)}, bf16[6,1536,384]{2,1,0:T(8,128)(2,1)}, u32[]{:S(2)}, u32[]{:S(2)}) collective-permute-start(bf16[6,1536,384]{2,1,0:T(8,128)(2,1)} %collective-permute-done), channel_id=1, source_target_pairs={{0,8},{8,0},{1,9},{9,1},{2,10},{10,2},{3,11},{11,3},{4,12},{12,4},... | collective-permute-start | bytes 21233672 | tf_op jit(solution)/shard_map/ppermute | solution.py:135
  366.6 378.9 %collective-permute-start.6 = (bf16[1536,4480]{1,0:T(8,128)(2,1)}, bf16[1536,4480]{1,0:T(8,128)(2,1)}, u32[]{:S(2)}, u32[]{:S(2)}) collective-permute-start(bf16[1536,4480]{1,0:T(8,128)(2,1)} %all-gather.13.cloned.1.call-done), channel_id=1, source_target_pairs={{0,8},{8,0},{1,9},{9,1},{2,10},{10,2},{3,11},{11,3},{4,12},{12,4},... | collective-permute-start | bytes 41287688 | tf_op jit(solution)/shard_map/ppermute | solution.py:135
  557.9 207.9 %collective-permute-start.7 = (bf16[8960,768]{1,0:T(8,128)(2,1)}, bf16[8960,768]{1,0:T(8,128)(2,1)}, u32[]{:S(2)}, u32[]{:S(2)}) collective-permute-start(bf16[8960,768]{1,0:T(8,128)(2,1)} %all-gather.15.cloned.1.call-done), channel_id=1, source_target_pairs={{0,8},{8,0},{1,9},{9,1},{2,10},{10,2},{3,11},{11,3},{4,12},{12,4},... | collective-permute-start | bytes 41287688 | tf_op jit(solution)/shard_map/ppermute | solution.py:135
  639.6 79.7 %all-gather.11.cloned.1.call-start = ((), (), s32[]{:S(2)}) async-start(), calls=%async_computation.24 | async-start | bytes 7864320 | tf_op jit(solution)/shard_map/all_gather | solution.py:423
  679.8 505.5 %reduce-scatter.19.cloned.1.call-start = ((), (), s32[]{:S(2)}) async-start(), calls=%async_computation.32 | async-start | bytes 7864320
  921.0 208.6 %collective-permute-start.18 = (bf16[1536,4480]{1,0:T(8,128)(2,1)}, bf16[1536,4480]{1,0:T(8,128)(2,1)}, u32[]{:S(2)}, u32[]{:S(2)}) collective-permute-start(bf16[1536,4480]{1,0:T(8,128)(2,1)} %convolution_convert_fusion), channel_id=1, source_target_pairs={{0,8},{8,0},{1,9},{9,1},{2,10},{10,2},{3,11},{11,3},{4,12},{12,4},... | collective-permute-start | bytes 41287688 | tf_op jit(solution)/shard_map/ppermute | solution.py:135
  948.0 43.9 %collective-permute-start.14 = (bf16[2,1536,384]{2,1,0:T(8,128)(2,1)}, bf16[2,1536,384]{2,1,0:T(8,128)(2,1)}, u32[]{:S(2)}, u32[]{:S(2)}) collective-permute-start(bf16[2,1536,384]{2,1,0:T(8,128)(2,1)} %pad_maximum_fusion.3), channel_id=1, source_target_pairs={{0,8},{8,0},{1,9},{9,1},{2,10},{10,2},{3,11},{11,3},{4,12},{12,4},... | collective-permute-start | bytes 7077896 | tf_op jit(solution)/shard_map/ppermute | solution.py:135
  964.8 121.5 %collective-permute-start.13 = (bf16[2,1536,384]{2,1,0:T(8,128)(2,1)}, bf16[2,1536,384]{2,1,0:T(8,128)(2,1)}, u32[]{:S(2)}, u32[]{:S(2)}) collective-permute-start(bf16[2,1536,384]{2,1,0:T(8,128)(2,1)} %pad_maximum_fusion.2), channel_id=1, source_target_pairs={{0,8},{8,0},{1,9},{9,1},{2,10},{10,2},{3,11},{11,3},{4,12},{12,4},... | collective-permute-start | bytes 7077896 | tf_op jit(solution)/shard_map/ppermute | solution.py:135
  996.8 89.5 %collective-permute-start.15 = (bf16[2,1536,384]{2,1,0:T(8,128)(2,1)}, bf16[2,1536,384]{2,1,0:T(8,128)(2,1)}, u32[]{:S(2)}, u32[]{:S(2)}) collective-permute-start(bf16[2,1536,384]{2,1,0:T(8,128)(2,1)} %fusion.6), channel_id=1, source_target_pairs={{0,16},{16,0},{1,17},{17,1},{2,18},{18,2},{3,19},{19,3},{4,20},{20... | collective-permute-start | bytes 7077896 | tf_op jit(solution)/shard_map/ppermute | solution.py:153
  1012.7 41.1 %all-to-all-start.14 = ((bf16[4,96,384]{2,1,0:T(8,128)(2,1)}), bf16[4,96,384]{2,1,0:T(8,128)(2,1)S(1)}, u32[]{:S(2)}, u32[]{:S(2)}) async-start(bf16[4,96,384]{2,1,0:T(8,128)(2,1)} %copy.365), calls=%async_computation.14 | async-start | bytes 589824 | tf_op jit(solution)/shard_map/all_to_all | solution.py:322
  1078.2 315.3 %reduce-scatter.13.cloned.1.call-start = ((), (), s32[]{:S(2)}) async-start(), calls=%async_computation.29 | async-start | bytes 2654208 | tf_op jit(solution)/shard_map/reduce_scatter | solution.py:206
  1094.7 317.1 %reduce-scatter.15.cloned.1.call-start = ((), (), s32[]{:S(2)}) async-start(), calls=%async_computation.30 | async-start | bytes 15482880 | tf_op jit(solution)/shard_map/reduce_scatter | solution.py:217
  1139.9 378.3 %reduce-scatter.11.cloned.1.call-start = ((), (), s32[]{:S(2)}) async-start(), calls=%async_computation.28 | async-start | bytes 7962624 | tf_op jit(solution)/shard_map/reduce_scatter | solution.py:206
  1214.4 155.1 %collective-permute-start.10 = (bf16[6,1536,384]{2,1,0:T(8,128)(2,1)}, bf16[6,1536,384]{2,1,0:T(8,128)(2,1)}, u32[]{:S(2)}, u32[]{:S(2)}) collective-permute-start(bf16[6,1536,384]{2,1,0:T(8,128)(2,1)} %add_convert_fusion.3), channel_id=1, source_target_pairs={{0,16},{16,0},{1,17},{17,1},{2,18},{18,2},{3,19},{19,3},{4,20},{20... | collective-permute-start | bytes 21233672 | tf_op jit(solution)/shard_map/ppermute | solution.py:153
  1224.4 154.2 %collective-permute-start.21 = (bf16[8960,768]{1,0:T(8,128)(2,1)}, bf16[8960,768]{1,0:T(8,128)(2,1)}, u32[]{:S(2)}, u32[]{:S(2)}) collective-permute-start(bf16[8960,768]{1,0:T(8,128)(2,1)} %convolution_convert_fusion.1), channel_id=1, source_target_pairs={{0,8},{8,0},{1,9},{9,1},{2,10},{10,2},{3,11},{11,3},{4,12},{12,4},... | collective-permute-start | bytes 41287688 | tf_op jit(solution)/shard_map/ppermute | solution.py:135
  1378.6 366.1 %reduce-scatter.17.cloned.1.call-start = ((), (), s32[]{:S(2)}) async-start(), calls=%async_computation.31 | async-start | bytes 15482880 | tf_op jit(solution)/shard_map/reduce_scatter | solution.py:217
  1391.7 419.2 %reduce-scatter.21.cloned.1.call-start = ((), (), s32[]{:S(2)}) async-start(), calls=%async_computation.33 | async-start | bytes 884736
  1411.8 334.4 %collective-permute-start.19 = (bf16[192,4480]{1,0:T(8,128)(2,1)}, bf16[192,4480]{1,0:T(8,128)(2,1)}, u32[]{:S(2)}, u32[]{:S(2)}) collective-permute-start(bf16[192,4480]{1,0:T(8,128)(2,1)} %reduce-scatter.15.cloned.1.call-done), channel_id=1, source_target_pairs={{0,16},{16,0},{1,17},{17,1},{2,18},{18,2},{3,19},{19,3},{4,20},{20... | collective-permute-start | bytes 5160968 | tf_op jit(solution)/shard_map/ppermute | solution.py:153
  1414.4 430.1 %all-reduce.20.cloned.1.call-start = ((), (), s32[]{:S(2)}) async-start(), calls=%async_computation.27 | async-start | bytes 196608 | tf_op jit(solution)/shard_map/psum | solution.py:243
  1518.2 235.2 %collective-permute-start.11 = (bf16[6,192,384]{2,1,0:T(8,128)(2,1)}, bf16[6,192,384]{2,1,0:T(8,128)(2,1)}, u32[]{:S(2)}, u32[]{:S(2)}) collective-permute-start(bf16[6,192,384]{2,1,0:T(8,128)(2,1)} %reduce-scatter.11.cloned.1.call-done), channel_id=1, source_target_pairs={{0,16},{16,0},{1,17},{17,1},{2,18},{18,2},{3,19},{19,3},{4,20},{20... | collective-permute-start | bytes 2654216 | tf_op jit(solution)/shard_map/ppermute | solution.py:153
  1750.3 107.9 %collective-permute-start.20 = (f32[192,4480]{1,0:T(8,128)}, f32[192,4480]{1,0:T(8,128)}, u32[]{:S(2)}, u32[]{:S(2)}) collective-permute-start(f32[192,4480]{1,0:T(8,128)} %convert_add_fusion.1), channel_id=1, source_target_pairs={{0,8},{8,0},{1,9},{9,1},{2,10},{10,2},{3,11},{11,3},{4,12},{12,4},... | collective-permute-start | bytes 10321928 | tf_op jit(solution)/shard_map/ppermute | solution.py:135
  1755.5 96.2 %collective-permute-start.12 = (bf16[6,192,768]{2,1,0:T(8,128)(2,1)S(1)}, bf16[6,192,768]{2,1,0:T(8,128)(2,1)}, u32[]{:S(2)}, u32[]{:S(2)}) collective-permute-start(bf16[6,192,768]{2,1,0:T(8,128)(2,1)S(1)} %fusion.97), channel_id=1, source_target_pairs={{0,8},{8,0},{1,9},{9,1},{2,10},{10,2},{3,11},{11,3},{4,12},{12,4},... | collective-permute-start | bytes 5308424 | tf_op jit(solution)/shard_map/ppermute | solution.py:135
  1786.3 77.3 %collective-permute-start.23 = (f32[1120,768]{1,0:T(8,128)}, f32[1120,768]{1,0:T(8,128)}, u32[]{:S(2)}, u32[]{:S(2)}) collective-permute-start(f32[1120,768]{1,0:T(8,128)} %convert_add_fusion), channel_id=1, source_target_pairs={{0,8},{8,0},{1,9},{9,1},{2,10},{10,2},{3,11},{11,3},{4,12},{12,4},... | collective-permute-start | bytes 10321928 | tf_op jit(solution)/shard_map/ppermute | solution.py:135
  (372 other events, 9428.2 us)
Sparse Core Ops, SparseCore 0:
  10.8 110.9 all-gather.6
  124.6 50.1 all-gather.8
  177.6 188.9 all-gather.12
  369.2 188.6 all-gather.14
  642.3 55.3 all-gather.10
  920.5 64.3 reduce-scatter.18
  1091.2 68.2 reduce-scatter.12
  1163.1 223.0 reduce-scatter.14
  1389.9 128.2 reduce-scatter.10
  1521.6 223.0 reduce-scatter.16
  1748.6 62.3 reduce-scatter.20
  1813.7 30.7 all-reduce.19

commit v6 on v5

--- a/solution.py
+++ b/solution.py
@@ -24,12 +24,12 @@
 
 def outer_cols(operand, factor):
     return lax.dot_general(
-        operand, factor, (((1,), (1,)), ((), ())), preferred_element_type=jnp.float32
+        operand, factor, (((operand.ndim - 1,), (1,)), ((), ())), preferred_element_type=jnp.float32
     )
 
 
 def column_sums(tensor):
-    return jnp.sum(tensor.astype(jnp.float32), axis=0)
+    return jnp.sum(tensor.astype(jnp.float32), axis=tuple(range(tensor.ndim - 1)))
 
 
 def layer_norm(tensor):
@@ -70,18 +70,18 @@
 
 
 def rotate(tensor, cosine, signed_sine):
-    even_lane = jnp.arange(tensor.shape[1]) % 2 == 0
-    swapped = jnp.where(even_lane, jnp.roll(tensor, -1, axis=1), jnp.roll(tensor, 1, axis=1))
+    even_lane = jnp.arange(tensor.shape[-1]) % 2 == 0
+    swapped = jnp.where(even_lane, jnp.roll(tensor, -1, axis=-1), jnp.roll(tensor, 1, axis=-1))
     return tensor * cosine + swapped * signed_sine
 
 
 def split_heads(tensor):
-    return tensor.reshape(tensor.shape[0], tensor.shape[1] // HEAD, HEAD)
+    return tensor.reshape(tensor.shape[0], tensor.shape[1], tensor.shape[2] // HEAD, HEAD)
 
 
 def attend(queries, key_rows, value_rows):
     scores = jnp.einsum(
-        "qhd,khd->hqk",
+        "bqhd,bkhd->bhqk",
         split_heads(queries),
         split_heads(key_rows),
         preferred_element_type=jnp.float32,
@@ -91,9 +91,9 @@
     row_total = jnp.sum(exponentials, axis=-1, keepdims=True)
     probabilities = (exponentials / row_total).astype(jnp.bfloat16)
     result = jnp.einsum(
-        "hqk,khd->qhd", probabilities, split_heads(value_rows), preferred_element_type=jnp.float32
-    )
-    return (result.reshape(queries.shape[0], -1).astype(jnp.bfloat16), row_max + jnp.log(row_total))
+        "bhqk,bkhd->bqhd", probabilities, split_heads(value_rows), preferred_element_type=jnp.float32
+    )
+    return (result.reshape(queries.shape).astype(jnp.bfloat16), row_max + jnp.log(row_total))
 
 
 def attend_back(queries, key_rows, value_rows, log_total, grad_rows):
@@ -102,32 +102,32 @@
     grad_split = split_heads(grad_rows)
     scale_factor = HEAD ** (-0.5)
     scores = (
-        jnp.einsum("qhd,khd->hqk", query_split, key_split, preferred_element_type=jnp.float32)
+        jnp.einsum("bqhd,bkhd->bhqk", query_split, key_split, preferred_element_type=jnp.float32)
         * scale_factor
     )
     probs_full = jnp.exp(scores - log_total)
     probs_low = probs_full.astype(jnp.bfloat16)
     grad_values = jnp.einsum(
-        "hqk,qhd->khd", probs_low, grad_split, preferred_element_type=jnp.float32
+        "bhqk,bqhd->bkhd", probs_low, grad_split, preferred_element_type=jnp.float32
     )
     grad_probs = jnp.einsum(
-        "qhd,khd->hqk", grad_split, split_heads(value_rows), preferred_element_type=jnp.float32
+        "bqhd,bkhd->bhqk", grad_split, split_heads(value_rows), preferred_element_type=jnp.float32
     )
     grad_scores = (
         probs_full * (grad_probs - jnp.sum(grad_probs * probs_full, axis=-1, keepdims=True))
     ).astype(jnp.bfloat16)
     grad_queries = (
-        jnp.einsum("hqk,khd->qhd", grad_scores, key_split, preferred_element_type=jnp.float32)
+        jnp.einsum("bhqk,bkhd->bqhd", grad_scores, key_split, preferred_element_type=jnp.float32)
         * scale_factor
     )
     grad_keys = (
-        jnp.einsum("hqk,qhd->khd", grad_scores, query_split, preferred_element_type=jnp.float32)
+        jnp.einsum("bhqk,bqhd->bkhd", grad_scores, query_split, preferred_element_type=jnp.float32)
         * scale_factor
     )
     return (
-        grad_queries.reshape(queries.shape[0], -1),
-        grad_keys.reshape(key_rows.shape[0], -1),
-        grad_values.reshape(value_rows.shape[0], -1),
+        grad_queries.reshape(queries.shape),
+        grad_keys.reshape(key_rows.shape),
+        grad_values.reshape(value_rows.shape),
     )
 
 
@@ -253,10 +253,11 @@
     )
     gain_rows = gains.astype(jnp.float32)
     bias_rows = biases.astype(jnp.float32)
-    modulated = modulation.astype(jnp.float32) + time_emb.astype(jnp.float32)
-    cosine, signed_sine = rotary_tables(places, HEAD, HEADS)
+    modulated = modulation.astype(jnp.float32)[None] + time_emb.astype(jnp.float32)
+    mod = [modulated[:, row, None, :] for row in range(6)]
+    cosine, signed_sine = jax.vmap(lambda clip_places: rotary_tables(clip_places, HEAD, HEADS))(places)
     residual_in = hidden.astype(jnp.float32)
-    normed_full, pull_first = jax.vjp(modulate_norm, residual_in, modulated[0], modulated[1])
+    normed_full, pull_first = jax.vjp(modulate_norm, residual_in, mod[0], mod[1])
     normed = normed_full.astype(jnp.bfloat16)
     query_pre = self_q.apply(normed) + bias_rows[0]
     key_pre = self_k.apply(normed) + bias_rows[1]
@@ -270,14 +271,14 @@
 
     turned, pull_turn = jax.vjp(turn_both, query_pre, key_pre, gain_rows[0], gain_rows[1])
     query_heads, key_heads, value_heads = (
-        lax.all_to_all(turned[0].astype(jnp.bfloat16), SEQ, split_axis=1, concat_axis=0, tiled=True),
-        lax.all_to_all(turned[1].astype(jnp.bfloat16), SEQ, split_axis=1, concat_axis=0, tiled=True),
-        lax.all_to_all(value_low, SEQ, split_axis=1, concat_axis=0, tiled=True),
+        lax.all_to_all(turned[0].astype(jnp.bfloat16), SEQ, split_axis=2, concat_axis=1, tiled=True),
+        lax.all_to_all(turned[1].astype(jnp.bfloat16), SEQ, split_axis=2, concat_axis=1, tiled=True),
+        lax.all_to_all(value_low, SEQ, split_axis=2, concat_axis=1, tiled=True),
     )
     attn_heads, log_total = attend(query_heads, key_heads, value_heads)
-    attended = lax.all_to_all(attn_heads, SEQ, split_axis=0, concat_axis=1, tiled=True)
+    attended = lax.all_to_all(attn_heads, SEQ, split_axis=1, concat_axis=2, tiled=True)
     branch = self_o.apply(attended) + bias_rows[3]
-    after_attn = residual_in + branch * modulated[2]
+    after_attn = residual_in + branch * mod[2]
     crossed_full, pull_cross = jax.vjp(affine_norm, after_attn, gain_rows[4], bias_rows[8])
     crossed = crossed_full.astype(jnp.bfloat16)
     cross_query_pre = cross_q.apply(crossed) + bias_rows[4]
@@ -285,16 +286,16 @@
     cross_query = cross_query_full.astype(jnp.bfloat16)
     cross_rows, cross_total = attend(cross_query, key_all, value_all)
     second = after_attn + cross_o.apply(cross_rows) + bias_rows[7]
-    ffn_normed_full, pull_second = jax.vjp(modulate_norm, second, modulated[3], modulated[4])
+    ffn_normed_full, pull_second = jax.vjp(modulate_norm, second, mod[3], mod[4])
     ffn_normed = ffn_normed_full.astype(jnp.bfloat16)
     pre_act = ffn_in.apply(ffn_normed) + ffn_bias.astype(jnp.float32)
     activation_full, pull_gelu = jax.vjp(gelu_tanh, pre_act)
     activation = activation_full.astype(jnp.bfloat16)
     ffn_branch = ffn_out.apply(activation) + bias_rows[9]
-    mixed = (second + ffn_branch * modulated[5]).astype(jnp.bfloat16)
+    mixed = (second + ffn_branch * mod[5]).astype(jnp.bfloat16)
     grad_output = cotangent.astype(jnp.float32)
-    gate_ffn = jnp.sum(grad_output * ffn_branch, axis=0)
-    grad_ffn_branch = (grad_output * modulated[5]).astype(jnp.bfloat16)
+    gate_ffn = jnp.sum(grad_output * ffn_branch, axis=1)
+    grad_ffn_branch = (grad_output * mod[5]).astype(jnp.bfloat16)
     grad_pre_full = pull_gelu(ffn_out.back(grad_ffn_branch))[0]
     grad_pre = grad_pre_full.astype(jnp.bfloat16)
     grad_second_part, shift_ffn, scale_ffn = pull_second(ffn_in.back(grad_pre))
@@ -308,22 +309,22 @@
     grad_cross_query_pre = grad_cross_query_full.astype(jnp.bfloat16)
     grad_after_part, gain_norm, bias_norm = pull_cross(cross_q.back(grad_cross_query_pre))
     grad_after = grad_second + grad_after_part
-    gate_attn = jnp.sum(grad_after * branch, axis=0)
-    grad_branch = (grad_after * modulated[2]).astype(jnp.bfloat16)
+    gate_attn = jnp.sum(grad_after * branch, axis=1)
+    grad_branch = (grad_after * mod[2]).astype(jnp.bfloat16)
     grad_attended = self_o.back(grad_branch).astype(jnp.bfloat16)
-    grad_attn_heads = lax.all_to_all(grad_attended, SEQ, split_axis=1, concat_axis=0, tiled=True)
+    grad_attn_heads = lax.all_to_all(grad_attended, SEQ, split_axis=2, concat_axis=1, tiled=True)
     grad_query_heads, grad_key_heads, grad_value_heads = attend_back(
         query_heads, key_heads, value_heads, log_total, grad_attn_heads
     )
     grad_query_turned, grad_key_turned, grad_value = (
         lax.all_to_all(
-            grad_query_heads.astype(jnp.bfloat16), SEQ, split_axis=0, concat_axis=1, tiled=True
+            grad_query_heads.astype(jnp.bfloat16), SEQ, split_axis=1, concat_axis=2, tiled=True
         ),
         lax.all_to_all(
-            grad_key_heads.astype(jnp.bfloat16), SEQ, split_axis=0, concat_axis=1, tiled=True
+            grad_key_heads.astype(jnp.bfloat16), SEQ, split_axis=1, concat_axis=2, tiled=True
         ),
         lax.all_to_all(
-            grad_value_heads.astype(jnp.bfloat16), SEQ, split_axis=0, concat_axis=1, tiled=True
+            grad_value_heads.astype(jnp.bfloat16), SEQ, split_axis=1, concat_axis=2, tiled=True
         ),
     )
     grad_query_full, grad_key_full, gain_query, gain_key = pull_turn(
@@ -334,7 +335,9 @@
     grad_normed = self_q.back(grad_query_pre) + self_k.back(grad_key_pre) + self_v.back(grad_value)
     grad_start, shift_attn, scale_attn = pull_first(grad_normed)
     grad_hidden = grad_after + grad_start
-    grad_modulated = jnp.stack((shift_attn, scale_attn, gate_attn, shift_ffn, scale_ffn, gate_ffn))
+    grad_modulated = jnp.stack(
+        (shift_attn[:, 0], scale_attn[:, 0], gate_attn, shift_ffn[:, 0], scale_ffn[:, 0], gate_ffn), axis=1
+    )
     grad_gains = jnp.stack((gain_query, gain_key, gain_cross_query, jnp.zeros_like(gain_query), gain_norm))
     grad_biases = jnp.stack(
         (
@@ -350,7 +353,7 @@
             column_sums(grad_ffn_branch),
         )
     )
-    small = (grad_modulated, grad_gains, grad_biases, column_sums(grad_pre))
+    small = (jnp.sum(grad_modulated, axis=0), grad_gains, grad_biases, column_sums(grad_pre))
     split = (
         (normed, grad_query_pre),
         (normed, grad_key_pre),
@@ -421,38 +424,14 @@
         [part[i * words : (i + 1) * words] for part in (text_key_low, text_value) for i in range(clips)], axis=1
     )
     all_kv = lax.all_gather(local_kv, SEQ, axis=0, tiled=True)
-    mixed_list = []
-    hidden_list = []
-    key_grads = []
-    value_grads = []
-    clock_list = []
-    small_totals = None
-    pair_lists = None
-    for batch_index in range(clips):
-        mixed, grad_hidden, text_grads, grad_clock, small, split = micro_step(
-            weights,
-            hidden[batch_index],
-            all_kv[:, batch_index * model : (batch_index + 1) * model],
-            all_kv[:, (clips + batch_index) * model : (clips + batch_index + 1) * model],
-            time_emb[batch_index],
-            positions[batch_index],
-            cotangent[batch_index],
-        )
-        mixed_list.append(mixed)
-        hidden_list.append(grad_hidden)
-        key_grads.append(text_grads[0])
-        value_grads.append(text_grads[1])
-        clock_list.append(grad_clock)
-        if small_totals is None:
-            small_totals, pair_lists = small, [[pair] for pair in split]
-        else:
-            small_totals = tuple(a + b for a, b in zip(small_totals, small))
-            for found, pair in zip(pair_lists, split):
-                found.append(pair)
-    pairs = [
-        (jnp.concatenate([p[0] for p in found]), jnp.concatenate([p[1] for p in found]))
-        for found in pair_lists
-    ]
+    key_all = jnp.stack([all_kv[:, i * model : (i + 1) * model] for i in range(clips)])
+    value_all = jnp.stack([all_kv[:, (clips + i) * model : (clips + i + 1) * model] for i in range(clips)])
+    mixed, grad_hidden, text_grads, grad_time, small_totals, split = micro_step(
+        weights, hidden, key_all, value_all, time_emb, positions, cotangent
+    )
+    key_grads = [text_grads[0][i] for i in range(clips)]
+    value_grads = [text_grads[1][i] for i in range(clips)]
+    pairs = [(rows.reshape(-1, rows.shape[-1]), grad.reshape(-1, grad.shape[-1])) for rows, grad in split]
     split_grads = [
         split_weight.grad(rows, grad, quarters=index < 6)
         for index, (split_weight, (rows, grad)) in enumerate(
@@ -487,13 +466,12 @@
     attn_out_final = reduce_split(attn_out_grads, 1, spot)
     ffn_in_final = reduce_half(split_grads[6], 0, spot)
     ffn_out_final = reduce_half(split_grads[7], 0, spot)
-    grad_time = jnp.stack(clock_list)
     grad_mod, grad_gains, grad_biases, grad_ffn_bias, grad_time = reduce_small(
         grad_mod, grad_gains, grad_biases, grad_ffn_bias_local, grad_time, width, length
     )
     return (
-        jnp.stack(mixed_list),
-        jnp.stack(hidden_list),
+        mixed,
+        grad_hidden,
         grad_words.reshape(clips, words, model),
         grad_time,
         grad_mod,

time: 1890 us -> 1670 us (0.88)
  matrix products: 408 us -> 294 us
  waiting for transfers between devices: 1080 us -> 1030 us
  starting transfers between devices: 80 us -> 45.3 us
  other arithmetic: 138 us -> 109 us
    all_gather x2, waiting for transfers between devices: 200 us -> 122 us  [fetch_split(): mine = lax.all_gather(part, 'fsdp', axis=gather_axis, tiled=True)]
    dot_general x88 -> x48, matrix products: 215 us -> 139 us  [the longest x36 117 us: outer_cols(): lax.dot_general(operand, factor, (((operand.ndim - 1,), (1,)), ((), ())),...]
    ppermute x8, waiting for transfers between devices: 314 us -> 386 us  [swap_y(): return lax.ppermute(tensor, 'y', SWAP)]
    all_to_all x16 -> x8, waiting for transfers between devices: 77.8 us -> 35.3 us  [the longest x1 11.5 us: micro_step(): lax.all_to_all(grad_attended, SEQ, split_axis=2, concat_axis=1, tiled=True)]
    reduce_scatter x2, waiting for transfers between devices: 91.6 us -> 50.9 us  [reduce_split(): lax.psum_scatter(total, 'fsdp', scatter_dimension=scatter_axis, tiled=True)]
    dot_general x64 -> x36, matrix products: 114 us -> 81.3 us  [matmul(): return jnp.dot(operand, factor, preferred_element_type=jnp.float32)]
    all_to_all x16 -> x8, starting transfers between devices: 62.7 us -> 30.1 us  [the longest x1 4.15 us: micro_step(): lax.all_to_all(grad_key_heads.astype(jnp.bfloat16), SEQ, split_axis=1, co...]
    all_gather x1, waiting for transfers between devices: 0.01 us -> 30.4 us  [body(): all_kv = lax.all_gather(local_kv, SEQ, axis=0, tiled=True)]
  transfers between devices with their start and end apart: 52 -> 44, of which waited for: 22 -> 23; matrix products, arithmetic and copies ran while one was open for 26% -> 25% of each run, Pallas kernels for 0% -> 0%
where the time goes in v6:
time: 1670 us; the launch traced here: 1660 us
  waiting for transfers between devices  1030 us (62%)
  matrix products  294 us (18%)
  local copies, waits for them, and re-layouts  134 us (8%)
  other arithmetic  109 us (7%)
  starting transfers between devices  45.3 us (3%)
  blocking collectives  30.8 us (2%)
  between operations  17.7 us (1%)
    ppermute x8, waiting for transfers between devices, swap_y(): return lax.ppermute(tensor, 'y', SWAP)  386 us
    reduce_scatter x2, waiting for transfers between devices, reduce_half(): lax.psum_scatter(chip, 'fsdp', scatter_dimension=scatter_axis, tiled=True)  225 us
    all_gather x2, waiting for transfers between devices, fetch_split(): own = lax.all_gather(part, 'fsdp', axis=gather_axis, tiled=True)  124 us
    all_gather x2, waiting for transfers between devices, fetch_split(): mine = lax.all_gather(part, 'fsdp', axis=gather_axis, tiled=True)  122 us
    dot_general x36, matrix products, outer_cols(): lax.dot_general(operand, factor, (((operand.ndim - 1,), (1,)), ((), ())),...  117 us
    dot_general x36, matrix products, matmul(): return jnp.dot(operand, factor, preferred_element_type=jnp.float32)  81.3 us
    dot_general x36, matrix products, inner_rows(): lax.dot_general(operand, factor, (((0,), (0,)), ((), ())), preferred_elem...  73.1 us
    reduce_scatter x2, waiting for transfers between devices, reduce_split(): lax.psum_scatter(total, 'fsdp', scatter_dimension=scatter_axis, tiled=True)  50.9 us
  transfers between devices with their start and end apart: 44, of which 23 were waited for; matrix products, arithmetic and copies ran while one was open for 25% of the time, Pallas kernels for 0%

profile of v6, /device:TPU:0, one launch (start us, length us, event | category | flops | bytes accessed | tf_op | source)
XLA Modules:
  0.0 1656.9 jit_solution(3561253700649343394)
XLA Ops:
  15.7 106.1 %all-gather.7.cloned.1.call-done = bf16[6,1536,384]{2,1,0:T(8,128)(2,1)} async-done(((bf16[6,192,384]{2,1,0:T(8,128)(2,1)}), bf16[6,1536,384]{2,1,0:T(8,128)(2,1)}) %all-gather.7.cloned.1.call-update) | async-done | bytes 7077904 | tf_op jit(solution)/shard_map/all_gather | solution.py:193
  123.4 30.8 %all-gather = bf16[8,192,27]{1,2,0:T(8,128)(2,1)S(1)} all-gather(bf16[1,192,27]{1,2,0:T(8,128)(2,1)S(1)} %maximum_bitcast_fusion), channel_id=1, replica_groups=mesh['y'=2,'core'=2,'fsdp'=8] {'fsdp'}, dimensions={0}, use_global_device_ids=true | all-gather | bytes 93312 | tf_op jit(solution)/shard_map/all_gather | solution.py:228
  156.4 18.4 %all-gather.9.cloned.1.call-done = bf16[2,1536,384]{2,1,0:T(8,128)(2,1)} async-done(((bf16[2,192,384]{2,1,0:T(8,128)(2,1)}), bf16[2,1536,384]{2,1,0:T(8,128)(2,1)}) %all-gather.9.cloned.1.call-update) | async-done | bytes 2359312 | tf_op jit(solution)/shard_map/all_gather | solution.py:193
  176.3 101.1 %collective-permute-done = bf16[6,1536,384]{2,1,0:T(8,128)(2,1)} collective-permute-done((bf16[6,1536,384]{2,1,0:T(8,128)(2,1)}, bf16[6,1536,384]{2,1,0:T(8,128)(2,1)}, u32[]{:S(2)}, u32[]{:S(2)}) %collective-permute-start) | collective-permute-done | bytes 7077920 | tf_op jit(solution)/shard_map/ppermute | solution.py:153
  283.7 42.0 %collective-permute-done.3 = bf16[2,1536,384]{2,1,0:T(8,128)(2,1)} collective-permute-done((bf16[2,1536,384]{2,1,0:T(8,128)(2,1)}, bf16[2,1536,384]{2,1,0:T(8,128)(2,1)}, u32[]{:S(2)}, u32[]{:S(2)}) %collective-permute-start.3) | collective-permute-done | bytes 2359328 | tf_op jit(solution)/shard_map/ppermute | solution.py:153
  389.4 6.1 all-to-all-done.1
  403.0 7.5 all-to-all-done.2
  436.3 121.7 %all-gather.15.cloned.1.call-done = bf16[8960,768]{1,0:T(8,128)(2,1)} async-done(((bf16[1120,768]{1,0:T(8,128)(2,1)}), bf16[8960,768]{1,0:T(8,128)(2,1)}) %all-gather.15.cloned.1.call-update) | async-done | bytes 13762576 | tf_op jit(solution)/shard_map/all_gather | solution.py:189
  574.9 30.4 %all-gather.11.cloned.1.call-done = bf16[512,6144]{0,1:T(8,128)(2,1)} async-done(((bf16[128,6144]{0,1:T(8,128)(2,1)}), bf16[512,6144]{0,1:T(8,128)(2,1)}) %all-gather.11.cloned.1.call-update) | async-done | bytes 6291472 | tf_op jit(solution)/shard_map/all_gather | solution.py:426
  605.3 5.6 fusion.480
  640.7 9.9 fusion.14
  650.6 6.9 multiply_convert_fusion
  660.4 7.8 fusion.6
  670.5 12.5 fusion
  683.0 15.3 convert_reduce_fusion
  698.4 11.1 fusion.8
  709.4 12.0 multiply_reduce_fusion.10
  744.1 8.6 copy.227
  753.8 10.7 convolution_convert_fusion
  792.3 68.2 %collective-permute-done.15 = bf16[2,1536,384]{2,1,0:T(8,128)(2,1)S(1)} collective-permute-done((bf16[2,1536,384]{2,1,0:T(8,128)(2,1)S(1)}, bf16[2,1536,384]{2,1,0:T(8,128)(2,1)S(1)}, u32[]{:S(2)}, u32[]{:S(2)}) %collective-permute-start.15) | collective-permute-done | bytes 2359328 | tf_op jit(solution)/shard_map/ppermute | solution.py:153
  862.9 10.8 add_convert_fusion.1
  887.0 11.5 all-to-all-done.4
  1005.9 7.2 convolution_convert_fusion.1
  1017.5 141.5 %collective-permute-done.10 = bf16[6,1536,384]{2,1,0:T(8,128)(2,1)} collective-permute-done((bf16[6,1536,384]{2,1,0:T(8,128)(2,1)}, bf16[6,1536,384]{2,1,0:T(8,128)(2,1)}, u32[]{:S(2)}, u32[]{:S(2)}) %collective-permute-start.10) | collective-permute-done | bytes 7077920 | tf_op jit(solution)/shard_map/ppermute | solution.py:153
  1159.0 9.1 add_convert_fusion.2
  1168.2 10.1 add_convert_fusion
  1247.6 50.9 %reduce-scatter.11.cloned.1.call-done = bf16[6,192,384]{2,1,0:T(8,128)(2,1)} async-done(((bf16[6,1536,384]{2,1,0:T(8,128)(2,1)}), bf16[6,192,384]{2,1,0:T(8,128)(2,1)}) %reduce-scatter.11.cloned.1.call-update) | async-done | bytes 884752 | tf_op jit(solution)/shard_map/reduce_scatter | solution.py:206
  1300.0 225.1 %reduce-scatter.17.cloned.1.call-done = bf16[1120,768]{1,0:T(8,128)(2,1)} async-done(((bf16[8960,768]{1,0:T(8,128)(2,1)}), bf16[1120,768]{1,0:T(8,128)(2,1)}) %reduce-scatter.17.cloned.1.call-update) | async-done | bytes 1720336 | tf_op jit(solution)/shard_map/reduce_scatter | solution.py:217
  1536.4 28.1 %collective-permute-done.22 = bf16[1120,768]{1,0:T(8,128)(2,1)S(1)} collective-permute-done((bf16[1120,768]{1,0:T(8,128)(2,1)}, bf16[1120,768]{1,0:T(8,128)(2,1)S(1)}, u32[]{:S(2)}, u32[]{:S(2)}) %collective-permute-start.22) | collective-permute-done | bytes 1720352 | tf_op jit(solution)/shard_map/ppermute | solution.py:153
  1569.7 21.7 %reduce-scatter.21.cloned.1.call-done = f32[192,27]{1,0:T(8,128)} async-done(((f32[1536,27]{1,0:T(8,128)}), f32[192,27]{1,0:T(8,128)}) %reduce-scatter.21.cloned.1.call-update) | async-done | bytes 20752
  1597.7 27.2 %all-reduce.12.cloned.1.call-done = f32[23616]{0:T(1024)} async-done(((f32[23616]{0:T(1024)}), f32[23616]{0:T(1024)}) %all-reduce.12.cloned.1.call-update) | async-done | bytes 94480 | tf_op jit(solution)/shard_map/psum | solution.py:243
  1643.9 5.9 fusion.27
  (807 shorter events, 457.2 us)
Async XLA Ops:
  7.2 114.6 %all-gather.7.cloned.1.call-start = ((), (), s32[]{:S(2)}) async-start(), calls=%async_computation.14 | async-start | bytes 7962624 | tf_op jit(solution)/shard_map/all_gather | solution.py:193
  9.6 165.2 %all-gather.9.cloned.1.call-start = ((), (), s32[]{:S(2)}) async-start(), calls=%async_computation.15 | async-start | bytes 2654208 | tf_op jit(solution)/shard_map/all_gather | solution.py:193
  11.4 372.6 %all-gather.13.cloned.1.call-start = ((), (), s32[]{:S(2)}) async-start(), calls=%async_computation.17 | async-start | bytes 15482880 | tf_op jit(solution)/shard_map/all_gather | solution.py:189
  12.8 545.2 %all-gather.15.cloned.1.call-start = ((), (), s32[]{:S(2)}) async-start(), calls=%async_computation.18 | async-start | bytes 15482880 | tf_op jit(solution)/shard_map/all_gather | solution.py:189
  15.7 589.7 %all-gather.11.cloned.1.call-start = ((), (), s32[]{:S(2)}) async-start(), calls=%async_computation.16 | async-start | bytes 7864320 | tf_op jit(solution)/shard_map/all_gather | solution.py:426
  121.8 155.6 %collective-permute-start = (bf16[6,1536,384]{2,1,0:T(8,128)(2,1)}, bf16[6,1536,384]{2,1,0:T(8,128)(2,1)}, u32[]{:S(2)}, u32[]{:S(2)}) collective-permute-start(bf16[6,1536,384]{2,1,0:T(8,128)(2,1)} %all-gather.7.cloned.1.call-done), channel_id=1, source_target_pairs={{0,16},{16,0},{1,17},{17,1},{2,18},{18,2},{3,19},{19,3},{4,20},{20... | collective-permute-start | bytes 21233672 | tf_op jit(solution)/shard_map/ppermute | solution.py:153
  154.6 189.2 %collective-permute-start.2 = (bf16[6,1536,384]{2,1,0:T(8,128)(2,1)}, bf16[6,1536,384]{2,1,0:T(8,128)(2,1)}, u32[]{:S(2)}, u32[]{:S(2)}) collective-permute-start(bf16[6,1536,384]{2,1,0:T(8,128)(2,1)} %all-gather.7.cloned.1.call-done), channel_id=1, source_target_pairs={{0,8},{8,0},{1,9},{9,1},{2,10},{10,2},{3,11},{11,3},{4,12},{12,4},... | collective-permute-start | bytes 21233672 | tf_op jit(solution)/shard_map/ppermute | solution.py:135
  174.8 150.9 %collective-permute-start.3 = (bf16[2,1536,384]{2,1,0:T(8,128)(2,1)}, bf16[2,1536,384]{2,1,0:T(8,128)(2,1)}, u32[]{:S(2)}, u32[]{:S(2)}) collective-permute-start(bf16[2,1536,384]{2,1,0:T(8,128)(2,1)} %all-gather.9.cloned.1.call-done), channel_id=1, source_target_pairs={{0,16},{16,0},{1,17},{17,1},{2,18},{18,2},{3,19},{19,3},{4,20},{20... | collective-permute-start | bytes 7077896 | tf_op jit(solution)/shard_map/ppermute | solution.py:153
  277.4 78.4 %collective-permute-start.1 = (bf16[6,1536,384]{2,1,0:T(8,128)(2,1)}, bf16[6,1536,384]{2,1,0:T(8,128)(2,1)}, u32[]{:S(2)}, u32[]{:S(2)}) collective-permute-start(bf16[6,1536,384]{2,1,0:T(8,128)(2,1)} %collective-permute-done), channel_id=1, source_target_pairs={{0,8},{8,0},{1,9},{9,1},{2,10},{10,2},{3,11},{11,3},{4,12},{12,4},... | collective-permute-start | bytes 21233672 | tf_op jit(solution)/shard_map/ppermute | solution.py:135
  325.7 232.4 %collective-permute-start.4 = (bf16[2,1536,384]{2,1,0:T(8,128)(2,1)}, bf16[2,1536,384]{2,1,0:T(8,128)(2,1)}, u32[]{:S(2)}, u32[]{:S(2)}) collective-permute-start(bf16[2,1536,384]{2,1,0:T(8,128)(2,1)} %collective-permute-done.3), channel_id=1, source_target_pairs={{0,8},{8,0},{1,9},{9,1},{2,10},{10,2},{3,11},{11,3},{4,12},{12,4},... | collective-permute-start | bytes 7077896 | tf_op jit(solution)/shard_map/ppermute | solution.py:135
  384.0 256.6 %collective-permute-start.6 = (bf16[1536,4480]{1,0:T(8,128)(2,1)}, bf16[1536,4480]{1,0:T(8,128)(2,1)}, u32[]{:S(2)}, u32[]{:S(2)}) collective-permute-start(bf16[1536,4480]{1,0:T(8,128)(2,1)} %all-gather.13.cloned.1.call-done), channel_id=1, source_target_pairs={{0,8},{8,0},{1,9},{9,1},{2,10},{10,2},{3,11},{11,3},{4,12},{12,4},... | collective-permute-start | bytes 41287688 | tf_op jit(solution)/shard_map/ppermute | solution.py:135
  414.2 145.8 %collective-permute-start.5 = (bf16[2,1536,384]{2,1,0:T(8,128)(2,1)}, bf16[2,1536,384]{2,1,0:T(8,128)(2,1)}, u32[]{:S(2)}, u32[]{:S(2)}) collective-permute-start(bf16[2,1536,384]{2,1,0:T(8,128)(2,1)} %all-gather.9.cloned.1.call-done), channel_id=1, source_target_pairs={{0,8},{8,0},{1,9},{9,1},{2,10},{10,2},{3,11},{11,3},{4,12},{12,4},... | collective-permute-start | bytes 7077896 | tf_op jit(solution)/shard_map/ppermute | solution.py:135
  432.0 125.9 %all-to-all-start.3 = ((bf16[2,384,384]{2,0,1:T(2,128)(2,1)}), bf16[2,384,384]{2,0,1:T(2,128)(2,1)S(1)}, u32[]{:S(2)}, u32[]{:S(2)}) async-start(bf16[2,384,384]{2,0,1:T(2,128)(2,1)} %copy.169), calls=%async_computation.3 | async-start | bytes 1179648 | tf_op jit(solution)/shard_map/all_to_all | solution.py:279
  435.5 540.8 %reduce-scatter.19.cloned.1.call-start = ((), (), s32[]{:S(2)}) async-start(), calls=%async_computation.24 | async-start | bytes 7864320
  557.9 102.4 %collective-permute-start.7 = (bf16[8960,768]{1,0:T(8,128)(2,1)}, bf16[8960,768]{1,0:T(8,128)(2,1)}, u32[]{:S(2)}, u32[]{:S(2)}) collective-permute-start(bf16[8960,768]{1,0:T(8,128)(2,1)} %all-gather.15.cloned.1.call-done), channel_id=1, source_target_pairs={{0,8},{8,0},{1,9},{9,1},{2,10},{10,2},{3,11},{11,3},{4,12},{12,4},... | collective-permute-start | bytes 41287688 | tf_op jit(solution)/shard_map/ppermute | solution.py:135
  752.8 457.0 %reduce-scatter.13.cloned.1.call-start = ((), (), s32[]{:S(2)}) async-start(), calls=%async_computation.21 | async-start | bytes 2654208 | tf_op jit(solution)/shard_map/reduce_scatter | solution.py:206
  764.5 98.3 %collective-permute-start.18 = (bf16[1536,4480]{1,0:T(8,128)(2,1)}, bf16[1536,4480]{1,0:T(8,128)(2,1)}, u32[]{:S(2)}, u32[]{:S(2)}) collective-permute-start(bf16[1536,4480]{1,0:T(8,128)(2,1)} %convolution_convert_fusion), channel_id=1, source_target_pairs={{0,8},{8,0},{1,9},{9,1},{2,10},{10,2},{3,11},{11,3},{4,12},{12,4},... | collective-permute-start | bytes 41287688 | tf_op jit(solution)/shard_map/ppermute | solution.py:135
  789.7 70.9 %collective-permute-start.15 = (bf16[2,1536,384]{2,1,0:T(8,128)(2,1)S(1)}, bf16[2,1536,384]{2,1,0:T(8,128)(2,1)S(1)}, u32[]{:S(2)}, u32[]{:S(2)}) collective-permute-start(bf16[2,1536,384]{2,1,0:T(8,128)(2,1)S(1)} %fusion.37), channel_id=1, source_target_pairs={{0,16},{16,0},{1,17},{17,1},{2,18},{18,2},{3,19},{19,3},{4,20},{20... | collective-permute-start | bytes 7077896 | tf_op jit(solution)/shard_map/ppermute | solution.py:153
  862.8 371.1 %reduce-scatter.15.cloned.1.call-start = ((), (), s32[]{:S(2)}) async-start(), calls=%async_computation.22 | async-start | bytes 15482880 | tf_op jit(solution)/shard_map/reduce_scatter | solution.py:217
  949.2 349.3 %reduce-scatter.11.cloned.1.call-start = ((), (), s32[]{:S(2)}) async-start(), calls=%async_computation.20 | async-start | bytes 7962624 | tf_op jit(solution)/shard_map/reduce_scatter | solution.py:206
  998.8 18.7 %collective-permute-start.8 = (bf16[6,1536,384]{2,1,0:T(8,128)(2,1)}, bf16[6,1536,384]{2,1,0:T(8,128)(2,1)}, u32[]{:S(2)}, u32[]{:S(2)}) collective-permute-start(bf16[6,1536,384]{2,1,0:T(8,128)(2,1)} %fusion.71), channel_id=1, source_target_pairs={{0,8},{8,0},{1,9},{9,1},{2,10},{10,2},{3,11},{11,3},{4,12},{12,4},... | collective-permute-start | bytes 21233672 | tf_op jit(solution)/shard_map/ppermute | solution.py:135
  1004.1 154.9 %collective-permute-start.10 = (bf16[6,1536,384]{2,1,0:T(8,128)(2,1)}, bf16[6,1536,384]{2,1,0:T(8,128)(2,1)}, u32[]{:S(2)}, u32[]{:S(2)}) collective-permute-start(bf16[6,1536,384]{2,1,0:T(8,128)(2,1)} %add_convert_fusion.3), channel_id=1, source_target_pairs={{0,16},{16,0},{1,17},{17,1},{2,18},{18,2},{3,19},{19,3},{4,20},{20... | collective-permute-start | bytes 21233672 | tf_op jit(solution)/shard_map/ppermute | solution.py:153
  1013.1 155.1 %collective-permute-start.21 = (bf16[8960,768]{1,0:T(8,128)(2,1)}, bf16[8960,768]{1,0:T(8,128)(2,1)}, u32[]{:S(2)}, u32[]{:S(2)}) collective-permute-start(bf16[8960,768]{1,0:T(8,128)(2,1)} %convolution_convert_fusion.1), channel_id=1, source_target_pairs={{0,8},{8,0},{1,9},{9,1},{2,10},{10,2},{3,11},{11,3},{4,12},{12,4},... | collective-permute-start | bytes 41287688 | tf_op jit(solution)/shard_map/ppermute | solution.py:135
  1168.1 357.0 %reduce-scatter.17.cloned.1.call-start = ((), (), s32[]{:S(2)}) async-start(), calls=%async_computation.23 | async-start | bytes 15482880 | tf_op jit(solution)/shard_map/reduce_scatter | solution.py:217
  1178.4 412.9 %reduce-scatter.21.cloned.1.call-start = ((), (), s32[]{:S(2)}) async-start(), calls=%async_computation.25 | async-start | bytes 884736
  1233.9 292.6 %collective-permute-start.19 = (bf16[192,4480]{1,0:T(8,128)(2,1)}, bf16[192,4480]{1,0:T(8,128)(2,1)}, u32[]{:S(2)}, u32[]{:S(2)}) collective-permute-start(bf16[192,4480]{1,0:T(8,128)(2,1)} %reduce-scatter.15.cloned.1.call-done), channel_id=1, source_target_pairs={{0,16},{16,0},{1,17},{17,1},{2,18},{18,2},{3,19},{19,3},{4,20},{20... | collective-permute-start | bytes 5160968 | tf_op jit(solution)/shard_map/ppermute | solution.py:153
  1236.6 388.2 %all-reduce.12.cloned.1.call-start = ((), (), s32[]{:S(2)}) async-start(), calls=%async_computation.19 | async-start | bytes 196608 | tf_op jit(solution)/shard_map/psum | solution.py:243
  1298.5 235.2 %collective-permute-start.11 = (bf16[6,192,384]{2,1,0:T(8,128)(2,1)}, bf16[6,192,384]{2,1,0:T(8,128)(2,1)}, u32[]{:S(2)}, u32[]{:S(2)}) collective-permute-start(bf16[6,192,384]{2,1,0:T(8,128)(2,1)} %reduce-scatter.11.cloned.1.call-done), channel_id=1, source_target_pairs={{0,16},{16,0},{1,17},{17,1},{2,18},{18,2},{3,19},{19,3},{4,20},{20... | collective-permute-start | bytes 2654216 | tf_op jit(solution)/shard_map/ppermute | solution.py:153
  1525.1 39.4 %collective-permute-start.22 = (bf16[1120,768]{1,0:T(8,128)(2,1)}, bf16[1120,768]{1,0:T(8,128)(2,1)S(1)}, u32[]{:S(2)}, u32[]{:S(2)}) collective-permute-start(bf16[1120,768]{1,0:T(8,128)(2,1)} %reduce-scatter.17.cloned.1.call-done), channel_id=1, source_target_pairs={{0,16},{16,0},{1,17},{17,1},{2,18},{18,2},{3,19},{19,3},{4,20},{20... | collective-permute-start | bytes 5160968 | tf_op jit(solution)/shard_map/ppermute | solution.py:153
  1530.6 107.9 %collective-permute-start.20 = (f32[192,4480]{1,0:T(8,128)}, f32[192,4480]{1,0:T(8,128)}, u32[]{:S(2)}, u32[]{:S(2)}) collective-permute-start(f32[192,4480]{1,0:T(8,128)} %convert_add_fusion.1), channel_id=1, source_target_pairs={{0,8},{8,0},{1,9},{9,1},{2,10},{10,2},{3,11},{11,3},{4,12},{12,4},... | collective-permute-start | bytes 10321928 | tf_op jit(solution)/shard_map/ppermute | solution.py:135
  1535.9 96.2 %collective-permute-start.12 = (bf16[6,192,768]{2,1,0:T(8,128)(2,1)S(1)}, bf16[6,192,768]{2,1,0:T(8,128)(2,1)}, u32[]{:S(2)}, u32[]{:S(2)}) collective-permute-start(bf16[6,192,768]{2,1,0:T(8,128)(2,1)S(1)} %fusion.115), channel_id=1, source_target_pairs={{0,8},{8,0},{1,9},{9,1},{2,10},{10,2},{3,11},{11,3},{4,12},{12,4},... | collective-permute-start | bytes 5308424 | tf_op jit(solution)/shard_map/ppermute | solution.py:135
  1566.6 77.3 %collective-permute-start.23 = (f32[1120,768]{1,0:T(8,128)}, f32[1120,768]{1,0:T(8,128)}, u32[]{:S(2)}, u32[]{:S(2)}) collective-permute-start(f32[1120,768]{1,0:T(8,128)} %convert_add_fusion), channel_id=1, source_target_pairs={{0,8},{8,0},{1,9},{9,1},{2,10},{10,2},{3,11},{11,3},{4,12},{12,4},... | collective-permute-start | bytes 10321928 | tf_op jit(solution)/shard_map/ppermute | solution.py:135
  (200 other events, 2050.5 us)
Sparse Core Ops, SparseCore 0:
  10.8 110.9 all-gather.6
  124.6 50.1 all-gather.8
  177.6 188.9 all-gather.12
  369.2 188.6 all-gather.14
  559.9 45.3 all-gather.10
  752.9 76.3 reduce-scatter.18
  862.9 69.5 reduce-scatter.12
  936.1 223.1 reduce-scatter.14
  1168.2 130.2 reduce-scatter.10
  1302.0 223.0 reduce-scatter.16
  1529.0 62.3 reduce-scatter.20
  1594.1 30.6 all-reduce.11

commit v7 on v6

--- a/solution.py
+++ b/solution.py
@@ -238,11 +238,14 @@
     bias_rows = jnp.pad(grad_ffn_bias.reshape(shards, length), ((0, 0), (0, rows * width - length)))
     bias_rows = bias_rows.reshape(shards, rows, width).transpose(1, 0, 2).reshape(rows, shards * width)
     packed = jnp.concatenate([grad_mod, grad_gains, grad_biases, bias_rows], axis=0)
-    owned = lax.psum_scatter(packed, "fsdp", scatter_dimension=1, tiled=True)
-    flat = jnp.concatenate([owned.reshape(-1), grad_time.reshape(-1)])
-    summed = lax.psum(flat, SEQ)
-    owned = summed[: owned.size].reshape(owned.shape)
-    grad_time = summed[owned.size :].reshape(grad_time.shape)
+    place = lax.axis_index("fsdp")
+    slots = jnp.zeros((shards, grad_time.size), jnp.float32)
+    slots = lax.dynamic_update_slice_in_dim(slots, grad_time.reshape(1, -1), place, axis=0)
+    flat = jnp.concatenate([packed.reshape(-1), slots.reshape(-1)])
+    summed = lax.psum(flat, ("y", "core", "fsdp"))
+    owned = lax.dynamic_slice_in_dim(summed[: packed.size].reshape(packed.shape), place * width, width, axis=1)
+    grad_time = lax.dynamic_slice_in_dim(summed[packed.size :].reshape(shards, -1), place, 1, axis=0)
+    grad_time = grad_time.reshape(grad_time.size // (6 * packed.shape[1]), 6, packed.shape[1])
     bias_owned = owned[21:].reshape(-1)[:length]
     return owned[:6], owned[6:11], owned[11:21], bias_owned, grad_time
 
@@ -433,7 +436,7 @@
     value_grads = [text_grads[1][i] for i in range(clips)]
     pairs = [(rows.reshape(-1, rows.shape[-1]), grad.reshape(-1, grad.shape[-1])) for rows, grad in split]
     split_grads = [
-        split_weight.grad(rows, grad, quarters=index < 6)
+        split_weight.grad(rows, grad, quarters=index != 6)
         for index, (split_weight, (rows, grad)) in enumerate(
             zip(
                 (in_split[0], in_split[1], in_split[2], out_split[0], in_split[3], out_split[1], weights[9], weights[10]),
@@ -462,10 +465,13 @@
         for q in range(4)
     )
     attn_out_grads = tuple(jnp.stack([split_grads[3][q], split_grads[5][q]]) for q in range(4))
-    attn_in_final = reduce_split(attn_in_grads, 1, spot)
-    attn_out_final = reduce_split(attn_out_grads, 1, spot)
+    attn_final = reduce_split(
+        tuple(jnp.concatenate([a, b]) for a, b in zip(attn_in_grads, attn_out_grads)), 1, spot
+    )
+    attn_in_final = attn_final[: 2 * heads_in]
+    attn_out_final = attn_final[2 * heads_in :]
     ffn_in_final = reduce_half(split_grads[6], 0, spot)
-    ffn_out_final = reduce_half(split_grads[7], 0, spot)
+    ffn_out_final = reduce_split(split_grads[7], 0, spot)
     grad_mod, grad_gains, grad_biases, grad_ffn_bias, grad_time = reduce_small(
         grad_mod, grad_gains, grad_biases, grad_ffn_bias_local, grad_time, width, length
     )

time: 1670 us -> 1650 us (0.988)
  waiting for transfers between devices: 1030 us -> 983 us
  matrix products: 294 us -> 317 us
    reduce_scatter x2 -> x1, waiting for transfers between devices: 225 us -> 0.02 us  [reduce_half(): lax.psum_scatter(chip, 'fsdp', scatter_dimension=scatter_axis, tiled=True)]
    ppermute x8 -> x7, waiting for transfers between devices: 386 us -> 494 us  [swap_y(): return lax.ppermute(tensor, 'y', SWAP)]
    psum x1, waiting for transfers between devices: 27.2 us -> 100 us  [reduce_small(): summed = lax.psum(flat, ('y', 'core', 'fsdp'))]
    reduce_scatter x2, waiting for transfers between devices: 50.9 us -> 81.5 us  [reduce_split(): lax.psum_scatter(total, 'fsdp', scatter_dimension=scatter_axis, tiled=True)]
    dot_general x36 -> x38, matrix products: 73.1 us -> 101 us  [inner_rows(): lax.dot_general(operand, factor, (((0,), (0,)), ((), ())), preferred_elem...]
    unnamed x14 -> x11, waiting for transfers between devices: 21.9 us -> 0.17 us
    unnamed x385 -> x396, local copies, waits for them, and re-layouts: 30.7 us -> 34.1 us
  transfers between devices with their start and end apart: 44 -> 39, of which waited for: 23 -> 17; matrix products, arithmetic and copies ran while one was open for 25% -> 28% of each run, Pallas kernels for 0% -> 0%
where the time goes in v7:
time: 1650 us; the launch traced here: 1640 us
  waiting for transfers between devices  983 us (60%)
  matrix products  317 us (19%)
  local copies, waits for them, and re-layouts  126 us (8%)
  other arithmetic  117 us (7%)
  starting transfers between devices  45.1 us (3%)
  blocking collectives  30.8 us (2%)
  between operations  18.2 us (1%)
    ppermute x7, waiting for transfers between devices, swap_y(): return lax.ppermute(tensor, 'y', SWAP)  494 us
    all_gather x2, waiting for transfers between devices, fetch_split(): own = lax.all_gather(part, 'fsdp', axis=gather_axis, tiled=True)  124 us
    all_gather x2, waiting for transfers between devices, fetch_split(): mine = lax.all_gather(part, 'fsdp', axis=gather_axis, tiled=True)  120 us
    dot_general x36, matrix products, outer_cols(): lax.dot_general(operand, factor, (((operand.ndim - 1,), (1,)), ((), ())),...  116 us
    dot_general x38, matrix products, inner_rows(): lax.dot_general(operand, factor, (((0,), (0,)), ((), ())), preferred_elem...  101 us
    psum x1, waiting for transfers between devices, reduce_small(): summed = lax.psum(flat, ('y', 'core', 'fsdp'))  100 us
    reduce_scatter x2, waiting for transfers between devices, reduce_split(): lax.psum_scatter(total, 'fsdp', scatter_dimension=scatter_axis, tiled=True)  81.5 us
    dot_general x36, matrix products, matmul(): return jnp.dot(operand, factor, preferred_element_type=jnp.float32)  78.3 us
  transfers between devices with their start and end apart: 39, of which 17 were waited for; matrix products, arithmetic and copies ran while one was open for 28% of the time, Pallas kernels for 0%

profile of v7, /device:TPU:0, one launch (start us, length us, event | category | flops | bytes accessed | tf_op | source)
XLA Modules:
  0.0 1636.7 jit_solution(18411990499337796379)
XLA Ops:
  15.7 106.1 %all-gather.7.cloned.1.call-done = bf16[6,1536,384]{2,1,0:T(8,128)(2,1)} async-done(((bf16[6,192,384]{2,1,0:T(8,128)(2,1)}), bf16[6,1536,384]{2,1,0:T(8,128)(2,1)}) %all-gather.7.cloned.1.call-update) | async-done | bytes 7077904 | tf_op jit(solution)/shard_map/all_gather | solution.py:193
  123.4 30.8 %all-gather = bf16[8,192,27]{1,2,0:T(8,128)(2,1)S(1)} all-gather(bf16[1,192,27]{1,2,0:T(8,128)(2,1)S(1)} %maximum_bitcast_fusion), channel_id=1, replica_groups=mesh['y'=2,'core'=2,'fsdp'=8] {'fsdp'}, dimensions={0}, use_global_device_ids=true | all-gather | bytes 93312 | tf_op jit(solution)/shard_map/all_gather | solution.py:228
  156.4 18.4 %all-gather.9.cloned.1.call-done = bf16[2,1536,384]{2,1,0:T(8,128)(2,1)} async-done(((bf16[2,192,384]{2,1,0:T(8,128)(2,1)}), bf16[2,1536,384]{2,1,0:T(8,128)(2,1)}) %all-gather.9.cloned.1.call-update) | async-done | bytes 2359312 | tf_op jit(solution)/shard_map/all_gather | solution.py:193
  176.3 101.1 %collective-permute-done = bf16[6,1536,384]{2,1,0:T(8,128)(2,1)} collective-permute-done((bf16[6,1536,384]{2,1,0:T(8,128)(2,1)}, bf16[6,1536,384]{2,1,0:T(8,128)(2,1)}, u32[]{:S(2)}, u32[]{:S(2)}) %collective-permute-start) | collective-permute-done | bytes 7077920 | tf_op jit(solution)/shard_map/ppermute | solution.py:153
  284.2 41.5 %collective-permute-done.3 = bf16[2,1536,384]{2,1,0:T(8,128)(2,1)} collective-permute-done((bf16[2,1536,384]{2,1,0:T(8,128)(2,1)}, bf16[2,1536,384]{2,1,0:T(8,128)(2,1)}, u32[]{:S(2)}, u32[]{:S(2)}) %collective-permute-start.3) | collective-permute-done | bytes 2359328 | tf_op jit(solution)/shard_map/ppermute | solution.py:153
  389.4 6.1 all-to-all-done.1
  403.0 7.5 all-to-all-done.2
  418.9 7.9 all-to-all-done
  438.3 119.7 %all-gather.15.cloned.1.call-done = bf16[8960,768]{1,0:T(8,128)(2,1)} async-done(((bf16[1120,768]{1,0:T(8,128)(2,1)}), bf16[8960,768]{1,0:T(8,128)(2,1)}) %all-gather.15.cloned.1.call-update) | async-done | bytes 13762576 | tf_op jit(solution)/shard_map/all_gather | solution.py:189
  574.9 30.5 %all-gather.11.cloned.1.call-done = bf16[512,6144]{0,1:T(8,128)(2,1)} async-done(((bf16[128,6144]{0,1:T(8,128)(2,1)}), bf16[512,6144]{0,1:T(8,128)(2,1)}) %all-gather.11.cloned.1.call-update) | async-done | bytes 6291472 | tf_op jit(solution)/shard_map/all_gather | solution.py:429
  640.2 6.6 fusion.14
  655.3 7.8 fusion.6
  665.4 12.5 fusion
  677.9 15.1 convert_reduce_fusion
  693.0 11.1 fusion.8
  704.1 12.4 multiply_reduce_fusion.10
  719.8 8.9 convolution_convert_fusion
  748.2 8.6 copy.227
  757.3 15.2 add_convert_fusion
  772.6 7.1 convolution_convert_fusion.1
  812.7 9.9 all-to-all-done.4
  844.5 6.7 convolution_convert_fusion.2
  897.3 12.0 add_convert_fusion.4
  954.1 106.4 %collective-permute-done.18 = bf16[8960,384]{1,0:T(8,128)(2,1)} collective-permute-done((bf16[8960,384]{1,0:T(8,128)(2,1)}, bf16[8960,384]{1,0:T(8,128)(2,1)}, u32[]{:S(2)}, u32[]{:S(2)}) %collective-permute-start.18) | collective-permute-done | bytes 6881312 | tf_op jit(solution)/shard_map/ppermute | solution.py:153
  1060.5 9.3 add_convert_fusion.3
  1075.7 14.4 add_convert_fusion.2
  1101.0 194.5 %collective-permute-done.10 = bf16[8,1536,384]{2,1,0:T(8,128)(2,1)} collective-permute-done((bf16[8,1536,384]{2,1,0:T(8,128)(2,1)}, bf16[8,1536,384]{2,1,0:T(8,128)(2,1)}, u32[]{:S(2)}, u32[]{:S(2)}) %collective-permute-start.10) | collective-permute-done | bytes 9437216 | tf_op jit(solution)/shard_map/ppermute | solution.py:153
  1295.5 10.7 add_convert_fusion.1
  1344.9 32.8 %collective-permute-done.14 = bf16[192,4480]{1,0:T(8,128)(2,1)} collective-permute-done((bf16[192,4480]{1,0:T(8,128)(2,1)}, bf16[192,4480]{1,0:T(8,128)(2,1)}, u32[]{:S(2)}, u32[]{:S(2)}) %collective-permute-start.14) | collective-permute-done | bytes 1720352 | tf_op jit(solution)/shard_map/ppermute | solution.py:153
  1388.0 81.5 %reduce-scatter.7.cloned.1.call-done = bf16[8,192,384]{2,1,0:T(8,128)(2,1)} async-done(((bf16[8,1536,384]{2,1,0:T(8,128)(2,1)}), bf16[8,192,384]{2,1,0:T(8,128)(2,1)}) %reduce-scatter.7.cloned.1.call-update) | async-done | bytes 1179664 | tf_op jit(solution)/shard_map/reduce_scatter | solution.py:206
  1480.8 18.1 %collective-permute-done.11 = bf16[8,192,384]{2,1,0:T(8,128)(2,1)S(1)} collective-permute-done((bf16[8,192,384]{2,1,0:T(8,128)(2,1)}, bf16[8,192,384]{2,1,0:T(8,128)(2,1)S(1)}, u32[]{:S(2)}, u32[]{:S(2)}) %collective-permute-start.11) | collective-permute-done | bytes 1179680 | tf_op jit(solution)/shard_map/ppermute | solution.py:153
  1503.2 100.5 %all-reduce.12.cloned.1.call-done = f32[188928]{0:T(1024)} async-done(((f32[188928]{0:T(1024)}), f32[188928]{0:T(1024)}) %all-reduce.12.cloned.1.call-update) | async-done | bytes 755728 | tf_op jit(solution)/shard_map/psum | solution.py:245
  (807 shorter events, 446.9 us)
Async XLA Ops:
  7.2 114.6 %all-gather.7.cloned.1.call-start = ((), (), s32[]{:S(2)}) async-start(), calls=%async_computation.12 | async-start | bytes 7962624 | tf_op jit(solution)/shard_map/all_gather | solution.py:193
  9.6 165.2 %all-gather.9.cloned.1.call-start = ((), (), s32[]{:S(2)}) async-start(), calls=%async_computation.13 | async-start | bytes 2654208 | tf_op jit(solution)/shard_map/all_gather | solution.py:193
  11.4 372.7 %all-gather.13.cloned.1.call-start = ((), (), s32[]{:S(2)}) async-start(), calls=%async_computation.15 | async-start | bytes 15482880 | tf_op jit(solution)/shard_map/all_gather | solution.py:189
  12.8 545.2 %all-gather.15.cloned.1.call-start = ((), (), s32[]{:S(2)}) async-start(), calls=%async_computation.16 | async-start | bytes 15482880 | tf_op jit(solution)/shard_map/all_gather | solution.py:189
  15.7 589.7 %all-gather.11.cloned.1.call-start = ((), (), s32[]{:S(2)}) async-start(), calls=%async_computation.14 | async-start | bytes 7864320 | tf_op jit(solution)/shard_map/all_gather | solution.py:429
  121.8 155.6 %collective-permute-start = (bf16[6,1536,384]{2,1,0:T(8,128)(2,1)}, bf16[6,1536,384]{2,1,0:T(8,128)(2,1)}, u32[]{:S(2)}, u32[]{:S(2)}) collective-permute-start(bf16[6,1536,384]{2,1,0:T(8,128)(2,1)} %all-gather.7.cloned.1.call-done), channel_id=1, source_target_pairs={{0,16},{16,0},{1,17},{17,1},{2,18},{18,2},{3,19},{19,3},{4,20},{20... | collective-permute-start | bytes 21233672 | tf_op jit(solution)/shard_map/ppermute | solution.py:153
  154.6 189.2 %collective-permute-start.2 = (bf16[6,1536,384]{2,1,0:T(8,128)(2,1)}, bf16[6,1536,384]{2,1,0:T(8,128)(2,1)}, u32[]{:S(2)}, u32[]{:S(2)}) collective-permute-start(bf16[6,1536,384]{2,1,0:T(8,128)(2,1)} %all-gather.7.cloned.1.call-done), channel_id=1, source_target_pairs={{0,8},{8,0},{1,9},{9,1},{2,10},{10,2},{3,11},{11,3},{4,12},{12,4},... | collective-permute-start | bytes 21233672 | tf_op jit(solution)/shard_map/ppermute | solution.py:135
  174.8 150.9 %collective-permute-start.3 = (bf16[2,1536,384]{2,1,0:T(8,128)(2,1)}, bf16[2,1536,384]{2,1,0:T(8,128)(2,1)}, u32[]{:S(2)}, u32[]{:S(2)}) collective-permute-start(bf16[2,1536,384]{2,1,0:T(8,128)(2,1)} %all-gather.9.cloned.1.call-done), channel_id=1, source_target_pairs={{0,16},{16,0},{1,17},{17,1},{2,18},{18,2},{3,19},{19,3},{4,20},{20... | collective-permute-start | bytes 7077896 | tf_op jit(solution)/shard_map/ppermute | solution.py:153
  277.4 78.4 %collective-permute-start.1 = (bf16[6,1536,384]{2,1,0:T(8,128)(2,1)}, bf16[6,1536,384]{2,1,0:T(8,128)(2,1)}, u32[]{:S(2)}, u32[]{:S(2)}) collective-permute-start(bf16[6,1536,384]{2,1,0:T(8,128)(2,1)} %collective-permute-done), channel_id=1, source_target_pairs={{0,8},{8,0},{1,9},{9,1},{2,10},{10,2},{3,11},{11,3},{4,12},{12,4},... | collective-permute-start | bytes 21233672 | tf_op jit(solution)/shard_map/ppermute | solution.py:135
  325.7 232.4 %collective-permute-start.4 = (bf16[2,1536,384]{2,1,0:T(8,128)(2,1)}, bf16[2,1536,384]{2,1,0:T(8,128)(2,1)}, u32[]{:S(2)}, u32[]{:S(2)}) collective-permute-start(bf16[2,1536,384]{2,1,0:T(8,128)(2,1)} %collective-permute-done.3), channel_id=1, source_target_pairs={{0,8},{8,0},{1,9},{9,1},{2,10},{10,2},{3,11},{11,3},{4,12},{12,4},... | collective-permute-start | bytes 7077896 | tf_op jit(solution)/shard_map/ppermute | solution.py:135
  384.1 256.0 %collective-permute-start.6 = (bf16[1536,4480]{1,0:T(8,128)(2,1)}, bf16[1536,4480]{1,0:T(8,128)(2,1)}, u32[]{:S(2)}, u32[]{:S(2)}) collective-permute-start(bf16[1536,4480]{1,0:T(8,128)(2,1)} %all-gather.13.cloned.1.call-done), channel_id=1, source_target_pairs={{0,8},{8,0},{1,9},{9,1},{2,10},{10,2},{3,11},{11,3},{4,12},{12,4},... | collective-permute-start | bytes 41287688 | tf_op jit(solution)/shard_map/ppermute | solution.py:135
  415.2 144.9 %collective-permute-start.5 = (bf16[2,1536,384]{2,1,0:T(8,128)(2,1)}, bf16[2,1536,384]{2,1,0:T(8,128)(2,1)}, u32[]{:S(2)}, u32[]{:S(2)}) collective-permute-start(bf16[2,1536,384]{2,1,0:T(8,128)(2,1)} %all-gather.9.cloned.1.call-done), channel_id=1, source_target_pairs={{0,8},{8,0},{1,9},{9,1},{2,10},{10,2},{3,11},{11,3},{4,12},{12,4},... | collective-permute-start | bytes 7077896 | tf_op jit(solution)/shard_map/ppermute | solution.py:135
  434.7 123.3 %all-to-all-start.3 = ((bf16[2,384,384]{2,0,1:T(2,128)(2,1)}), bf16[2,384,384]{2,0,1:T(2,128)(2,1)S(1)}, u32[]{:S(2)}, u32[]{:S(2)}) async-start(bf16[2,384,384]{2,0,1:T(2,128)(2,1)} %copy.169), calls=%async_computation.3 | async-start | bytes 1179648 | tf_op jit(solution)/shard_map/all_to_all | solution.py:282
  438.1 473.6 %reduce-scatter.13.cloned.1.call-start = ((), (), s32[]{:S(2)}) async-start(), calls=%async_computation.21 | async-start | bytes 7864320
  557.9 97.3 %collective-permute-start.7 = (bf16[8960,768]{1,0:T(8,128)(2,1)}, bf16[8960,768]{1,0:T(8,128)(2,1)}, u32[]{:S(2)}, u32[]{:S(2)}) collective-permute-start(bf16[8960,768]{1,0:T(8,128)(2,1)} %all-gather.15.cloned.1.call-done), channel_id=1, source_target_pairs={{0,8},{8,0},{1,9},{9,1},{2,10},{10,2},{3,11},{11,3},{4,12},{12,4},... | collective-permute-start | bytes 41287688 | tf_op jit(solution)/shard_map/ppermute | solution.py:135
  728.7 28.6 %collective-permute-start.13 = (bf16[1536,4480]{1,0:T(8,128)(2,1)}, bf16[1536,4480]{1,0:T(8,128)(2,1)}, u32[]{:S(2)}, u32[]{:S(2)}) collective-permute-start(bf16[1536,4480]{1,0:T(8,128)(2,1)} %convolution_convert_fusion), channel_id=1, source_target_pairs={{0,8},{8,0},{1,9},{9,1},{2,10},{10,2},{3,11},{11,3},{4,12},{12,4},... | collective-permute-start | bytes 41287688 | tf_op jit(solution)/shard_map/ppermute | solution.py:135
  756.8 580.0 %reduce-scatter.9.cloned.1.call-start = ((), (), s32[]{:S(2)}) async-start(), calls=%async_computation.19 | async-start | bytes 15482880 | tf_op jit(solution)/shard_map/reduce_scatter | solution.py:217
  779.7 117.5 %collective-permute-start.17 = (bf16[8960,384]{1,0:T(8,128)(2,1)}, bf16[8960,384]{1,0:T(8,128)(2,1)}, u32[]{:S(2)}, u32[]{:S(2)}) collective-permute-start(bf16[8960,384]{1,0:T(8,128)(2,1)} %convolution_convert_fusion.1), channel_id=1, source_target_pairs={{0,8},{8,0},{1,9},{9,1},{2,10},{10,2},{3,11},{11,3},{4,12},{12,4},... | collective-permute-start | bytes 20643848 | tf_op jit(solution)/shard_map/ppermute | solution.py:135
  851.2 102.9 %collective-permute-start.16 = (bf16[8960,384]{1,0:T(8,128)(2,1)}, bf16[8960,384]{1,0:T(8,128)(2,1)}, u32[]{:S(2)}, u32[]{:S(2)}) collective-permute-start(bf16[8960,384]{1,0:T(8,128)(2,1)} %convolution_convert_fusion.2), channel_id=1, source_target_pairs={{0,8},{8,0},{1,9},{9,1},{2,10},{10,2},{3,11},{11,3},{4,12},{12,4},... | collective-permute-start | bytes 20643848 | tf_op jit(solution)/shard_map/ppermute | solution.py:135
  874.0 470.3 %reduce-scatter.11.cloned.1.call-start = ((), (), s32[]{:S(2)}) async-start(), calls=%async_computation.20 | async-start | bytes 7741440 | tf_op jit(solution)/shard_map/reduce_scatter | solution.py:206
  909.3 151.2 %collective-permute-start.18 = (bf16[8960,384]{1,0:T(8,128)(2,1)}, bf16[8960,384]{1,0:T(8,128)(2,1)}, u32[]{:S(2)}, u32[]{:S(2)}) collective-permute-start(bf16[8960,384]{1,0:T(8,128)(2,1)} %add_convert_fusion.4), channel_id=1, source_target_pairs={{0,16},{16,0},{1,17},{17,1},{2,18},{18,2},{3,19},{19,3},{4,20},{20... | collective-permute-start | bytes 20643848 | tf_op jit(solution)/shard_map/ppermute | solution.py:153
  927.9 147.9 %collective-permute-start.9 = (bf16[8,1536,384]{2,1,0:T(8,128)(2,1)}, bf16[8,1536,384]{2,1,0:T(8,128)(2,1)}, u32[]{:S(2)}, u32[]{:S(2)}) collective-permute-start(bf16[8,1536,384]{2,1,0:T(8,128)(2,1)} %fusion.101), channel_id=1, source_target_pairs={{0,8},{8,0},{1,9},{9,1},{2,10},{10,2},{3,11},{11,3},{4,12},{12,4},... | collective-permute-start | bytes 28311560 | tf_op jit(solution)/shard_map/ppermute | solution.py:135
  1069.8 399.7 %reduce-scatter.7.cloned.1.call-start = ((), (), s32[]{:S(2)}) async-start(), calls=%async_computation.18 | async-start | bytes 10616832 | tf_op jit(solution)/shard_map/reduce_scatter | solution.py:206
  1073.6 27.4 %collective-permute-start.8 = (bf16[8,1536,384]{2,1,0:T(8,128)(2,1)}, bf16[8,1536,384]{2,1,0:T(8,128)(2,1)S(1)}, u32[]{:S(2)}, u32[]{:S(2)}) collective-permute-start(bf16[8,1536,384]{2,1,0:T(8,128)(2,1)} %fusion.89), channel_id=1, source_target_pairs={{0,8},{8,0},{1,9},{9,1},{2,10},{10,2},{3,11},{11,3},{4,12},{12,4},... | collective-permute-start | bytes 28311560 | tf_op jit(solution)/shard_map/ppermute | solution.py:135
  1090.1 205.4 %collective-permute-start.10 = (bf16[8,1536,384]{2,1,0:T(8,128)(2,1)}, bf16[8,1536,384]{2,1,0:T(8,128)(2,1)}, u32[]{:S(2)}, u32[]{:S(2)}) collective-permute-start(bf16[8,1536,384]{2,1,0:T(8,128)(2,1)} %add_convert_fusion.2), channel_id=1, source_target_pairs={{0,16},{16,0},{1,17},{17,1},{2,18},{18,2},{3,19},{19,3},{4,20},{20... | collective-permute-start | bytes 28311560 | tf_op jit(solution)/shard_map/ppermute | solution.py:153
  1306.4 297.3 %all-reduce.12.cloned.1.call-start = ((), (), s32[]{:S(2)}) async-start(), calls=%async_computation.17 | async-start | bytes 1515520 | tf_op jit(solution)/shard_map/psum | solution.py:245
  1336.9 40.8 %collective-permute-start.14 = (bf16[192,4480]{1,0:T(8,128)(2,1)}, bf16[192,4480]{1,0:T(8,128)(2,1)}, u32[]{:S(2)}, u32[]{:S(2)}) collective-permute-start(bf16[192,4480]{1,0:T(8,128)(2,1)} %reduce-scatter.9.cloned.1.call-done), channel_id=1, source_target_pairs={{0,16},{16,0},{1,17},{17,1},{2,18},{18,2},{3,19},{19,3},{4,20},{20... | collective-permute-start | bytes 5160968 | tf_op jit(solution)/shard_map/ppermute | solution.py:153
  1344.3 126.7 %collective-permute-start.19 = (bf16[1120,384]{1,0:T(8,128)(2,1)}, bf16[1120,384]{1,0:T(8,128)(2,1)}, u32[]{:S(2)}, u32[]{:S(2)}) collective-permute-start(bf16[1120,384]{1,0:T(8,128)(2,1)} %reduce-scatter.11.cloned.1.call-done), channel_id=1, source_target_pairs={{0,16},{16,0},{1,17},{17,1},{2,18},{18,2},{3,19},{19,3},{4,20},{20... | collective-permute-start | bytes 2580488 | tf_op jit(solution)/shard_map/ppermute | solution.py:153
  1381.8 233.8 %collective-permute-start.15 = (f32[192,4480]{1,0:T(8,128)}, f32[192,4480]{1,0:T(8,128)}, u32[]{:S(2)}, u32[]{:S(2)}) collective-permute-start(f32[192,4480]{1,0:T(8,128)} %convert_add_fusion), channel_id=1, source_target_pairs={{0,8},{8,0},{1,9},{9,1},{2,10},{10,2},{3,11},{11,3},{4,12},{12,4},... | collective-permute-start | bytes 10321928 | tf_op jit(solution)/shard_map/ppermute | solution.py:135
  1469.5 29.4 %collective-permute-start.11 = (bf16[8,192,384]{2,1,0:T(8,128)(2,1)}, bf16[8,192,384]{2,1,0:T(8,128)(2,1)S(1)}, u32[]{:S(2)}, u32[]{:S(2)}) collective-permute-start(bf16[8,192,384]{2,1,0:T(8,128)(2,1)} %reduce-scatter.7.cloned.1.call-done), channel_id=1, source_target_pairs={{0,16},{16,0},{1,17},{17,1},{2,18},{18,2},{3,19},{19,3},{4,20},{20... | collective-permute-start | bytes 3538952 | tf_op jit(solution)/shard_map/ppermute | solution.py:153
  1474.4 136.1 %collective-permute-start.20 = (bf16[1120,768]{1,0:T(8,128)(2,1)}, bf16[1120,768]{1,0:T(8,128)(2,1)}, u32[]{:S(2)}, u32[]{:S(2)}) collective-permute-start(bf16[1120,768]{1,0:T(8,128)(2,1)} %fusion.130), channel_id=1, source_target_pairs={{0,8},{8,0},{1,9},{9,1},{2,10},{10,2},{3,11},{11,3},{4,12},{12,4},... | collective-permute-start | bytes 5160968 | tf_op jit(solution)/shard_map/ppermute | solution.py:135
  1500.1 120.9 %collective-permute-start.12 = (bf16[8,192,768]{2,1,0:T(8,128)(2,1)S(1)}, bf16[8,192,768]{2,1,0:T(8,128)(2,1)}, u32[]{:S(2)}, u32[]{:S(2)}) collective-permute-start(bf16[8,192,768]{2,1,0:T(8,128)(2,1)S(1)} %fusion.110), channel_id=1, source_target_pairs={{0,8},{8,0},{1,9},{9,1},{2,10},{10,2},{3,11},{11,3},{4,12},{12,4},... | collective-permute-start | bytes 7077896 | tf_op jit(solution)/shard_map/ppermute | solution.py:135
  (202 other events, 2553.5 us)
Sparse Core Ops, SparseCore 0:
  10.8 110.9 all-gather.6
  124.6 50.1 all-gather.8
  177.6 188.9 all-gather.12
  369.2 188.6 all-gather.14
  559.9 45.3 all-gather.10
  757.0 60.5 reduce-scatter.12
  821.2 224.1 reduce-scatter.8
  1070.0 127.8 reduce-scatter.10
  1306.5 162.9 reduce-scatter.6
  1475.2 128.4 all-reduce.11

commit v8 on v6

--- a/solution.py
+++ b/solution.py
@@ -433,7 +433,7 @@
     value_grads = [text_grads[1][i] for i in range(clips)]
     pairs = [(rows.reshape(-1, rows.shape[-1]), grad.reshape(-1, grad.shape[-1])) for rows, grad in split]
     split_grads = [
-        split_weight.grad(rows, grad, quarters=index < 6)
+        split_weight.grad(rows, grad, quarters=index == 7)
         for index, (split_weight, (rows, grad)) in enumerate(
             zip(
                 (in_split[0], in_split[1], in_split[2], out_split[0], in_split[3], out_split[1], weights[9], weights[10]),
@@ -448,24 +448,33 @@
     grad_text_value = jnp.concatenate(owned_parts[clips:], axis=0).astype(jnp.bfloat16)
     grad_text_key_full, gain_cross_key = pull_text_key(grad_text_key)
     grad_text_key_pre = grad_text_key_full.astype(jnp.bfloat16)
-    weight_cross_key = cross_k.grad(text_flat, grad_text_key_pre)
-    weight_cross_value = cross_v.grad(text_flat, grad_text_value)
+    weight_cross_key = cross_k.grad(text_flat, grad_text_key_pre, quarters=False)
+    weight_cross_value = cross_v.grad(text_flat, grad_text_value, quarters=False)
     grad_words = cross_k.back(grad_text_key_pre) + cross_v.back(grad_text_value)
     grad_mod, grad_gains, grad_biases, grad_ffn_bias_local = small_totals
     grad_gains = grad_gains.at[3].add(gain_cross_key)
     grad_biases = grad_biases.at[5].add(column_sums(grad_text_key_pre))
     grad_biases = grad_biases.at[6].add(column_sums(grad_text_value))
-    attn_in_grads = tuple(
+    attn_grads = tuple(
         jnp.stack(
-            [split_grads[0][q], split_grads[1][q], split_grads[2][q], split_grads[4][q], weight_cross_key[q], weight_cross_value[q]]
+            [
+                split_grads[0][h],
+                split_grads[1][h],
+                split_grads[2][h],
+                split_grads[4][h],
+                weight_cross_key[h],
+                weight_cross_value[h],
+                split_grads[3][h],
+                split_grads[5][h],
+            ]
         )
-        for q in range(4)
-    )
-    attn_out_grads = tuple(jnp.stack([split_grads[3][q], split_grads[5][q]]) for q in range(4))
-    attn_in_final = reduce_split(attn_in_grads, 1, spot)
-    attn_out_final = reduce_split(attn_out_grads, 1, spot)
+        for h in range(2)
+    )
+    attn_final = reduce_half(attn_grads, 1, spot)
+    attn_in_final = attn_final[: 2 * heads_in]
+    attn_out_final = attn_final[2 * heads_in :]
     ffn_in_final = reduce_half(split_grads[6], 0, spot)
-    ffn_out_final = reduce_half(split_grads[7], 0, spot)
+    ffn_out_final = reduce_split(split_grads[7], 0, spot)
     grad_mod, grad_gains, grad_biases, grad_ffn_bias, grad_time = reduce_small(
         grad_mod, grad_gains, grad_biases, grad_ffn_bias_local, grad_time, width, length
     )

time: 1670 us -> 1720 us (1.030)
  other arithmetic: 109 us -> 132 us
    ppermute x8 -> x6, waiting for transfers between devices: 386 us -> 292 us  [swap_y(): return lax.ppermute(tensor, 'y', SWAP)]
    reduce_scatter x2 -> x1, waiting for transfers between devices: 50.9 us -> 122 us  [reduce_split(): lax.psum_scatter(total, 'fsdp', scatter_dimension=scatter_axis, tiled=True)]
    convert_element_type x2 -> x1, other arithmetic: 4.56 us -> 26.5 us  [reduce_half(): chip = (mine + received).astype(jnp.bfloat16)]
    unnamed x14 -> x13, waiting for transfers between devices: 21.9 us -> 36 us
    dot_general x36 -> x22, matrix products: 73.1 us -> 75.9 us  [inner_rows(): lax.dot_general(operand, factor, (((0,), (0,)), ((), ())), preferred_elem...]
  transfers between devices with their start and end apart: 44 -> 38, of which waited for: 23 -> 22; matrix products, arithmetic and copies ran while one was open for 25% -> 27% of each run, Pallas kernels for 0% -> 0%
where the time goes in v8:
time: 1720 us; the launch traced here: 1700 us
  waiting for transfers between devices  1040 us (60%)
  matrix products  297 us (17%)
  local copies, waits for them, and re-layouts  141 us (8%)
  other arithmetic  132 us (8%)
  starting transfers between devices  42.9 us (2%)
  blocking collectives  30.8 us (2%)
  between operations  17.2 us (1%)
    ppermute x6, waiting for transfers between devices, swap_y(): return lax.ppermute(tensor, 'y', SWAP)  292 us
    reduce_scatter x2, waiting for transfers between devices, reduce_half(): lax.psum_scatter(chip, 'fsdp', scatter_dimension=scatter_axis, tiled=True)  232 us
    all_gather x2, waiting for transfers between devices, fetch_split(): own = lax.all_gather(part, 'fsdp', axis=gather_axis, tiled=True)  124 us
    reduce_scatter x1, waiting for transfers between devices, reduce_split(): lax.psum_scatter(total, 'fsdp', scatter_dimension=scatter_axis, tiled=True)  122 us
    all_gather x2, waiting for transfers between devices, fetch_split(): mine = lax.all_gather(part, 'fsdp', axis=gather_axis, tiled=True)  122 us
    dot_general x36, matrix products, outer_cols(): lax.dot_general(operand, factor, (((operand.ndim - 1,), (1,)), ((), ())),...  118 us
    dot_general x36, matrix products, matmul(): return jnp.dot(operand, factor, preferred_element_type=jnp.float32)  81.3 us
    dot_general x22, matrix products, inner_rows(): lax.dot_general(operand, factor, (((0,), (0,)), ((), ())), preferred_elem...  75.9 us
  transfers between devices with their start and end apart: 38, of which 22 were waited for; matrix products, arithmetic and copies ran while one was open for 27% of the time, Pallas kernels for 0%

profile of v8, /device:TPU:0, one launch (start us, length us, event | category | flops | bytes accessed | tf_op | source)
XLA Modules:
  0.0 1702.8 jit_solution(13806931591809677113)
XLA Ops:
  15.7 106.1 %all-gather.7.cloned.1.call-done = bf16[6,1536,384]{2,1,0:T(8,128)(2,1)} async-done(((bf16[6,192,384]{2,1,0:T(8,128)(2,1)}), bf16[6,1536,384]{2,1,0:T(8,128)(2,1)}) %all-gather.7.cloned.1.call-update) | async-done | bytes 7077904 | tf_op jit(solution)/shard_map/all_gather | solution.py:193
  123.4 30.8 %all-gather = bf16[8,192,27]{1,2,0:T(8,128)(2,1)S(1)} all-gather(bf16[1,192,27]{1,2,0:T(8,128)(2,1)S(1)} %maximum_bitcast_fusion), channel_id=1, replica_groups=mesh['y'=2,'core'=2,'fsdp'=8] {'fsdp'}, dimensions={0}, use_global_device_ids=true | all-gather | bytes 93312 | tf_op jit(solution)/shard_map/all_gather | solution.py:228
  156.4 18.4 %all-gather.9.cloned.1.call-done = bf16[2,1536,384]{2,1,0:T(8,128)(2,1)} async-done(((bf16[2,192,384]{2,1,0:T(8,128)(2,1)}), bf16[2,1536,384]{2,1,0:T(8,128)(2,1)}) %all-gather.9.cloned.1.call-update) | async-done | bytes 2359312 | tf_op jit(solution)/shard_map/all_gather | solution.py:193
  176.3 101.1 %collective-permute-done = bf16[6,1536,384]{2,1,0:T(8,128)(2,1)} collective-permute-done((bf16[6,1536,384]{2,1,0:T(8,128)(2,1)}, bf16[6,1536,384]{2,1,0:T(8,128)(2,1)}, u32[]{:S(2)}, u32[]{:S(2)}) %collective-permute-start) | collective-permute-done | bytes 7077920 | tf_op jit(solution)/shard_map/ppermute | solution.py:153
  283.6 42.1 %collective-permute-done.3 = bf16[2,1536,384]{2,1,0:T(8,128)(2,1)} collective-permute-done((bf16[2,1536,384]{2,1,0:T(8,128)(2,1)}, bf16[2,1536,384]{2,1,0:T(8,128)(2,1)}, u32[]{:S(2)}, u32[]{:S(2)}) %collective-permute-start.3) | collective-permute-done | bytes 2359328 | tf_op jit(solution)/shard_map/ppermute | solution.py:153
  389.3 6.1 all-to-all-done.1
  403.0 7.5 all-to-all-done.2
  436.4 121.5 %all-gather.15.cloned.1.call-done = bf16[8960,768]{1,0:T(8,128)(2,1)} async-done(((bf16[1120,768]{1,0:T(8,128)(2,1)}), bf16[8960,768]{1,0:T(8,128)(2,1)}) %all-gather.15.cloned.1.call-update) | async-done | bytes 13762576 | tf_op jit(solution)/shard_map/all_gather | solution.py:189
  574.9 30.5 %all-gather.11.cloned.1.call-done = bf16[512,6144]{0,1:T(8,128)(2,1)} async-done(((bf16[128,6144]{0,1:T(8,128)(2,1)}), bf16[512,6144]{0,1:T(8,128)(2,1)}) %all-gather.11.cloned.1.call-update) | async-done | bytes 6291472 | tf_op jit(solution)/shard_map/all_gather | solution.py:426
  605.3 5.6 fusion.433
  640.5 9.8 fusion.14
  650.3 6.9 multiply_convert_fusion
  660.2 7.8 fusion.6
  670.3 12.5 fusion
  682.8 15.4 convert_reduce_fusion
  698.1 11.1 fusion.8
  709.2 12.0 multiply_reduce_fusion.10
  724.9 9.1 convolution_convert_fusion
  753.4 8.6 copy.207
  791.8 20.4 %all-to-all-done.4 = bf16[2,96,1536]{1,0,2:T(2,128)(2,1)S(1)} async-done(((bf16[2,96,1536]{1,0,2:T(2,128)(2,1)}), bf16[2,96,1536]{1,0,2:T(2,128)(2,1)S(1)}, u32[]{:S(2)}, u32[]{:S(2)}) %all-to-all-start.4) | async-done | bytes 589856 | tf_op jit(solution)/shard_map/all_to_all | solution.py:315
  873.6 6.3 multiply_reduce_fusion.9
  879.9 10.4 add_convert_fusion.1
  946.6 26.5 %add_convert_fusion = bf16[8,1536,768]{2,1,0:T(8,128)(2,1)} fusion(f32[8,1536,768]{2,1,0:T(8,128)} %bitcast_dynamic-update-slice_fusion.2, bf16[8,1536,768]{2,1,0:T(8,128)(2,1)} %collective-permute-done.8), kind=kLoop, calls=%fused_computation | loop fusion | flops 28311552 | bytes 75497472 | tf_op jit(solution)/shard_map/convert_element_type | solution.py:216
  999.9 143.0 %collective-permute-done.16 = bf16[8960,384]{1,0:T(8,128)(2,1)S(1)} collective-permute-done((bf16[8960,384]{1,0:T(8,128)(2,1)S(1)}, bf16[8960,384]{1,0:T(8,128)(2,1)S(1)}, u32[]{:S(2)}, u32[]{:S(2)}) %collective-permute-start.16) | collective-permute-done | bytes 6881312 | tf_op jit(solution)/shard_map/ppermute | solution.py:153
  1142.9 8.1 add_convert_fusion.2
  1196.2 231.9 %reduce-scatter.10.cloned.1.call-done = bf16[8,192,768]{2,1,0:T(8,128)(2,1)} async-done(((bf16[8,1536,768]{2,1,0:T(8,128)(2,1)}), bf16[8,192,768]{2,1,0:T(8,128)(2,1)}) %reduce-scatter.10.cloned.1.call-update) | async-done | bytes 2359312 | tf_op jit(solution)/shard_map/reduce_scatter | solution.py:217
  1436.3 122.1 %reduce-scatter.14.cloned.1.call-done = bf16[1120,384]{1,0:T(8,128)(2,1)} async-done(((bf16[8960,384]{1,0:T(8,128)(2,1)}), bf16[1120,384]{1,0:T(8,128)(2,1)}) %reduce-scatter.14.cloned.1.call-update) | async-done | bytes 860176 | tf_op jit(solution)/shard_map/reduce_scatter | solution.py:206
  1572.9 5.7 collective-permute-done.17
  1588.8 35.8 %reduce-scatter.18.cloned.1.call-done = f32[192,27]{1,0:T(8,128)} async-done(((f32[1536,27]{1,0:T(8,128)}), f32[192,27]{1,0:T(8,128)}) %reduce-scatter.18.cloned.1.call-update) | async-done | bytes 20752
  1630.8 27.3 %all-reduce.12.cloned.1.call-done = f32[23616]{0:T(1024)} async-done(((f32[23616]{0:T(1024)}), f32[23616]{0:T(1024)}) %all-reduce.12.cloned.1.call-update) | async-done | bytes 94480 | tf_op jit(solution)/shard_map/psum | solution.py:243
  1675.6 10.1 fusion.20
  1685.7 7.2 fusion.432
  (782 shorter events, 468.1 us)
Async XLA Ops:
  7.2 114.6 %all-gather.7.cloned.1.call-start = ((), (), s32[]{:S(2)}) async-start(), calls=%async_computation.13 | async-start | bytes 7962624 | tf_op jit(solution)/shard_map/all_gather | solution.py:193
  9.6 165.2 %all-gather.9.cloned.1.call-start = ((), (), s32[]{:S(2)}) async-start(), calls=%async_computation.14 | async-start | bytes 2654208 | tf_op jit(solution)/shard_map/all_gather | solution.py:193
  11.4 372.6 %all-gather.13.cloned.1.call-start = ((), (), s32[]{:S(2)}) async-start(), calls=%async_computation.16 | async-start | bytes 15482880 | tf_op jit(solution)/shard_map/all_gather | solution.py:189
  12.8 545.2 %all-gather.15.cloned.1.call-start = ((), (), s32[]{:S(2)}) async-start(), calls=%async_computation.17 | async-start | bytes 15482880 | tf_op jit(solution)/shard_map/all_gather | solution.py:189
  15.7 589.7 %all-gather.11.cloned.1.call-start = ((), (), s32[]{:S(2)}) async-start(), calls=%async_computation.15 | async-start | bytes 7864320 | tf_op jit(solution)/shard_map/all_gather | solution.py:426
  121.8 155.6 %collective-permute-start = (bf16[6,1536,384]{2,1,0:T(8,128)(2,1)}, bf16[6,1536,384]{2,1,0:T(8,128)(2,1)}, u32[]{:S(2)}, u32[]{:S(2)}) collective-permute-start(bf16[6,1536,384]{2,1,0:T(8,128)(2,1)} %all-gather.7.cloned.1.call-done), channel_id=1, source_target_pairs={{0,16},{16,0},{1,17},{17,1},{2,18},{18,2},{3,19},{19,3},{4,20},{20... | collective-permute-start | bytes 21233672 | tf_op jit(solution)/shard_map/ppermute | solution.py:153
  154.6 189.1 %collective-permute-start.2 = (bf16[6,1536,384]{2,1,0:T(8,128)(2,1)}, bf16[6,1536,384]{2,1,0:T(8,128)(2,1)}, u32[]{:S(2)}, u32[]{:S(2)}) collective-permute-start(bf16[6,1536,384]{2,1,0:T(8,128)(2,1)} %all-gather.7.cloned.1.call-done), channel_id=1, source_target_pairs={{0,8},{8,0},{1,9},{9,1},{2,10},{10,2},{3,11},{11,3},{4,12},{12,4},... | collective-permute-start | bytes 21233672 | tf_op jit(solution)/shard_map/ppermute | solution.py:135
  174.8 150.9 %collective-permute-start.3 = (bf16[2,1536,384]{2,1,0:T(8,128)(2,1)}, bf16[2,1536,384]{2,1,0:T(8,128)(2,1)}, u32[]{:S(2)}, u32[]{:S(2)}) collective-permute-start(bf16[2,1536,384]{2,1,0:T(8,128)(2,1)} %all-gather.9.cloned.1.call-done), channel_id=1, source_target_pairs={{0,16},{16,0},{1,17},{17,1},{2,18},{18,2},{3,19},{19,3},{4,20},{20... | collective-permute-start | bytes 7077896 | tf_op jit(solution)/shard_map/ppermute | solution.py:153
  277.4 78.4 %collective-permute-start.1 = (bf16[6,1536,384]{2,1,0:T(8,128)(2,1)}, bf16[6,1536,384]{2,1,0:T(8,128)(2,1)}, u32[]{:S(2)}, u32[]{:S(2)}) collective-permute-start(bf16[6,1536,384]{2,1,0:T(8,128)(2,1)} %collective-permute-done), channel_id=1, source_target_pairs={{0,8},{8,0},{1,9},{9,1},{2,10},{10,2},{3,11},{11,3},{4,12},{12,4},... | collective-permute-start | bytes 21233672 | tf_op jit(solution)/shard_map/ppermute | solution.py:135
  325.7 232.4 %collective-permute-start.4 = (bf16[2,1536,384]{2,1,0:T(8,128)(2,1)}, bf16[2,1536,384]{2,1,0:T(8,128)(2,1)}, u32[]{:S(2)}, u32[]{:S(2)}) collective-permute-start(bf16[2,1536,384]{2,1,0:T(8,128)(2,1)} %collective-permute-done.3), channel_id=1, source_target_pairs={{0,8},{8,0},{1,9},{9,1},{2,10},{10,2},{3,11},{11,3},{4,12},{12,4},... | collective-permute-start | bytes 7077896 | tf_op jit(solution)/shard_map/ppermute | solution.py:135
  384.0 256.4 %collective-permute-start.6 = (bf16[1536,4480]{1,0:T(8,128)(2,1)}, bf16[1536,4480]{1,0:T(8,128)(2,1)}, u32[]{:S(2)}, u32[]{:S(2)}) collective-permute-start(bf16[1536,4480]{1,0:T(8,128)(2,1)} %all-gather.13.cloned.1.call-done), channel_id=1, source_target_pairs={{0,8},{8,0},{1,9},{9,1},{2,10},{10,2},{3,11},{11,3},{4,12},{12,4},... | collective-permute-start | bytes 41287688 | tf_op jit(solution)/shard_map/ppermute | solution.py:135
  410.5 15.5 all-to-all-start
  414.4 145.6 %collective-permute-start.5 = (bf16[2,1536,384]{2,1,0:T(8,128)(2,1)}, bf16[2,1536,384]{2,1,0:T(8,128)(2,1)}, u32[]{:S(2)}, u32[]{:S(2)}) collective-permute-start(bf16[2,1536,384]{2,1,0:T(8,128)(2,1)} %all-gather.9.cloned.1.call-done), channel_id=1, source_target_pairs={{0,8},{8,0},{1,9},{9,1},{2,10},{10,2},{3,11},{11,3},{4,12},{12,4},... | collective-permute-start | bytes 7077896 | tf_op jit(solution)/shard_map/ppermute | solution.py:135
  432.2 125.8 %all-to-all-start.3 = ((bf16[2,384,384]{2,0,1:T(2,128)(2,1)}), bf16[2,384,384]{2,0,1:T(2,128)(2,1)S(1)}, u32[]{:S(2)}, u32[]{:S(2)}) async-start(bf16[2,384,384]{2,0,1:T(2,128)(2,1)} %copy.157), calls=%async_computation.3 | async-start | bytes 1179648 | tf_op jit(solution)/shard_map/all_to_all | solution.py:279
  435.7 467.5 %reduce-scatter.16.cloned.1.call-start = ((), (), s32[]{:S(2)}) async-start(), calls=%async_computation.22 | async-start | bytes 7864320
  557.9 102.2 %collective-permute-start.7 = (bf16[8960,768]{1,0:T(8,128)(2,1)}, bf16[8960,768]{1,0:T(8,128)(2,1)}, u32[]{:S(2)}, u32[]{:S(2)}) collective-permute-start(bf16[8960,768]{1,0:T(8,128)(2,1)} %all-gather.15.cloned.1.call-done), channel_id=1, source_target_pairs={{0,8},{8,0},{1,9},{9,1},{2,10},{10,2},{3,11},{11,3},{4,12},{12,4},... | collective-permute-start | bytes 41287688 | tf_op jit(solution)/shard_map/ppermute | solution.py:135
  734.0 145.9 %collective-permute-start.11 = (bf16[1536,4480]{1,0:T(8,128)(2,1)}, bf16[1536,4480]{1,0:T(8,128)(2,1)}, u32[]{:S(2)}, u32[]{:S(2)}) collective-permute-start(bf16[1536,4480]{1,0:T(8,128)(2,1)} %convolution_convert_fusion), channel_id=1, source_target_pairs={{0,8},{8,0},{1,9},{9,1},{2,10},{10,2},{3,11},{11,3},{4,12},{12,4},... | collective-permute-start | bytes 41287688 | tf_op jit(solution)/shard_map/ppermute | solution.py:135
  787.8 24.3 %all-to-all-start.4 = ((bf16[2,96,1536]{1,0,2:T(2,128)(2,1)}), bf16[2,96,1536]{1,0,2:T(2,128)(2,1)S(1)}, u32[]{:S(2)}, u32[]{:S(2)}) async-start(bf16[2,96,1536]{1,0,2:T(2,128)(2,1)} %copy.169), calls=%async_computation.4 | async-start | bytes 1572864 | tf_op jit(solution)/shard_map/all_to_all | solution.py:315
  861.4 323.1 %reduce-scatter.12.cloned.1.call-start = ((), (), s32[]{:S(2)}) async-start(), calls=%async_computation.20 | async-start | bytes 15482880 | tf_op jit(solution)/shard_map/reduce_scatter | solution.py:217
  890.4 537.7 %reduce-scatter.10.cloned.1.call-start = ((), (), s32[]{:S(2)}) async-start(), calls=%async_computation.19 | async-start | bytes 21233664 | tf_op jit(solution)/shard_map/reduce_scatter | solution.py:217
  918.1 28.5 %collective-permute-start.8 = (bf16[8,1536,768]{2,1,0:T(8,128)(2,1)}, bf16[8,1536,768]{2,1,0:T(8,128)(2,1)}, u32[]{:S(2)}, u32[]{:S(2)}) collective-permute-start(bf16[8,1536,768]{2,1,0:T(8,128)(2,1)} %fusion.57), channel_id=1, source_target_pairs={{0,8},{8,0},{1,9},{9,1},{2,10},{10,2},{3,11},{11,3},{4,12},{12,4},... | collective-permute-start | bytes 56623112 | tf_op jit(solution)/shard_map/ppermute | solution.py:135
  973.1 585.2 %reduce-scatter.14.cloned.1.call-start = ((), (), s32[]{:S(2)}) async-start(), calls=%async_computation.21 | async-start | bytes 7741440 | tf_op jit(solution)/shard_map/reduce_scatter | solution.py:206
  984.7 15.1 collective-permute-start.14
  992.6 150.3 %collective-permute-start.16 = (bf16[8960,384]{1,0:T(8,128)(2,1)S(1)}, bf16[8960,384]{1,0:T(8,128)(2,1)S(1)}, u32[]{:S(2)}, u32[]{:S(2)}) collective-permute-start(bf16[8960,384]{1,0:T(8,128)(2,1)S(1)} %add_convert_fusion.3), channel_id=1, source_target_pairs={{0,16},{16,0},{1,17},{17,1},{2,18},{18,2},{3,19},{19,3},{4,20},{20... | collective-permute-start | bytes 20643848 | tf_op jit(solution)/shard_map/ppermute | solution.py:153
  1151.1 473.4 %reduce-scatter.18.cloned.1.call-start = ((), (), s32[]{:S(2)}) async-start(), calls=%async_computation.23 | async-start | bytes 884736
  1184.5 375.3 %collective-permute-start.12 = (bf16[192,4480]{1,0:T(8,128)(2,1)}, bf16[192,4480]{1,0:T(8,128)(2,1)}, u32[]{:S(2)}, u32[]{:S(2)}) collective-permute-start(bf16[192,4480]{1,0:T(8,128)(2,1)} %reduce-scatter.12.cloned.1.call-done), channel_id=1, source_target_pairs={{0,16},{16,0},{1,17},{17,1},{2,18},{18,2},{3,19},{19,3},{4,20},{20... | collective-permute-start | bytes 5160968 | tf_op jit(solution)/shard_map/ppermute | solution.py:153
  1428.0 136.0 %collective-permute-start.9 = (bf16[8,192,768]{2,1,0:T(8,128)(2,1)}, bf16[8,192,768]{2,1,0:T(8,128)(2,1)}, u32[]{:S(2)}, u32[]{:S(2)}) collective-permute-start(bf16[8,192,768]{2,1,0:T(8,128)(2,1)} %reduce-scatter.10.cloned.1.call-done), channel_id=1, source_target_pairs={{0,16},{16,0},{1,17},{17,1},{2,18},{18,2},{3,19},{19,3},{4,20},{20... | collective-permute-start | bytes 7077896 | tf_op jit(solution)/shard_map/ppermute | solution.py:153
  1431.1 227.0 %all-reduce.12.cloned.1.call-start = ((), (), s32[]{:S(2)}) async-start(), calls=%async_computation.18 | async-start | bytes 196608 | tf_op jit(solution)/shard_map/psum | solution.py:243
  1558.4 20.2 %collective-permute-start.17 = (bf16[1120,384]{1,0:T(8,128)(2,1)}, bf16[1120,384]{1,0:T(8,128)(2,1)S(1)}, u32[]{:S(2)}, u32[]{:S(2)}) collective-permute-start(bf16[1120,384]{1,0:T(8,128)(2,1)} %reduce-scatter.14.cloned.1.call-done), channel_id=1, source_target_pairs={{0,16},{16,0},{1,17},{17,1},{2,18},{18,2},{3,19},{19,3},{4,20},{20... | collective-permute-start | bytes 2580488 | tf_op jit(solution)/shard_map/ppermute | solution.py:153
  1564.1 106.2 %collective-permute-start.13 = (f32[192,4480]{1,0:T(8,128)}, f32[192,4480]{1,0:T(8,128)}, u32[]{:S(2)}, u32[]{:S(2)}) collective-permute-start(f32[192,4480]{1,0:T(8,128)} %convert_add_fusion.1), channel_id=1, source_target_pairs={{0,8},{8,0},{1,9},{9,1},{2,10},{10,2},{3,11},{11,3},{4,12},{12,4},... | collective-permute-start | bytes 10321928 | tf_op jit(solution)/shard_map/ppermute | solution.py:135
  1568.5 107.1 %collective-permute-start.10 = (f32[8,192,768]{2,1,0:T(8,128)}, f32[8,192,768]{2,1,0:T(8,128)}, u32[]{:S(2)}, u32[]{:S(2)}) collective-permute-start(f32[8,192,768]{2,1,0:T(8,128)} %convert_add_fusion), channel_id=1, source_target_pairs={{0,8},{8,0},{1,9},{9,1},{2,10},{10,2},{3,11},{11,3},{4,12},{12,4},... | collective-permute-start | bytes 14155784 | tf_op jit(solution)/shard_map/ppermute | solution.py:135
  1579.4 86.0 %collective-permute-start.18 = (bf16[1120,768]{1,0:T(8,128)(2,1)S(1)}, bf16[1120,768]{1,0:T(8,128)(2,1)}, u32[]{:S(2)}, u32[]{:S(2)}) collective-permute-start(bf16[1120,768]{1,0:T(8,128)(2,1)S(1)} %fusion.95), channel_id=1, source_target_pairs={{0,8},{8,0},{1,9},{9,1},{2,10},{10,2},{3,11},{11,3},{4,12},{12,4},... | collective-permute-start | bytes 5160968 | tf_op jit(solution)/shard_map/ppermute | solution.py:135
  (198 other events, 2615.3 us)
Sparse Core Ops, SparseCore 0:
  10.8 110.9 all-gather.6
  124.6 50.1 all-gather.8
  177.6 188.9 all-gather.12
  369.2 188.6 all-gather.14
  559.9 45.3 all-gather.10
  762.2 67.2 reduce-scatter.15
  890.5 224.7 reduce-scatter.11
  1119.2 308.8 reduce-scatter.9
  1432.3 126.0 reduce-scatter.13
  1562.1 62.3 reduce-scatter.17
  1627.4 30.7 all-reduce.11

commit v9 on v6

--- a/solution.py
+++ b/solution.py
@@ -195,14 +195,17 @@
     return (own, y_part, swap_core(own), swap_core(y_part))
 
 
-def reduce_split(parts, scatter_axis, spot):
+def reduce_split(parts, scatter_axis, spot, after=None):
     y, core = spot
     own, y_part, core_part, cross_part = parts
     from_core = swap_core(core_part.astype(jnp.bfloat16)).astype(jnp.float32)
     from_cross = swap_core(cross_part.astype(jnp.bfloat16)).astype(jnp.float32)
     chip_own = own + from_core
     chip_y = (y_part + from_cross).astype(jnp.bfloat16)
-    total = (chip_own + swap_y(chip_y).astype(jnp.float32)).astype(jnp.bfloat16)
+    from_y = swap_y(chip_y)
+    if after is not None:
+        from_y, _ = lax.optimization_barrier((from_y, after))
+    total = (chip_own + from_y.astype(jnp.float32)).astype(jnp.bfloat16)
     owned = lax.psum_scatter(total, "fsdp", scatter_dimension=scatter_axis, tiled=True)
     owned_y = swap_y(owned)
     mine = join(owned, owned_y, y)
@@ -433,7 +436,7 @@
     value_grads = [text_grads[1][i] for i in range(clips)]
     pairs = [(rows.reshape(-1, rows.shape[-1]), grad.reshape(-1, grad.shape[-1])) for rows, grad in split]
     split_grads = [
-        split_weight.grad(rows, grad, quarters=index < 6)
+        split_weight.grad(rows, grad, quarters=index != 6)
         for index, (split_weight, (rows, grad)) in enumerate(
             zip(
                 (in_split[0], in_split[1], in_split[2], out_split[0], in_split[3], out_split[1], weights[9], weights[10]),
@@ -462,13 +465,15 @@
         for q in range(4)
     )
     attn_out_grads = tuple(jnp.stack([split_grads[3][q], split_grads[5][q]]) for q in range(4))
-    attn_in_final = reduce_split(attn_in_grads, 1, spot)
-    attn_out_final = reduce_split(attn_out_grads, 1, spot)
-    ffn_in_final = reduce_half(split_grads[6], 0, spot)
-    ffn_out_final = reduce_half(split_grads[7], 0, spot)
+    attn_parts = tuple(jnp.concatenate([a, b]) for a, b in zip(attn_in_grads, attn_out_grads))
     grad_mod, grad_gains, grad_biases, grad_ffn_bias, grad_time = reduce_small(
         grad_mod, grad_gains, grad_biases, grad_ffn_bias_local, grad_time, width, length
     )
+    attn_final = reduce_split(attn_parts, 1, spot, after=grad_gains)
+    attn_in_final = attn_final[: 2 * heads_in]
+    attn_out_final = attn_final[2 * heads_in :]
+    ffn_in_final = reduce_half(split_grads[6], 0, spot)
+    ffn_out_final = reduce_split(split_grads[7], 0, spot, after=attn_parts[0])
     return (
         mixed,
         grad_hidden,

time: 1670 us -> 1680 us (level)
  waiting for transfers between devices: 1030 us -> 987 us
  matrix products: 294 us -> 321 us
    reduce_scatter x2 -> x1, waiting for transfers between devices: 225 us -> 0.02 us  [reduce_half(): lax.psum_scatter(chip, 'fsdp', scatter_dimension=scatter_axis, tiled=True)]
    ppermute x8 -> x7, waiting for transfers between devices: 386 us -> 502 us  [swap_y(): return lax.ppermute(tensor, 'y', SWAP)]
    reduce_scatter x2, waiting for transfers between devices: 50.9 us -> 103 us  [reduce_split(): lax.psum_scatter(total, 'fsdp', scatter_dimension=scatter_axis, tiled=True)]
    unnamed x14 -> x13, waiting for transfers between devices: 21.9 us -> 65 us
    dot_general x36 -> x38, matrix products: 73.1 us -> 103 us  [inner_rows(): lax.dot_general(operand, factor, (((0,), (0,)), ((), ())), preferred_elem...]
    psum x1, waiting for transfers between devices: 27.2 us -> 0.01 us  [reduce_small(): summed = lax.psum(flat, SEQ)]
  transfers between devices with their start and end apart: 44 -> 40, of which waited for: 23 -> 18; matrix products, arithmetic and copies ran while one was open for 25% -> 28% of each run, Pallas kernels for 0% -> 0%
where the time goes in v9:
time: 1680 us; the launch traced here: 1660 us
  waiting for transfers between devices  987 us (59%)
  matrix products  321 us (19%)
  local copies, waits for them, and re-layouts  139 us (8%)
  other arithmetic  123 us (7%)
  starting transfers between devices  42.9 us (3%)
  blocking collectives  30.8 us (2%)
  between operations  17.5 us (1%)
    ppermute x7, waiting for transfers between devices, swap_y(): return lax.ppermute(tensor, 'y', SWAP)  502 us
    all_gather x2, waiting for transfers between devices, fetch_split(): own = lax.all_gather(part, 'fsdp', axis=gather_axis, tiled=True)  124 us
    all_gather x2, waiting for transfers between devices, fetch_split(): mine = lax.all_gather(part, 'fsdp', axis=gather_axis, tiled=True)  121 us
    dot_general x36, matrix products, outer_cols(): lax.dot_general(operand, factor, (((operand.ndim - 1,), (1,)), ((), ())),...  114 us
    reduce_scatter x2, waiting for transfers between devices, reduce_split(): lax.psum_scatter(total, 'fsdp', scatter_dimension=scatter_axis, tiled=True)  103 us
    dot_general x38, matrix products, inner_rows(): lax.dot_general(operand, factor, (((0,), (0,)), ((), ())), preferred_elem...  103 us
    dot_general x36, matrix products, matmul(): return jnp.dot(operand, factor, preferred_element_type=jnp.float32)  81.3 us
    unnamed x13, waiting for transfers between devices  65 us
  transfers between devices with their start and end apart: 40, of which 18 were waited for; matrix products, arithmetic and copies ran while one was open for 28% of the time, Pallas kernels for 0%

profile of v9, /device:TPU:0, one launch (start us, length us, event | category | flops | bytes accessed | tf_op | source)
XLA Modules:
  0.0 1661.7 jit_solution(6650504013794667891)
XLA Ops:
  15.7 106.1 %all-gather.7.cloned.1.call-done = bf16[6,1536,384]{2,1,0:T(8,128)(2,1)} async-done(((bf16[6,192,384]{2,1,0:T(8,128)(2,1)}), bf16[6,1536,384]{2,1,0:T(8,128)(2,1)}) %all-gather.7.cloned.1.call-update) | async-done | bytes 7077904 | tf_op jit(solution)/shard_map/all_gather | solution.py:193
  123.4 30.8 %all-gather = bf16[8,192,27]{1,2,0:T(8,128)(2,1)S(1)} all-gather(bf16[1,192,27]{1,2,0:T(8,128)(2,1)S(1)} %maximum_bitcast_fusion), channel_id=1, replica_groups=mesh['y'=2,'core'=2,'fsdp'=8] {'fsdp'}, dimensions={0}, use_global_device_ids=true | all-gather | bytes 93312 | tf_op jit(solution)/shard_map/all_gather | solution.py:231
  156.4 18.4 %all-gather.9.cloned.1.call-done = bf16[2,1536,384]{2,1,0:T(8,128)(2,1)} async-done(((bf16[2,192,384]{2,1,0:T(8,128)(2,1)}), bf16[2,1536,384]{2,1,0:T(8,128)(2,1)}) %all-gather.9.cloned.1.call-update) | async-done | bytes 2359312 | tf_op jit(solution)/shard_map/all_gather | solution.py:193
  176.3 101.1 %collective-permute-done = bf16[6,1536,384]{2,1,0:T(8,128)(2,1)} collective-permute-done((bf16[6,1536,384]{2,1,0:T(8,128)(2,1)}, bf16[6,1536,384]{2,1,0:T(8,128)(2,1)}, u32[]{:S(2)}, u32[]{:S(2)}) %collective-permute-start) | collective-permute-done | bytes 7077920 | tf_op jit(solution)/shard_map/ppermute | solution.py:153
  283.7 42.0 %collective-permute-done.3 = bf16[2,1536,384]{2,1,0:T(8,128)(2,1)} collective-permute-done((bf16[2,1536,384]{2,1,0:T(8,128)(2,1)}, bf16[2,1536,384]{2,1,0:T(8,128)(2,1)}, u32[]{:S(2)}, u32[]{:S(2)}) %collective-permute-start.3) | collective-permute-done | bytes 2359328 | tf_op jit(solution)/shard_map/ppermute | solution.py:153
  389.4 6.1 all-to-all-done.1
  403.0 7.5 all-to-all-done.2
  436.5 121.4 %all-gather.15.cloned.1.call-done = bf16[8960,768]{1,0:T(8,128)(2,1)} async-done(((bf16[1120,768]{1,0:T(8,128)(2,1)}), bf16[8960,768]{1,0:T(8,128)(2,1)}) %all-gather.15.cloned.1.call-update) | async-done | bytes 13762576 | tf_op jit(solution)/shard_map/all_gather | solution.py:189
  574.9 30.5 %all-gather.11.cloned.1.call-done = bf16[512,6144]{0,1:T(8,128)(2,1)} async-done(((bf16[128,6144]{0,1:T(8,128)(2,1)}), bf16[512,6144]{0,1:T(8,128)(2,1)}) %all-gather.11.cloned.1.call-update) | async-done | bytes 6291472 | tf_op jit(solution)/shard_map/all_gather | solution.py:429
  605.3 5.6 fusion.488
  640.5 9.8 fusion.14
  650.3 6.9 multiply_convert_fusion
  660.2 7.8 fusion.6
  670.3 12.5 fusion
  682.8 15.4 convert_reduce_fusion
  698.2 11.1 fusion.8
  709.3 12.0 multiply_reduce_fusion.10
  747.2 8.6 copy.227
  756.9 10.6 convolution_convert_fusion
  791.1 20.4 %all-to-all-done.4 = bf16[2,96,1536]{1,0,2:T(2,128)(2,1)S(1)} async-done(((bf16[2,96,1536]{1,0,2:T(2,128)(2,1)}), bf16[2,96,1536]{1,0,2:T(2,128)(2,1)S(1)}, u32[]{:S(2)}, u32[]{:S(2)}) %all-to-all-start.4) | async-done | bytes 589856 | tf_op jit(solution)/shard_map/all_to_all | solution.py:318
  932.9 64.8 %reduce-scatter.18.cloned.1.call-done = f32[192,27]{1,0:T(8,128)} async-done(((f32[1536,27]{1,0:T(8,128)}), f32[192,27]{1,0:T(8,128)}) %reduce-scatter.18.cloned.1.call-update) | async-done | bytes 20752
  999.5 10.5 add_convert_fusion
  1034.2 9.7 add_convert_fusion.4
  1095.5 98.7 %collective-permute-done.18 = bf16[8960,384]{1,0:T(8,128)(2,1)S(1)} collective-permute-done((bf16[8960,384]{1,0:T(8,128)(2,1)}, bf16[8960,384]{1,0:T(8,128)(2,1)S(1)}, u32[]{:S(2)}, u32[]{:S(2)}) %collective-permute-start.18) | collective-permute-done | bytes 6881312 | tf_op jit(solution)/shard_map/ppermute | solution.py:153
  1194.2 8.2 add_convert_fusion.3
  1205.2 13.5 add_convert_fusion.2
  1223.0 199.9 %collective-permute-done.10 = bf16[8,1536,384]{2,1,0:T(8,128)(2,1)} collective-permute-done((bf16[8,1536,384]{2,1,0:T(8,128)(2,1)}, bf16[8,1536,384]{2,1,0:T(8,128)(2,1)}, u32[]{:S(2)}, u32[]{:S(2)}) %collective-permute-start.10) | collective-permute-done | bytes 9437216 | tf_op jit(solution)/shard_map/ppermute | solution.py:153
  1422.9 16.5 add_convert_fusion.1
  1446.7 33.5 %collective-permute-done.14 = bf16[192,4480]{1,0:T(8,128)(2,1)} collective-permute-done((bf16[192,4480]{1,0:T(8,128)(2,1)}, bf16[192,4480]{1,0:T(8,128)(2,1)}, u32[]{:S(2)}, u32[]{:S(2)}) %collective-permute-start.14) | collective-permute-done | bytes 1720352 | tf_op jit(solution)/shard_map/ppermute | solution.py:153
  1487.4 8.3 collective-permute-done.19
  1497.7 103.3 %reduce-scatter.10.cloned.1.call-done = bf16[8,192,384]{2,1,0:T(8,128)(2,1)} async-done(((bf16[8,1536,384]{2,1,0:T(8,128)(2,1)}), bf16[8,192,384]{2,1,0:T(8,128)(2,1)}) %reduce-scatter.10.cloned.1.call-update) | async-done | bytes 1179664 | tf_op jit(solution)/shard_map/reduce_scatter | solution.py:209
  1610.6 18.3 %collective-permute-done.11 = bf16[8,192,384]{2,1,0:T(8,128)(2,1)S(1)} collective-permute-done((bf16[8,192,384]{2,1,0:T(8,128)(2,1)}, bf16[8,192,384]{2,1,0:T(8,128)(2,1)S(1)}, u32[]{:S(2)}, u32[]{:S(2)}) %collective-permute-start.11) | collective-permute-done | bytes 1179680 | tf_op jit(solution)/shard_map/ppermute | solution.py:153
  (796 shorter events, 474.3 us)
Async XLA Ops:
  7.2 114.6 %all-gather.7.cloned.1.call-start = ((), (), s32[]{:S(2)}) async-start(), calls=%async_computation.13 | async-start | bytes 7962624 | tf_op jit(solution)/shard_map/all_gather | solution.py:193
  9.6 165.2 %all-gather.9.cloned.1.call-start = ((), (), s32[]{:S(2)}) async-start(), calls=%async_computation.14 | async-start | bytes 2654208 | tf_op jit(solution)/shard_map/all_gather | solution.py:193
  11.4 372.7 %all-gather.13.cloned.1.call-start = ((), (), s32[]{:S(2)}) async-start(), calls=%async_computation.16 | async-start | bytes 15482880 | tf_op jit(solution)/shard_map/all_gather | solution.py:189
  12.8 545.2 %all-gather.15.cloned.1.call-start = ((), (), s32[]{:S(2)}) async-start(), calls=%async_computation.17 | async-start | bytes 15482880 | tf_op jit(solution)/shard_map/all_gather | solution.py:189
  15.7 589.7 %all-gather.11.cloned.1.call-start = ((), (), s32[]{:S(2)}) async-start(), calls=%async_computation.15 | async-start | bytes 7864320 | tf_op jit(solution)/shard_map/all_gather | solution.py:429
  121.8 155.6 %collective-permute-start = (bf16[6,1536,384]{2,1,0:T(8,128)(2,1)}, bf16[6,1536,384]{2,1,0:T(8,128)(2,1)}, u32[]{:S(2)}, u32[]{:S(2)}) collective-permute-start(bf16[6,1536,384]{2,1,0:T(8,128)(2,1)} %all-gather.7.cloned.1.call-done), channel_id=1, source_target_pairs={{0,16},{16,0},{1,17},{17,1},{2,18},{18,2},{3,19},{19,3},{4,20},{20... | collective-permute-start | bytes 21233672 | tf_op jit(solution)/shard_map/ppermute | solution.py:153
  154.6 189.2 %collective-permute-start.2 = (bf16[6,1536,384]{2,1,0:T(8,128)(2,1)}, bf16[6,1536,384]{2,1,0:T(8,128)(2,1)}, u32[]{:S(2)}, u32[]{:S(2)}) collective-permute-start(bf16[6,1536,384]{2,1,0:T(8,128)(2,1)} %all-gather.7.cloned.1.call-done), channel_id=1, source_target_pairs={{0,8},{8,0},{1,9},{9,1},{2,10},{10,2},{3,11},{11,3},{4,12},{12,4},... | collective-permute-start | bytes 21233672 | tf_op jit(solution)/shard_map/ppermute | solution.py:135
  174.8 150.9 %collective-permute-start.3 = (bf16[2,1536,384]{2,1,0:T(8,128)(2,1)}, bf16[2,1536,384]{2,1,0:T(8,128)(2,1)}, u32[]{:S(2)}, u32[]{:S(2)}) collective-permute-start(bf16[2,1536,384]{2,1,0:T(8,128)(2,1)} %all-gather.9.cloned.1.call-done), channel_id=1, source_target_pairs={{0,16},{16,0},{1,17},{17,1},{2,18},{18,2},{3,19},{19,3},{4,20},{20... | collective-permute-start | bytes 7077896 | tf_op jit(solution)/shard_map/ppermute | solution.py:153
  277.4 78.4 %collective-permute-start.1 = (bf16[6,1536,384]{2,1,0:T(8,128)(2,1)}, bf16[6,1536,384]{2,1,0:T(8,128)(2,1)}, u32[]{:S(2)}, u32[]{:S(2)}) collective-permute-start(bf16[6,1536,384]{2,1,0:T(8,128)(2,1)} %collective-permute-done), channel_id=1, source_target_pairs={{0,8},{8,0},{1,9},{9,1},{2,10},{10,2},{3,11},{11,3},{4,12},{12,4},... | collective-permute-start | bytes 21233672 | tf_op jit(solution)/shard_map/ppermute | solution.py:135
  325.7 232.4 %collective-permute-start.4 = (bf16[2,1536,384]{2,1,0:T(8,128)(2,1)}, bf16[2,1536,384]{2,1,0:T(8,128)(2,1)}, u32[]{:S(2)}, u32[]{:S(2)}) collective-permute-start(bf16[2,1536,384]{2,1,0:T(8,128)(2,1)} %collective-permute-done.3), channel_id=1, source_target_pairs={{0,8},{8,0},{1,9},{9,1},{2,10},{10,2},{3,11},{11,3},{4,12},{12,4},... | collective-permute-start | bytes 7077896 | tf_op jit(solution)/shard_map/ppermute | solution.py:135
  384.1 256.4 %collective-permute-start.6 = (bf16[1536,4480]{1,0:T(8,128)(2,1)}, bf16[1536,4480]{1,0:T(8,128)(2,1)}, u32[]{:S(2)}, u32[]{:S(2)}) collective-permute-start(bf16[1536,4480]{1,0:T(8,128)(2,1)} %all-gather.13.cloned.1.call-done), channel_id=1, source_target_pairs={{0,8},{8,0},{1,9},{9,1},{2,10},{10,2},{3,11},{11,3},{4,12},{12,4},... | collective-permute-start | bytes 41287688 | tf_op jit(solution)/shard_map/ppermute | solution.py:135
  414.5 145.5 %collective-permute-start.5 = (bf16[2,1536,384]{2,1,0:T(8,128)(2,1)}, bf16[2,1536,384]{2,1,0:T(8,128)(2,1)}, u32[]{:S(2)}, u32[]{:S(2)}) collective-permute-start(bf16[2,1536,384]{2,1,0:T(8,128)(2,1)} %all-gather.9.cloned.1.call-done), channel_id=1, source_target_pairs={{0,8},{8,0},{1,9},{9,1},{2,10},{10,2},{3,11},{11,3},{4,12},{12,4},... | collective-permute-start | bytes 7077896 | tf_op jit(solution)/shard_map/ppermute | solution.py:135
  432.2 125.7 %all-to-all-start.3 = ((bf16[2,384,384]{2,0,1:T(2,128)(2,1)}), bf16[2,384,384]{2,0,1:T(2,128)(2,1)S(1)}, u32[]{:S(2)}, u32[]{:S(2)}) async-start(bf16[2,384,384]{2,0,1:T(2,128)(2,1)} %copy.169), calls=%async_computation.3 | async-start | bytes 1179648 | tf_op jit(solution)/shard_map/all_to_all | solution.py:282
  435.7 488.7 %reduce-scatter.16.cloned.1.call-start = ((), (), s32[]{:S(2)}) async-start(), calls=%async_computation.22 | async-start | bytes 7864320
  558.0 102.2 %collective-permute-start.7 = (bf16[8960,768]{1,0:T(8,128)(2,1)}, bf16[8960,768]{1,0:T(8,128)(2,1)}, u32[]{:S(2)}, u32[]{:S(2)}) collective-permute-start(bf16[8960,768]{1,0:T(8,128)(2,1)} %all-gather.15.cloned.1.call-done), channel_id=1, source_target_pairs={{0,8},{8,0},{1,9},{9,1},{2,10},{10,2},{3,11},{11,3},{4,12},{12,4},... | collective-permute-start | bytes 41287688 | tf_op jit(solution)/shard_map/ppermute | solution.py:135
  767.5 232.0 %collective-permute-start.13 = (bf16[1536,4480]{1,0:T(8,128)(2,1)}, bf16[1536,4480]{1,0:T(8,128)(2,1)}, u32[]{:S(2)}, u32[]{:S(2)}) collective-permute-start(bf16[1536,4480]{1,0:T(8,128)(2,1)} %convolution_convert_fusion), channel_id=1, source_target_pairs={{0,8},{8,0},{1,9},{9,1},{2,10},{10,2},{3,11},{11,3},{4,12},{12,4},... | collective-permute-start | bytes 41287688 | tf_op jit(solution)/shard_map/ppermute | solution.py:135
  830.5 30.6 %all-to-all-start.5 = ((bf16[2,384,384]{2,0,1:T(2,128)(2,1)}), bf16[2,384,384]{2,0,1:T(2,128)(2,1)}, u32[]{:S(2)}, u32[]{:S(2)}) async-start(bf16[2,384,384]{2,0,1:T(2,128)(2,1)} %copy.187), calls=%async_computation.5 | async-start | bytes 1179648 | tf_op jit(solution)/shard_map/all_to_all | solution.py:323
  879.0 118.7 %reduce-scatter.18.cloned.1.call-start = ((), (), s32[]{:S(2)}) async-start(), calls=%async_computation.23 | async-start | bytes 884736
  932.8 288.8 %all-reduce.12.cloned.1.call-start = ((), (), s32[]{:S(2)}) async-start(), calls=%async_computation.18 | async-start | bytes 196608 | tf_op jit(solution)/shard_map/psum | solution.py:246
  999.5 439.9 %reduce-scatter.12.cloned.1.call-start = ((), (), s32[]{:S(2)}) async-start(), calls=%async_computation.20 | async-start | bytes 15482880 | tf_op jit(solution)/shard_map/reduce_scatter | solution.py:220
  1010.1 435.7 %reduce-scatter.14.cloned.1.call-start = ((), (), s32[]{:S(2)}) async-start(), calls=%async_computation.21 | async-start | bytes 7741440 | tf_op jit(solution)/shard_map/reduce_scatter | solution.py:209
  1023.0 171.2 %collective-permute-start.16 = (bf16[8960,384]{1,0:T(8,128)(2,1)}, bf16[8960,384]{1,0:T(8,128)(2,1)}, u32[]{:S(2)}, u32[]{:S(2)}) collective-permute-start(bf16[8960,384]{1,0:T(8,128)(2,1)} %convolution_convert_fusion.2), channel_id=1, source_target_pairs={{0,8},{8,0},{1,9},{9,1},{2,10},{10,2},{3,11},{11,3},{4,12},{12,4},... | collective-permute-start | bytes 20643848 | tf_op jit(solution)/shard_map/ppermute | solution.py:135
  1043.9 150.3 %collective-permute-start.18 = (bf16[8960,384]{1,0:T(8,128)(2,1)}, bf16[8960,384]{1,0:T(8,128)(2,1)S(1)}, u32[]{:S(2)}, u32[]{:S(2)}) collective-permute-start(bf16[8960,384]{1,0:T(8,128)(2,1)} %add_convert_fusion.4), channel_id=1, source_target_pairs={{0,16},{16,0},{1,17},{17,1},{2,18},{18,2},{3,19},{19,3},{4,20},{20... | collective-permute-start | bytes 20643848 | tf_op jit(solution)/shard_map/ppermute | solution.py:153
  1052.0 153.2 %collective-permute-start.9 = (bf16[8,1536,384]{2,1,0:T(8,128)(2,1)}, bf16[8,1536,384]{2,1,0:T(8,128)(2,1)}, u32[]{:S(2)}, u32[]{:S(2)}) collective-permute-start(bf16[8,1536,384]{2,1,0:T(8,128)(2,1)} %fusion.101), channel_id=1, source_target_pairs={{0,8},{8,0},{1,9},{9,1},{2,10},{10,2},{3,11},{11,3},{4,12},{12,4},... | collective-permute-start | bytes 28311560 | tf_op jit(solution)/shard_map/ppermute | solution.py:135
  1202.4 398.6 %reduce-scatter.10.cloned.1.call-start = ((), (), s32[]{:S(2)}) async-start(), calls=%async_computation.19 | async-start | bytes 10616832 | tf_op jit(solution)/shard_map/reduce_scatter | solution.py:209
  1218.8 204.1 %collective-permute-start.10 = (bf16[8,1536,384]{2,1,0:T(8,128)(2,1)}, bf16[8,1536,384]{2,1,0:T(8,128)(2,1)}, u32[]{:S(2)}, u32[]{:S(2)}) collective-permute-start(bf16[8,1536,384]{2,1,0:T(8,128)(2,1)} %add_convert_fusion.2), channel_id=1, source_target_pairs={{0,16},{16,0},{1,17},{17,1},{2,18},{18,2},{3,19},{19,3},{4,20},{20... | collective-permute-start | bytes 28311560 | tf_op jit(solution)/shard_map/ppermute | solution.py:153
  1221.6 201.3 %collective-permute-start.8 = (bf16[8,1536,384]{2,1,0:T(8,128)(2,1)}, bf16[8,1536,384]{2,1,0:T(8,128)(2,1)}, u32[]{:S(2)}, u32[]{:S(2)}) collective-permute-start(bf16[8,1536,384]{2,1,0:T(8,128)(2,1)} %fusion.89), channel_id=1, source_target_pairs={{0,8},{8,0},{1,9},{9,1},{2,10},{10,2},{3,11},{11,3},{4,12},{12,4},... | collective-permute-start | bytes 28311560 | tf_op jit(solution)/shard_map/ppermute | solution.py:135
  1439.4 40.8 %collective-permute-start.14 = (bf16[192,4480]{1,0:T(8,128)(2,1)}, bf16[192,4480]{1,0:T(8,128)(2,1)}, u32[]{:S(2)}, u32[]{:S(2)}) collective-permute-start(bf16[192,4480]{1,0:T(8,128)(2,1)} %reduce-scatter.12.cloned.1.call-done), channel_id=1, source_target_pairs={{0,16},{16,0},{1,17},{17,1},{2,18},{18,2},{3,19},{19,3},{4,20},{20... | collective-permute-start | bytes 5160968 | tf_op jit(solution)/shard_map/ppermute | solution.py:153
  1445.7 50.0 %collective-permute-start.19 = (bf16[1120,384]{1,0:T(8,128)(2,1)}, bf16[1120,384]{1,0:T(8,128)(2,1)S(1)}, u32[]{:S(2)}, u32[]{:S(2)}) collective-permute-start(bf16[1120,384]{1,0:T(8,128)(2,1)} %reduce-scatter.14.cloned.1.call-done), channel_id=1, source_target_pairs={{0,16},{16,0},{1,17},{17,1},{2,18},{18,2},{3,19},{19,3},{4,20},{20... | collective-permute-start | bytes 2580488 | tf_op jit(solution)/shard_map/ppermute | solution.py:153
  1484.3 156.9 %collective-permute-start.15 = (f32[192,4480]{1,0:T(8,128)}, f32[192,4480]{1,0:T(8,128)}, u32[]{:S(2)}, u32[]{:S(2)}) collective-permute-start(f32[192,4480]{1,0:T(8,128)} %convert_add_fusion), channel_id=1, source_target_pairs={{0,8},{8,0},{1,9},{9,1},{2,10},{10,2},{3,11},{11,3},{4,12},{12,4},... | collective-permute-start | bytes 10321928 | tf_op jit(solution)/shard_map/ppermute | solution.py:135
  1497.7 138.4 %collective-permute-start.20 = (bf16[1120,768]{1,0:T(8,128)(2,1)}, bf16[1120,768]{1,0:T(8,128)(2,1)}, u32[]{:S(2)}, u32[]{:S(2)}) collective-permute-start(bf16[1120,768]{1,0:T(8,128)(2,1)} %fusion.130), channel_id=1, source_target_pairs={{0,8},{8,0},{1,9},{9,1},{2,10},{10,2},{3,11},{11,3},{4,12},{12,4},... | collective-permute-start | bytes 5160968 | tf_op jit(solution)/shard_map/ppermute | solution.py:135
  1601.1 27.8 %collective-permute-start.11 = (bf16[8,192,384]{2,1,0:T(8,128)(2,1)}, bf16[8,192,384]{2,1,0:T(8,128)(2,1)S(1)}, u32[]{:S(2)}, u32[]{:S(2)}) collective-permute-start(bf16[8,192,384]{2,1,0:T(8,128)(2,1)} %reduce-scatter.10.cloned.1.call-done), channel_id=1, source_target_pairs={{0,16},{16,0},{1,17},{17,1},{2,18},{18,2},{3,19},{19,3},{4,20},{20... | collective-permute-start | bytes 3538952 | tf_op jit(solution)/shard_map/ppermute | solution.py:153
  (197 other events, 2171.6 us)
Sparse Core Ops, SparseCore 0:
  10.8 110.9 all-gather.6
  124.6 50.1 all-gather.8
  177.6 188.9 all-gather.12
  369.2 188.6 all-gather.14
  559.9 45.3 all-gather.10
  755.9 67.2 reduce-scatter.15
  932.9 64.6 reduce-scatter.17
  1000.0 30.7 all-reduce.11
  1034.3 223.9 reduce-scatter.11
  1262.4 126.0 reduce-scatter.13
  1439.5 161.4 reduce-scatter.9

commit v10 on v6

--- a/solution.py
+++ b/solution.py
@@ -433,7 +433,7 @@
     value_grads = [text_grads[1][i] for i in range(clips)]
     pairs = [(rows.reshape(-1, rows.shape[-1]), grad.reshape(-1, grad.shape[-1])) for rows, grad in split]
     split_grads = [
-        split_weight.grad(rows, grad, quarters=index < 6)
+        split_weight.grad(rows, grad, quarters=index != 6)
         for index, (split_weight, (rows, grad)) in enumerate(
             zip(
                 (in_split[0], in_split[1], in_split[2], out_split[0], in_split[3], out_split[1], weights[9], weights[10]),
@@ -462,10 +462,13 @@
         for q in range(4)
     )
     attn_out_grads = tuple(jnp.stack([split_grads[3][q], split_grads[5][q]]) for q in range(4))
-    attn_in_final = reduce_split(attn_in_grads, 1, spot)
-    attn_out_final = reduce_split(attn_out_grads, 1, spot)
+    attn_final = reduce_split(
+        tuple(jnp.concatenate([a, b]) for a, b in zip(attn_in_grads, attn_out_grads)), 1, spot
+    )
+    attn_in_final = attn_final[: 2 * heads_in]
+    attn_out_final = attn_final[2 * heads_in :]
     ffn_in_final = reduce_half(split_grads[6], 0, spot)
-    ffn_out_final = reduce_half(split_grads[7], 0, spot)
+    ffn_out_final = reduce_split(split_grads[7], 0, spot)
     grad_mod, grad_gains, grad_biases, grad_ffn_bias, grad_time = reduce_small(
         grad_mod, grad_gains, grad_biases, grad_ffn_bias_local, grad_time, width, length
     )

time: 1670 us -> 1620 us (0.970)
  waiting for transfers between devices: 1030 us -> 944 us
  matrix products: 294 us -> 320 us
    reduce_scatter x2 -> x1, waiting for transfers between devices: 225 us -> 0.02 us  [reduce_half(): lax.psum_scatter(chip, 'fsdp', scatter_dimension=scatter_axis, tiled=True)]
    ppermute x8 -> x7, waiting for transfers between devices: 386 us -> 481 us  [swap_y(): return lax.ppermute(tensor, 'y', SWAP)]
    unnamed x14 -> x13, waiting for transfers between devices: 21.9 us -> 55.5 us
    dot_general x36 -> x38, matrix products: 73.1 us -> 101 us  [inner_rows(): lax.dot_general(operand, factor, (((0,), (0,)), ((), ())), preferred_elem...]
    reduce_scatter x2, waiting for transfers between devices: 50.9 us -> 75.6 us  [reduce_split(): lax.psum_scatter(total, 'fsdp', scatter_dimension=scatter_axis, tiled=True)]
    unnamed x385 -> x403, local copies, waits for them, and re-layouts: 30.7 us -> 35.8 us
  transfers between devices with their start and end apart: 44 -> 40, of which waited for: 23 -> 18; matrix products, arithmetic and copies ran while one was open for 25% -> 29% of each run, Pallas kernels for 0% -> 0%
where the time goes in v10:
time: 1620 us; the launch traced here: 1600 us
  waiting for transfers between devices  944 us (58%)
  matrix products  320 us (20%)
  local copies, waits for them, and re-layouts  127 us (8%)
  other arithmetic  117 us (7%)
  starting transfers between devices  45.5 us (3%)
  blocking collectives  30.8 us (2%)
  between operations  17.9 us (1%)
    ppermute x7, waiting for transfers between devices, swap_y(): return lax.ppermute(tensor, 'y', SWAP)  481 us
    all_gather x2, waiting for transfers between devices, fetch_split(): own = lax.all_gather(part, 'fsdp', axis=gather_axis, tiled=True)  124 us
    all_gather x2, waiting for transfers between devices, fetch_split(): mine = lax.all_gather(part, 'fsdp', axis=gather_axis, tiled=True)  120 us
    dot_general x36, matrix products, outer_cols(): lax.dot_general(operand, factor, (((operand.ndim - 1,), (1,)), ((), ())),...  119 us
    dot_general x38, matrix products, inner_rows(): lax.dot_general(operand, factor, (((0,), (0,)), ((), ())), preferred_elem...  101 us
    dot_general x36, matrix products, matmul(): return jnp.dot(operand, factor, preferred_element_type=jnp.float32)  78.2 us
    reduce_scatter x2, waiting for transfers between devices, reduce_split(): lax.psum_scatter(total, 'fsdp', scatter_dimension=scatter_axis, tiled=True)  75.6 us
    unnamed x13, waiting for transfers between devices  55.5 us
  transfers between devices with their start and end apart: 40, of which 18 were waited for; matrix products, arithmetic and copies ran while one was open for 29% of the time, Pallas kernels for 0%

profile of v10, /device:TPU:0, one launch (start us, length us, event | category | flops | bytes accessed | tf_op | source)
XLA Modules:
  0.0 1602.5 jit_solution(2112738797691936656)
XLA Ops:
  15.7 106.1 %all-gather.7.cloned.1.call-done = bf16[6,1536,384]{2,1,0:T(8,128)(2,1)} async-done(((bf16[6,192,384]{2,1,0:T(8,128)(2,1)}), bf16[6,1536,384]{2,1,0:T(8,128)(2,1)}) %all-gather.7.cloned.1.call-update) | async-done | bytes 7077904 | tf_op jit(solution)/shard_map/all_gather | solution.py:193
  123.4 30.8 %all-gather = bf16[8,192,27]{1,2,0:T(8,128)(2,1)S(1)} all-gather(bf16[1,192,27]{1,2,0:T(8,128)(2,1)S(1)} %maximum_bitcast_fusion), channel_id=1, replica_groups=mesh['y'=2,'core'=2,'fsdp'=8] {'fsdp'}, dimensions={0}, use_global_device_ids=true | all-gather | bytes 93312 | tf_op jit(solution)/shard_map/all_gather | solution.py:228
  156.4 18.4 %all-gather.9.cloned.1.call-done = bf16[2,1536,384]{2,1,0:T(8,128)(2,1)} async-done(((bf16[2,192,384]{2,1,0:T(8,128)(2,1)}), bf16[2,1536,384]{2,1,0:T(8,128)(2,1)}) %all-gather.9.cloned.1.call-update) | async-done | bytes 2359312 | tf_op jit(solution)/shard_map/all_gather | solution.py:193
  176.3 101.1 %collective-permute-done = bf16[6,1536,384]{2,1,0:T(8,128)(2,1)} collective-permute-done((bf16[6,1536,384]{2,1,0:T(8,128)(2,1)}, bf16[6,1536,384]{2,1,0:T(8,128)(2,1)}, u32[]{:S(2)}, u32[]{:S(2)}) %collective-permute-start) | collective-permute-done | bytes 7077920 | tf_op jit(solution)/shard_map/ppermute | solution.py:153
  284.2 41.5 %collective-permute-done.3 = bf16[2,1536,384]{2,1,0:T(8,128)(2,1)} collective-permute-done((bf16[2,1536,384]{2,1,0:T(8,128)(2,1)}, bf16[2,1536,384]{2,1,0:T(8,128)(2,1)}, u32[]{:S(2)}, u32[]{:S(2)}) %collective-permute-start.3) | collective-permute-done | bytes 2359328 | tf_op jit(solution)/shard_map/ppermute | solution.py:153
  402.9 7.5 all-to-all-done.2
  418.8 7.9 all-to-all-done
  438.2 119.8 %all-gather.15.cloned.1.call-done = bf16[8960,768]{1,0:T(8,128)(2,1)} async-done(((bf16[1120,768]{1,0:T(8,128)(2,1)}), bf16[8960,768]{1,0:T(8,128)(2,1)}) %all-gather.15.cloned.1.call-update) | async-done | bytes 13762576 | tf_op jit(solution)/shard_map/all_gather | solution.py:189
  574.9 30.5 %all-gather.11.cloned.1.call-done = bf16[512,6144]{0,1:T(8,128)(2,1)} async-done(((bf16[128,6144]{0,1:T(8,128)(2,1)}), bf16[512,6144]{0,1:T(8,128)(2,1)}) %all-gather.11.cloned.1.call-update) | async-done | bytes 6291472 | tf_op jit(solution)/shard_map/all_gather | solution.py:426
  640.2 6.6 fusion.14
  655.3 7.8 fusion.6
  665.4 12.5 fusion
  677.9 15.1 convert_reduce_fusion
  693.0 11.1 fusion.8
  704.1 12.4 multiply_reduce_fusion.10
  719.8 8.9 convolution_convert_fusion
  748.1 8.7 copy.227
  757.3 15.2 add_convert_fusion
  772.6 7.1 convolution_convert_fusion.1
  812.8 9.8 all-to-all-done.4
  844.6 6.7 convolution_convert_fusion.2
  897.3 12.0 add_convert_fusion.4
  954.2 106.3 %collective-permute-done.18 = bf16[8960,384]{1,0:T(8,128)(2,1)} collective-permute-done((bf16[8960,384]{1,0:T(8,128)(2,1)}, bf16[8960,384]{1,0:T(8,128)(2,1)}, u32[]{:S(2)}, u32[]{:S(2)}) %collective-permute-start.18) | collective-permute-done | bytes 6881312 | tf_op jit(solution)/shard_map/ppermute | solution.py:153
  1060.6 9.3 add_convert_fusion.3
  1075.7 14.4 add_convert_fusion.2
  1101.0 194.6 %collective-permute-done.10 = bf16[8,1536,384]{2,1,0:T(8,128)(2,1)} collective-permute-done((bf16[8,1536,384]{2,1,0:T(8,128)(2,1)}, bf16[8,1536,384]{2,1,0:T(8,128)(2,1)}, u32[]{:S(2)}, u32[]{:S(2)}) %collective-permute-start.10) | collective-permute-done | bytes 9437216 | tf_op jit(solution)/shard_map/ppermute | solution.py:153
  1295.6 10.7 add_convert_fusion.1
  1347.1 27.9 %collective-permute-done.14 = bf16[192,4480]{1,0:T(8,128)(2,1)} collective-permute-done((bf16[192,4480]{1,0:T(8,128)(2,1)}, bf16[192,4480]{1,0:T(8,128)(2,1)}, u32[]{:S(2)}, u32[]{:S(2)}) %collective-permute-start.14) | collective-permute-done | bytes 1720352 | tf_op jit(solution)/shard_map/ppermute | solution.py:153
  1382.3 9.7 collective-permute-done.19
  1394.0 75.6 %reduce-scatter.10.cloned.1.call-done = bf16[8,192,384]{2,1,0:T(8,128)(2,1)} async-done(((bf16[8,1536,384]{2,1,0:T(8,128)(2,1)}), bf16[8,192,384]{2,1,0:T(8,128)(2,1)}) %reduce-scatter.10.cloned.1.call-update) | async-done | bytes 1179664 | tf_op jit(solution)/shard_map/reduce_scatter | solution.py:206
  1480.4 55.3 %reduce-scatter.18.cloned.1.call-done = f32[192,27]{1,0:T(8,128)} async-done(((f32[1536,27]{1,0:T(8,128)}), f32[192,27]{1,0:T(8,128)}) %reduce-scatter.18.cloned.1.call-update) | async-done | bytes 20752
  1543.6 25.7 %all-reduce.12.cloned.1.call-done = f32[23616]{0:T(1024)} async-done(((f32[23616]{0:T(1024)}), f32[23616]{0:T(1024)}) %all-reduce.12.cloned.1.call-update) | async-done | bytes 94480 | tf_op jit(solution)/shard_map/psum | solution.py:243
  (813 shorter events, 457.6 us)
Async XLA Ops:
  7.2 114.6 %all-gather.7.cloned.1.call-start = ((), (), s32[]{:S(2)}) async-start(), calls=%async_computation.13 | async-start | bytes 7962624 | tf_op jit(solution)/shard_map/all_gather | solution.py:193
  9.6 165.2 %all-gather.9.cloned.1.call-start = ((), (), s32[]{:S(2)}) async-start(), calls=%async_computation.14 | async-start | bytes 2654208 | tf_op jit(solution)/shard_map/all_gather | solution.py:193
  11.4 372.6 %all-gather.13.cloned.1.call-start = ((), (), s32[]{:S(2)}) async-start(), calls=%async_computation.16 | async-start | bytes 15482880 | tf_op jit(solution)/shard_map/all_gather | solution.py:189
  12.8 545.2 %all-gather.15.cloned.1.call-start = ((), (), s32[]{:S(2)}) async-start(), calls=%async_computation.17 | async-start | bytes 15482880 | tf_op jit(solution)/shard_map/all_gather | solution.py:189
  15.7 589.7 %all-gather.11.cloned.1.call-start = ((), (), s32[]{:S(2)}) async-start(), calls=%async_computation.15 | async-start | bytes 7864320 | tf_op jit(solution)/shard_map/all_gather | solution.py:426
  121.8 155.6 %collective-permute-start = (bf16[6,1536,384]{2,1,0:T(8,128)(2,1)}, bf16[6,1536,384]{2,1,0:T(8,128)(2,1)}, u32[]{:S(2)}, u32[]{:S(2)}) collective-permute-start(bf16[6,1536,384]{2,1,0:T(8,128)(2,1)} %all-gather.7.cloned.1.call-done), channel_id=1, source_target_pairs={{0,16},{16,0},{1,17},{17,1},{2,18},{18,2},{3,19},{19,3},{4,20},{20... | collective-permute-start | bytes 21233672 | tf_op jit(solution)/shard_map/ppermute | solution.py:153
  154.6 189.2 %collective-permute-start.2 = (bf16[6,1536,384]{2,1,0:T(8,128)(2,1)}, bf16[6,1536,384]{2,1,0:T(8,128)(2,1)}, u32[]{:S(2)}, u32[]{:S(2)}) collective-permute-start(bf16[6,1536,384]{2,1,0:T(8,128)(2,1)} %all-gather.7.cloned.1.call-done), channel_id=1, source_target_pairs={{0,8},{8,0},{1,9},{9,1},{2,10},{10,2},{3,11},{11,3},{4,12},{12,4},... | collective-permute-start | bytes 21233672 | tf_op jit(solution)/shard_map/ppermute | solution.py:135
  174.8 150.9 %collective-permute-start.3 = (bf16[2,1536,384]{2,1,0:T(8,128)(2,1)}, bf16[2,1536,384]{2,1,0:T(8,128)(2,1)}, u32[]{:S(2)}, u32[]{:S(2)}) collective-permute-start(bf16[2,1536,384]{2,1,0:T(8,128)(2,1)} %all-gather.9.cloned.1.call-done), channel_id=1, source_target_pairs={{0,16},{16,0},{1,17},{17,1},{2,18},{18,2},{3,19},{19,3},{4,20},{20... | collective-permute-start | bytes 7077896 | tf_op jit(solution)/shard_map/ppermute | solution.py:153
  277.4 78.4 %collective-permute-start.1 = (bf16[6,1536,384]{2,1,0:T(8,128)(2,1)}, bf16[6,1536,384]{2,1,0:T(8,128)(2,1)}, u32[]{:S(2)}, u32[]{:S(2)}) collective-permute-start(bf16[6,1536,384]{2,1,0:T(8,128)(2,1)} %collective-permute-done), channel_id=1, source_target_pairs={{0,8},{8,0},{1,9},{9,1},{2,10},{10,2},{3,11},{11,3},{4,12},{12,4},... | collective-permute-start | bytes 21233672 | tf_op jit(solution)/shard_map/ppermute | solution.py:135
  325.7 232.4 %collective-permute-start.4 = (bf16[2,1536,384]{2,1,0:T(8,128)(2,1)}, bf16[2,1536,384]{2,1,0:T(8,128)(2,1)}, u32[]{:S(2)}, u32[]{:S(2)}) collective-permute-start(bf16[2,1536,384]{2,1,0:T(8,128)(2,1)} %collective-permute-done.3), channel_id=1, source_target_pairs={{0,8},{8,0},{1,9},{9,1},{2,10},{10,2},{3,11},{11,3},{4,12},{12,4},... | collective-permute-start | bytes 7077896 | tf_op jit(solution)/shard_map/ppermute | solution.py:135
  384.0 256.1 %collective-permute-start.6 = (bf16[1536,4480]{1,0:T(8,128)(2,1)}, bf16[1536,4480]{1,0:T(8,128)(2,1)}, u32[]{:S(2)}, u32[]{:S(2)}) collective-permute-start(bf16[1536,4480]{1,0:T(8,128)(2,1)} %all-gather.13.cloned.1.call-done), channel_id=1, source_target_pairs={{0,8},{8,0},{1,9},{9,1},{2,10},{10,2},{3,11},{11,3},{4,12},{12,4},... | collective-permute-start | bytes 41287688 | tf_op jit(solution)/shard_map/ppermute | solution.py:135
  415.1 145.0 %collective-permute-start.5 = (bf16[2,1536,384]{2,1,0:T(8,128)(2,1)}, bf16[2,1536,384]{2,1,0:T(8,128)(2,1)}, u32[]{:S(2)}, u32[]{:S(2)}) collective-permute-start(bf16[2,1536,384]{2,1,0:T(8,128)(2,1)} %all-gather.9.cloned.1.call-done), channel_id=1, source_target_pairs={{0,8},{8,0},{1,9},{9,1},{2,10},{10,2},{3,11},{11,3},{4,12},{12,4},... | collective-permute-start | bytes 7077896 | tf_op jit(solution)/shard_map/ppermute | solution.py:135
  434.5 123.4 %all-to-all-start.3 = ((bf16[2,384,384]{2,0,1:T(2,128)(2,1)}), bf16[2,384,384]{2,0,1:T(2,128)(2,1)S(1)}, u32[]{:S(2)}, u32[]{:S(2)}) async-start(bf16[2,384,384]{2,0,1:T(2,128)(2,1)} %copy.169), calls=%async_computation.3 | async-start | bytes 1179648 | tf_op jit(solution)/shard_map/all_to_all | solution.py:279
  438.0 473.8 %reduce-scatter.16.cloned.1.call-start = ((), (), s32[]{:S(2)}) async-start(), calls=%async_computation.22 | async-start | bytes 7864320
  557.9 97.3 %collective-permute-start.7 = (bf16[8960,768]{1,0:T(8,128)(2,1)}, bf16[8960,768]{1,0:T(8,128)(2,1)}, u32[]{:S(2)}, u32[]{:S(2)}) collective-permute-start(bf16[8960,768]{1,0:T(8,128)(2,1)} %all-gather.15.cloned.1.call-done), channel_id=1, source_target_pairs={{0,8},{8,0},{1,9},{9,1},{2,10},{10,2},{3,11},{11,3},{4,12},{12,4},... | collective-permute-start | bytes 41287688 | tf_op jit(solution)/shard_map/ppermute | solution.py:135
  728.7 28.7 %collective-permute-start.13 = (bf16[1536,4480]{1,0:T(8,128)(2,1)}, bf16[1536,4480]{1,0:T(8,128)(2,1)}, u32[]{:S(2)}, u32[]{:S(2)}) collective-permute-start(bf16[1536,4480]{1,0:T(8,128)(2,1)} %convolution_convert_fusion), channel_id=1, source_target_pairs={{0,8},{8,0},{1,9},{9,1},{2,10},{10,2},{3,11},{11,3},{4,12},{12,4},... | collective-permute-start | bytes 41287688 | tf_op jit(solution)/shard_map/ppermute | solution.py:135
  756.9 577.3 %reduce-scatter.12.cloned.1.call-start = ((), (), s32[]{:S(2)}) async-start(), calls=%async_computation.20 | async-start | bytes 15482880 | tf_op jit(solution)/shard_map/reduce_scatter | solution.py:217
  779.8 117.6 %collective-permute-start.17 = (bf16[8960,384]{1,0:T(8,128)(2,1)}, bf16[8960,384]{1,0:T(8,128)(2,1)}, u32[]{:S(2)}, u32[]{:S(2)}) collective-permute-start(bf16[8960,384]{1,0:T(8,128)(2,1)} %convolution_convert_fusion.1), channel_id=1, source_target_pairs={{0,8},{8,0},{1,9},{9,1},{2,10},{10,2},{3,11},{11,3},{4,12},{12,4},... | collective-permute-start | bytes 20643848 | tf_op jit(solution)/shard_map/ppermute | solution.py:135
  851.3 103.0 %collective-permute-start.16 = (bf16[8960,384]{1,0:T(8,128)(2,1)}, bf16[8960,384]{1,0:T(8,128)(2,1)}, u32[]{:S(2)}, u32[]{:S(2)}) collective-permute-start(bf16[8960,384]{1,0:T(8,128)(2,1)} %convolution_convert_fusion.2), channel_id=1, source_target_pairs={{0,8},{8,0},{1,9},{9,1},{2,10},{10,2},{3,11},{11,3},{4,12},{12,4},... | collective-permute-start | bytes 20643848 | tf_op jit(solution)/shard_map/ppermute | solution.py:135
  874.0 472.3 %reduce-scatter.14.cloned.1.call-start = ((), (), s32[]{:S(2)}) async-start(), calls=%async_computation.21 | async-start | bytes 7741440 | tf_op jit(solution)/shard_map/reduce_scatter | solution.py:206
  909.3 151.2 %collective-permute-start.18 = (bf16[8960,384]{1,0:T(8,128)(2,1)}, bf16[8960,384]{1,0:T(8,128)(2,1)}, u32[]{:S(2)}, u32[]{:S(2)}) collective-permute-start(bf16[8960,384]{1,0:T(8,128)(2,1)} %add_convert_fusion.4), channel_id=1, source_target_pairs={{0,16},{16,0},{1,17},{17,1},{2,18},{18,2},{3,19},{19,3},{4,20},{20... | collective-permute-start | bytes 20643848 | tf_op jit(solution)/shard_map/ppermute | solution.py:153
  927.9 147.9 %collective-permute-start.9 = (bf16[8,1536,384]{2,1,0:T(8,128)(2,1)}, bf16[8,1536,384]{2,1,0:T(8,128)(2,1)}, u32[]{:S(2)}, u32[]{:S(2)}) collective-permute-start(bf16[8,1536,384]{2,1,0:T(8,128)(2,1)} %fusion.101), channel_id=1, source_target_pairs={{0,8},{8,0},{1,9},{9,1},{2,10},{10,2},{3,11},{11,3},{4,12},{12,4},... | collective-permute-start | bytes 28311560 | tf_op jit(solution)/shard_map/ppermute | solution.py:135
  1069.9 399.7 %reduce-scatter.10.cloned.1.call-start = ((), (), s32[]{:S(2)}) async-start(), calls=%async_computation.19 | async-start | bytes 10616832 | tf_op jit(solution)/shard_map/reduce_scatter | solution.py:206
  1090.1 205.5 %collective-permute-start.10 = (bf16[8,1536,384]{2,1,0:T(8,128)(2,1)}, bf16[8,1536,384]{2,1,0:T(8,128)(2,1)}, u32[]{:S(2)}, u32[]{:S(2)}) collective-permute-start(bf16[8,1536,384]{2,1,0:T(8,128)(2,1)} %add_convert_fusion.2), channel_id=1, source_target_pairs={{0,16},{16,0},{1,17},{17,1},{2,18},{18,2},{3,19},{19,3},{4,20},{20... | collective-permute-start | bytes 28311560 | tf_op jit(solution)/shard_map/ppermute | solution.py:153
  1306.5 229.2 %reduce-scatter.18.cloned.1.call-start = ((), (), s32[]{:S(2)}) async-start(), calls=%async_computation.23 | async-start | bytes 884736
  1334.2 40.8 %collective-permute-start.14 = (bf16[192,4480]{1,0:T(8,128)(2,1)}, bf16[192,4480]{1,0:T(8,128)(2,1)}, u32[]{:S(2)}, u32[]{:S(2)}) collective-permute-start(bf16[192,4480]{1,0:T(8,128)(2,1)} %reduce-scatter.12.cloned.1.call-done), channel_id=1, source_target_pairs={{0,16},{16,0},{1,17},{17,1},{2,18},{18,2},{3,19},{19,3},{4,20},{20... | collective-permute-start | bytes 5160968 | tf_op jit(solution)/shard_map/ppermute | solution.py:153
  1338.0 231.4 %all-reduce.12.cloned.1.call-start = ((), (), s32[]{:S(2)}) async-start(), calls=%async_computation.18 | async-start | bytes 196608 | tf_op jit(solution)/shard_map/psum | solution.py:243
  1346.3 45.7 %collective-permute-start.19 = (bf16[1120,384]{1,0:T(8,128)(2,1)}, bf16[1120,384]{1,0:T(8,128)(2,1)S(1)}, u32[]{:S(2)}, u32[]{:S(2)}) collective-permute-start(bf16[1120,384]{1,0:T(8,128)(2,1)} %reduce-scatter.14.cloned.1.call-done), channel_id=1, source_target_pairs={{0,16},{16,0},{1,17},{17,1},{2,18},{18,2},{3,19},{19,3},{4,20},{20... | collective-permute-start | bytes 2580488 | tf_op jit(solution)/shard_map/ppermute | solution.py:153
  1379.2 202.5 %collective-permute-start.15 = (f32[192,4480]{1,0:T(8,128)}, f32[192,4480]{1,0:T(8,128)}, u32[]{:S(2)}, u32[]{:S(2)}) collective-permute-start(f32[192,4480]{1,0:T(8,128)} %convert_add_fusion), channel_id=1, source_target_pairs={{0,8},{8,0},{1,9},{9,1},{2,10},{10,2},{3,11},{11,3},{4,12},{12,4},... | collective-permute-start | bytes 10321928 | tf_op jit(solution)/shard_map/ppermute | solution.py:135
  1394.0 182.6 %collective-permute-start.20 = (bf16[1120,768]{1,0:T(8,128)(2,1)}, bf16[1120,768]{1,0:T(8,128)(2,1)}, u32[]{:S(2)}, u32[]{:S(2)}) collective-permute-start(bf16[1120,768]{1,0:T(8,128)(2,1)} %fusion.130), channel_id=1, source_target_pairs={{0,8},{8,0},{1,9},{9,1},{2,10},{10,2},{3,11},{11,3},{4,12},{12,4},... | collective-permute-start | bytes 5160968 | tf_op jit(solution)/shard_map/ppermute | solution.py:135
  1469.6 68.0 %collective-permute-start.11 = (bf16[8,192,384]{2,1,0:T(8,128)(2,1)}, bf16[8,192,384]{2,1,0:T(8,128)(2,1)}, u32[]{:S(2)}, u32[]{:S(2)}) collective-permute-start(bf16[8,192,384]{2,1,0:T(8,128)(2,1)} %reduce-scatter.10.cloned.1.call-done), channel_id=1, source_target_pairs={{0,16},{16,0},{1,17},{17,1},{2,18},{18,2},{3,19},{19,3},{4,20},{20... | collective-permute-start | bytes 3538952 | tf_op jit(solution)/shard_map/ppermute | solution.py:153
  1540.4 46.7 %collective-permute-start.12 = (bf16[8,192,768]{2,1,0:T(8,128)(2,1)S(1)}, bf16[8,192,768]{2,1,0:T(8,128)(2,1)}, u32[]{:S(2)}, u32[]{:S(2)}) collective-permute-start(bf16[8,192,768]{2,1,0:T(8,128)(2,1)S(1)} %fusion.110), channel_id=1, source_target_pairs={{0,8},{8,0},{1,9},{9,1},{2,10},{10,2},{3,11},{11,3},{4,12},{12,4},... | collective-permute-start | bytes 7077896 | tf_op jit(solution)/shard_map/ppermute | solution.py:135
  (205 other events, 2662.3 us)
Sparse Core Ops, SparseCore 0:
  10.8 110.9 all-gather.6
  124.6 50.1 all-gather.8
  177.6 188.9 all-gather.12
  369.2 188.6 all-gather.14
  559.9 45.3 all-gather.10
  757.0 60.5 reduce-scatter.15
  821.2 224.1 reduce-scatter.11
  1070.0 127.8 reduce-scatter.13
  1306.6 162.9 reduce-scatter.9
  1473.3 62.3 reduce-scatter.17
  1538.6 30.7 all-reduce.11

commit v11 on v10

--- a/solution.py
+++ b/solution.py
@@ -390,7 +390,7 @@
     heads_in = self_in.shape[0]
     attn_in_parts = fetch_split(jnp.concatenate([self_in, cross_in], axis=0), 1, spot)
     attn_out_parts = fetch_split(jnp.stack([self_out, cross_out]), 1, spot)
-    ffn_in_parts = fetch_split(ffn_in, 0, spot, quarters=False)
+    ffn_in_parts = fetch_split(ffn_in, 0, spot)
     ffn_out_parts = fetch_split(ffn_out, 0, spot, quarters=False)
     modulation_full, gains_full, biases_full, ffn_bias_full = fetch_small(modulation, gains, biases, ffn_bias)
     in_split = [Split(tuple(part[i] for part in attn_in_parts), spot) for i in range(2 * heads_in)]

time: 1620 us -> 1610 us (level)
  waiting for transfers between devices: 944 us -> 897 us
  local copies, waits for them, and re-layouts: 127 us -> 162 us
    all_gather x2 -> x1, waiting for transfers between devices: 120 us -> 0.01 us  [fetch_split(): mine = lax.all_gather(part, 'fsdp', axis=gather_axis, tiled=True)]
    all_to_all x1, waiting for transfers between devices: 6.07 us -> 90.9 us  [micro_step(): lax.all_to_all(turned[0].astype(jnp.bfloat16), SEQ, split_axis=2, concat_...]
    all_gather x1, waiting for transfers between devices: 30.5 us -> 0.02 us  [body(): all_kv = lax.all_gather(local_kv, SEQ, axis=0, tiled=True)]
    dot_general x36 -> x38, matrix products: 78.2 us -> 92 us  [matmul(): return jnp.dot(operand, factor, preferred_element_type=jnp.float32)]
    dot_general x36 -> x38, matrix products: 119 us -> 116 us  [outer_cols(): lax.dot_general(operand, factor, (((operand.ndim - 1,), (1,)), ((), ())),...]
    unnamed x403 -> x391, local copies, waits for them, and re-layouts: 35.8 us -> 37.4 us
    all_gather x2 -> x3, waiting for transfers between devices: 124 us -> 126 us  [fetch_split(): own = lax.all_gather(part, 'fsdp', axis=gather_axis, tiled=True)]
    ppermute x7 -> x8, waiting for transfers between devices: 481 us -> 481 us  [swap_y(): return lax.ppermute(tensor, 'y', SWAP)]
  transfers between devices with their start and end apart: 40 -> 42, of which waited for: 18 -> 17; matrix products, arithmetic and copies ran while one was open for 29% -> 32% of each run, Pallas kernels for 0% -> 0%
where the time goes in v11:
time: 1610 us; the launch traced here: 1600 us
  waiting for transfers between devices  897 us (56%)
  matrix products  330 us (20%)
  local copies, waits for them, and re-layouts  162 us (10%)
  other arithmetic  116 us (7%)
  starting transfers between devices  47.9 us (3%)
  blocking collectives  30.8 us (2%)
  between operations  17.6 us (1%)
    ppermute x8, waiting for transfers between devices, swap_y(): return lax.ppermute(tensor, 'y', SWAP)  481 us
    all_gather x3, waiting for transfers between devices, fetch_split(): own = lax.all_gather(part, 'fsdp', axis=gather_axis, tiled=True)  126 us
    dot_general x38, matrix products, outer_cols(): lax.dot_general(operand, factor, (((operand.ndim - 1,), (1,)), ((), ())),...  116 us
    dot_general x38, matrix products, inner_rows(): lax.dot_general(operand, factor, (((0,), (0,)), ((), ())), preferred_elem...  99.6 us
    dot_general x38, matrix products, matmul(): return jnp.dot(operand, factor, preferred_element_type=jnp.float32)  92 us
    all_to_all x1, waiting for transfers between devices, micro_step(): lax.all_to_all(turned[0].astype(jnp.bfloat16), SEQ, split_axis=2, concat_...  90.9 us
    reduce_scatter x2, waiting for transfers between devices, reduce_split(): lax.psum_scatter(total, 'fsdp', scatter_dimension=scatter_axis, tiled=True)  75.7 us
    unnamed x13, waiting for transfers between devices  55.5 us
  transfers between devices with their start and end apart: 42, of which 17 were waited for; matrix products, arithmetic and copies ran while one was open for 32% of the time, Pallas kernels for 0%

profile of v11, /device:TPU:0, one launch (start us, length us, event | category | flops | bytes accessed | tf_op | source)
XLA Modules:
  0.0 1602.5 jit_solution(10152955822676128676)
XLA Ops:
  15.4 106.4 %all-gather.7.cloned.1.call-done = bf16[6,1536,384]{2,1,0:T(8,128)(2,1)} async-done(((bf16[6,192,384]{2,1,0:T(8,128)(2,1)}), bf16[6,1536,384]{2,1,0:T(8,128)(2,1)}) %all-gather.7.cloned.1.call-update) | async-done | bytes 7077904 | tf_op jit(solution)/shard_map/all_gather | solution.py:193
  123.4 30.8 %all-gather = bf16[8,192,27]{1,2,0:T(8,128)(2,1)S(1)} all-gather(bf16[1,192,27]{1,2,0:T(8,128)(2,1)S(1)} %maximum_bitcast_fusion), channel_id=1, replica_groups=mesh['y'=2,'core'=2,'fsdp'=8] {'fsdp'}, dimensions={0}, use_global_device_ids=true | all-gather | bytes 93312 | tf_op jit(solution)/shard_map/all_gather | solution.py:228
  155.3 19.5 %all-gather.9.cloned.1.call-done = bf16[2,1536,384]{2,1,0:T(8,128)(2,1)} async-done(((bf16[2,192,384]{2,1,0:T(8,128)(2,1)}), bf16[2,1536,384]{2,1,0:T(8,128)(2,1)}) %all-gather.9.cloned.1.call-update) | async-done | bytes 2359312 | tf_op jit(solution)/shard_map/all_gather | solution.py:193
  176.2 101.1 %collective-permute-done = bf16[6,1536,384]{2,1,0:T(8,128)(2,1)} collective-permute-done((bf16[6,1536,384]{2,1,0:T(8,128)(2,1)}, bf16[6,1536,384]{2,1,0:T(8,128)(2,1)}, u32[]{:S(2)}, u32[]{:S(2)}) %collective-permute-start) | collective-permute-done | bytes 7077920 | tf_op jit(solution)/shard_map/ppermute | solution.py:153
  282.5 43.2 %collective-permute-done.3 = bf16[2,1536,384]{2,1,0:T(8,128)(2,1)} collective-permute-done((bf16[2,1536,384]{2,1,0:T(8,128)(2,1)}, bf16[2,1536,384]{2,1,0:T(8,128)(2,1)}, u32[]{:S(2)}, u32[]{:S(2)}) %collective-permute-start.3) | collective-permute-done | bytes 2359328 | tf_op jit(solution)/shard_map/ppermute | solution.py:153
  325.7 10.6 copy.187
  382.0 10.9 fusion.515
  414.0 90.9 %all-to-all-done.1 = bf16[2,96,1536]{1,0,2:T(2,128)(2,1)S(1)} async-done(((bf16[2,96,1536]{1,0,2:T(2,128)(2,1)}), bf16[2,96,1536]{1,0,2:T(2,128)(2,1)S(1)}, u32[]{:S(2)}, u32[]{:S(2)}) %all-to-all-start.1) | async-done | bytes 589856 | tf_op jit(solution)/shard_map/all_to_all | solution.py:274
  512.6 16.6 %all-to-all-done.2 = bf16[2,96,1536]{1,0,2:T(2,128)(2,1)S(1)} async-done(((bf16[2,96,1536]{1,0,2:T(2,128)(2,1)}), bf16[2,96,1536]{1,0,2:T(2,128)(2,1)S(1)}, u32[]{:S(2)}, u32[]{:S(2)}) %all-to-all-start.2) | async-done | bytes 589856 | tf_op jit(solution)/shard_map/all_to_all | solution.py:275
  537.1 9.2 all-to-all-done
  558.7 8.3 all-to-all-done.3
  665.0 7.8 fusion.6
  674.9 12.6 fusion
  687.6 13.6 convert_reduce_fusion
  701.2 6.7 fusion.11
  724.2 7.0 convolution_convert_fusion
  751.1 8.7 copy.238
  760.0 15.4 add_convert_fusion
  775.5 6.8 convolution_convert_fusion.1
  815.5 8.5 all-to-all-done.4
  845.9 6.7 convolution_convert_fusion.2
  898.9 12.0 add_convert_fusion.4
  955.6 106.5 %collective-permute-done.20 = bf16[8960,384]{1,0:T(8,128)(2,1)} collective-permute-done((bf16[8960,384]{1,0:T(8,128)(2,1)}, bf16[8960,384]{1,0:T(8,128)(2,1)}, u32[]{:S(2)}, u32[]{:S(2)}) %collective-permute-start.20) | collective-permute-done | bytes 6881312 | tf_op jit(solution)/shard_map/ppermute | solution.py:153
  1062.1 9.3 add_convert_fusion.3
  1076.5 13.8 add_convert_fusion.2
  1103.8 192.1 %collective-permute-done.12 = bf16[8,1536,384]{2,1,0:T(8,128)(2,1)} collective-permute-done((bf16[8,1536,384]{2,1,0:T(8,128)(2,1)}, bf16[8,1536,384]{2,1,0:T(8,128)(2,1)}, u32[]{:S(2)}, u32[]{:S(2)}) %collective-permute-start.12) | collective-permute-done | bytes 9437216 | tf_op jit(solution)/shard_map/ppermute | solution.py:153
  1295.9 10.7 add_convert_fusion.1
  1347.3 28.0 %collective-permute-done.16 = bf16[192,4480]{1,0:T(8,128)(2,1)} collective-permute-done((bf16[192,4480]{1,0:T(8,128)(2,1)}, bf16[192,4480]{1,0:T(8,128)(2,1)}, u32[]{:S(2)}, u32[]{:S(2)}) %collective-permute-start.16) | collective-permute-done | bytes 1720352 | tf_op jit(solution)/shard_map/ppermute | solution.py:153
  1382.6 9.6 collective-permute-done.21
  1394.2 75.7 %reduce-scatter.10.cloned.1.call-done = bf16[8,192,384]{2,1,0:T(8,128)(2,1)} async-done(((bf16[8,1536,384]{2,1,0:T(8,128)(2,1)}), bf16[8,192,384]{2,1,0:T(8,128)(2,1)}) %reduce-scatter.10.cloned.1.call-update) | async-done | bytes 1179664 | tf_op jit(solution)/shard_map/reduce_scatter | solution.py:206
  1480.7 55.3 %reduce-scatter.18.cloned.1.call-done = f32[192,27]{1,0:T(8,128)} async-done(((f32[1536,27]{1,0:T(8,128)}), f32[192,27]{1,0:T(8,128)}) %reduce-scatter.18.cloned.1.call-update) | async-done | bytes 20752
  1543.9 25.7 %all-reduce.12.cloned.1.call-done = f32[23616]{0:T(1024)} async-done(((f32[23616]{0:T(1024)}), f32[23616]{0:T(1024)}) %all-reduce.12.cloned.1.call-update) | async-done | bytes 94480 | tf_op jit(solution)/shard_map/psum | solution.py:243
  (814 shorter events, 504.7 us)
Async XLA Ops:
  7.2 114.6 %all-gather.7.cloned.1.call-start = ((), (), s32[]{:S(2)}) async-start(), calls=%async_computation.13 | async-start | bytes 7962624 | tf_op jit(solution)/shard_map/all_gather | solution.py:193
  9.6 165.2 %all-gather.9.cloned.1.call-start = ((), (), s32[]{:S(2)}) async-start(), calls=%async_computation.14 | async-start | bytes 2654208 | tf_op jit(solution)/shard_map/all_gather | solution.py:193
  11.4 314.3 %all-gather.13.cloned.1.call-start = ((), (), s32[]{:S(2)}) async-start(), calls=%async_computation.16 | async-start | bytes 7962624 | tf_op jit(solution)/shard_map/all_gather | solution.py:193
  13.9 544.4 %all-gather.15.cloned.1.call-start = ((), (), s32[]{:S(2)}) async-start(), calls=%async_computation.17 | async-start | bytes 15482880 | tf_op jit(solution)/shard_map/all_gather | solution.py:189
  15.3 568.3 %all-gather.11.cloned.1.call-start = ((), (), s32[]{:S(2)}) async-start(), calls=%async_computation.15 | async-start | bytes 7864320 | tf_op jit(solution)/shard_map/all_gather | solution.py:426
  121.8 155.6 %collective-permute-start = (bf16[6,1536,384]{2,1,0:T(8,128)(2,1)}, bf16[6,1536,384]{2,1,0:T(8,128)(2,1)}, u32[]{:S(2)}, u32[]{:S(2)}) collective-permute-start(bf16[6,1536,384]{2,1,0:T(8,128)(2,1)} %all-gather.7.cloned.1.call-done), channel_id=1, source_target_pairs={{0,16},{16,0},{1,17},{17,1},{2,18},{18,2},{3,19},{19,3},{4,20},{20... | collective-permute-start | bytes 21233672 | tf_op jit(solution)/shard_map/ppermute | solution.py:153
  154.6 202.7 %collective-permute-start.2 = (bf16[6,1536,384]{2,1,0:T(8,128)(2,1)}, bf16[6,1536,384]{2,1,0:T(8,128)(2,1)}, u32[]{:S(2)}, u32[]{:S(2)}) collective-permute-start(bf16[6,1536,384]{2,1,0:T(8,128)(2,1)} %all-gather.7.cloned.1.call-done), channel_id=1, source_target_pairs={{0,8},{8,0},{1,9},{9,1},{2,10},{10,2},{3,11},{11,3},{4,12},{12,4},... | collective-permute-start | bytes 21233672 | tf_op jit(solution)/shard_map/ppermute | solution.py:135
  174.8 150.9 %collective-permute-start.3 = (bf16[2,1536,384]{2,1,0:T(8,128)(2,1)}, bf16[2,1536,384]{2,1,0:T(8,128)(2,1)}, u32[]{:S(2)}, u32[]{:S(2)}) collective-permute-start(bf16[2,1536,384]{2,1,0:T(8,128)(2,1)} %all-gather.9.cloned.1.call-done), channel_id=1, source_target_pairs={{0,16},{16,0},{1,17},{17,1},{2,18},{18,2},{3,19},{19,3},{4,20},{20... | collective-permute-start | bytes 7077896 | tf_op jit(solution)/shard_map/ppermute | solution.py:153
  277.4 92.4 %collective-permute-start.1 = (bf16[6,1536,384]{2,1,0:T(8,128)(2,1)}, bf16[6,1536,384]{2,1,0:T(8,128)(2,1)}, u32[]{:S(2)}, u32[]{:S(2)}) collective-permute-start(bf16[6,1536,384]{2,1,0:T(8,128)(2,1)} %collective-permute-done), channel_id=1, source_target_pairs={{0,8},{8,0},{1,9},{9,1},{2,10},{10,2},{3,11},{11,3},{4,12},{12,4},... | collective-permute-start | bytes 21233672 | tf_op jit(solution)/shard_map/ppermute | solution.py:135
  325.7 241.5 %collective-permute-start.4 = (bf16[2,1536,384]{2,1,0:T(8,128)(2,1)}, bf16[2,1536,384]{2,1,0:T(8,128)(2,1)}, u32[]{:S(2)}, u32[]{:S(2)}) collective-permute-start(bf16[2,1536,384]{2,1,0:T(8,128)(2,1)} %collective-permute-done.3), channel_id=1, source_target_pairs={{0,8},{8,0},{1,9},{9,1},{2,10},{10,2},{3,11},{11,3},{4,12},{12,4},... | collective-permute-start | bytes 7077896 | tf_op jit(solution)/shard_map/ppermute | solution.py:135
  336.3 221.9 %collective-permute-start.6 = (bf16[1536,2240]{0,1:T(8,128)(2,1)}, bf16[1536,2240]{0,1:T(8,128)(2,1)}, u32[]{:S(2)}, u32[]{:S(2)}) collective-permute-start(bf16[1536,2240]{0,1:T(8,128)(2,1)} %copy.187), channel_id=1, source_target_pairs={{0,16},{16,0},{1,17},{17,1},{2,18},{18,2},{3,19},{19,3},{4,20},{20... | collective-permute-start | bytes 20643848 | tf_op jit(solution)/shard_map/ppermute | solution.py:153
  405.4 99.6 %all-to-all-start.1 = ((bf16[2,96,1536]{1,0,2:T(2,128)(2,1)}), bf16[2,96,1536]{1,0,2:T(2,128)(2,1)S(1)}, u32[]{:S(2)}, u32[]{:S(2)}) async-start(bf16[2,96,1536]{1,0,2:T(2,128)(2,1)} %copy.170), calls=%async_computation.1 | async-start | bytes 1572864 | tf_op jit(solution)/shard_map/all_to_all | solution.py:274
  557.6 355.8 %reduce-scatter.16.cloned.1.call-start = ((), (), s32[]{:S(2)}) async-start(), calls=%async_computation.22 | async-start | bytes 7864320
  557.7 65.4 %collective-permute-start.8 = (bf16[1536,2240]{0,1:T(8,128)(2,1)}, bf16[1536,2240]{0,1:T(8,128)(2,1)}, u32[]{:S(2)}, u32[]{:S(2)}) collective-permute-start(bf16[1536,2240]{0,1:T(8,128)(2,1)} %copy.187), channel_id=1, source_target_pairs={{0,8},{8,0},{1,9},{9,1},{2,10},{10,2},{3,11},{11,3},{4,12},{12,4},... | collective-permute-start | bytes 20643848 | tf_op jit(solution)/shard_map/ppermute | solution.py:135
  558.2 58.2 %collective-permute-start.7 = (bf16[1536,2240]{0,1:T(8,128)(2,1)}, bf16[1536,2240]{0,1:T(8,128)(2,1)}, u32[]{:S(2)}, u32[]{:S(2)}) collective-permute-start(bf16[1536,2240]{0,1:T(8,128)(2,1)} %collective-permute-done.6), channel_id=1, source_target_pairs={{0,8},{8,0},{1,9},{9,1},{2,10},{10,2},{3,11},{11,3},{4,12},{12,4},... | collective-permute-start | bytes 20643848 | tf_op jit(solution)/shard_map/ppermute | solution.py:135
  558.3 106.7 %collective-permute-start.9 = (bf16[8960,768]{1,0:T(8,128)(2,1)}, bf16[8960,768]{1,0:T(8,128)(2,1)}, u32[]{:S(2)}, u32[]{:S(2)}) collective-permute-start(bf16[8960,768]{1,0:T(8,128)(2,1)} %all-gather.15.cloned.1.call-done), channel_id=1, source_target_pairs={{0,8},{8,0},{1,9},{9,1},{2,10},{10,2},{3,11},{11,3},{4,12},{12,4},... | collective-permute-start | bytes 41287688 | tf_op jit(solution)/shard_map/ppermute | solution.py:135
  759.8 574.7 %reduce-scatter.12.cloned.1.call-start = ((), (), s32[]{:S(2)}) async-start(), calls=%async_computation.20 | async-start | bytes 15482880 | tf_op jit(solution)/shard_map/reduce_scatter | solution.py:217
  782.3 116.6 %collective-permute-start.19 = (bf16[8960,384]{1,0:T(8,128)(2,1)}, bf16[8960,384]{1,0:T(8,128)(2,1)}, u32[]{:S(2)}, u32[]{:S(2)}) collective-permute-start(bf16[8960,384]{1,0:T(8,128)(2,1)} %convolution_convert_fusion.1), channel_id=1, source_target_pairs={{0,8},{8,0},{1,9},{9,1},{2,10},{10,2},{3,11},{11,3},{4,12},{12,4},... | collective-permute-start | bytes 20643848 | tf_op jit(solution)/shard_map/ppermute | solution.py:135
  852.6 103.0 %collective-permute-start.18 = (bf16[8960,384]{1,0:T(8,128)(2,1)}, bf16[8960,384]{1,0:T(8,128)(2,1)}, u32[]{:S(2)}, u32[]{:S(2)}) collective-permute-start(bf16[8960,384]{1,0:T(8,128)(2,1)} %convolution_convert_fusion.2), channel_id=1, source_target_pairs={{0,8},{8,0},{1,9},{9,1},{2,10},{10,2},{3,11},{11,3},{4,12},{12,4},... | collective-permute-start | bytes 20643848 | tf_op jit(solution)/shard_map/ppermute | solution.py:135
  875.4 471.3 %reduce-scatter.14.cloned.1.call-start = ((), (), s32[]{:S(2)}) async-start(), calls=%async_computation.21 | async-start | bytes 7741440 | tf_op jit(solution)/shard_map/reduce_scatter | solution.py:206
  911.0 151.2 %collective-permute-start.20 = (bf16[8960,384]{1,0:T(8,128)(2,1)}, bf16[8960,384]{1,0:T(8,128)(2,1)}, u32[]{:S(2)}, u32[]{:S(2)}) collective-permute-start(bf16[8960,384]{1,0:T(8,128)(2,1)} %add_convert_fusion.4), channel_id=1, source_target_pairs={{0,16},{16,0},{1,17},{17,1},{2,18},{18,2},{3,19},{19,3},{4,20},{20... | collective-permute-start | bytes 20643848 | tf_op jit(solution)/shard_map/ppermute | solution.py:153
  929.3 147.2 %collective-permute-start.11 = (bf16[8,1536,384]{2,1,0:T(8,128)(2,1)}, bf16[8,1536,384]{2,1,0:T(8,128)(2,1)}, u32[]{:S(2)}, u32[]{:S(2)}) collective-permute-start(bf16[8,1536,384]{2,1,0:T(8,128)(2,1)} %fusion.109), channel_id=1, source_target_pairs={{0,8},{8,0},{1,9},{9,1},{2,10},{10,2},{3,11},{11,3},{4,12},{12,4},... | collective-permute-start | bytes 28311560 | tf_op jit(solution)/shard_map/ppermute | solution.py:135
  1071.4 398.4 %reduce-scatter.10.cloned.1.call-start = ((), (), s32[]{:S(2)}) async-start(), calls=%async_computation.19 | async-start | bytes 10616832 | tf_op jit(solution)/shard_map/reduce_scatter | solution.py:206
  1090.3 205.6 %collective-permute-start.12 = (bf16[8,1536,384]{2,1,0:T(8,128)(2,1)}, bf16[8,1536,384]{2,1,0:T(8,128)(2,1)}, u32[]{:S(2)}, u32[]{:S(2)}) collective-permute-start(bf16[8,1536,384]{2,1,0:T(8,128)(2,1)} %add_convert_fusion.2), channel_id=1, source_target_pairs={{0,16},{16,0},{1,17},{17,1},{2,18},{18,2},{3,19},{19,3},{4,20},{20... | collective-permute-start | bytes 28311560 | tf_op jit(solution)/shard_map/ppermute | solution.py:153
  1306.7 229.2 %reduce-scatter.18.cloned.1.call-start = ((), (), s32[]{:S(2)}) async-start(), calls=%async_computation.23 | async-start | bytes 884736
  1334.5 40.8 %collective-permute-start.16 = (bf16[192,4480]{1,0:T(8,128)(2,1)}, bf16[192,4480]{1,0:T(8,128)(2,1)}, u32[]{:S(2)}, u32[]{:S(2)}) collective-permute-start(bf16[192,4480]{1,0:T(8,128)(2,1)} %reduce-scatter.12.cloned.1.call-done), channel_id=1, source_target_pairs={{0,16},{16,0},{1,17},{17,1},{2,18},{18,2},{3,19},{19,3},{4,20},{20... | collective-permute-start | bytes 5160968 | tf_op jit(solution)/shard_map/ppermute | solution.py:153
  1338.4 231.2 %all-reduce.12.cloned.1.call-start = ((), (), s32[]{:S(2)}) async-start(), calls=%async_computation.18 | async-start | bytes 196608 | tf_op jit(solution)/shard_map/psum | solution.py:243
  1346.7 45.5 %collective-permute-start.21 = (bf16[1120,384]{1,0:T(8,128)(2,1)}, bf16[1120,384]{1,0:T(8,128)(2,1)S(1)}, u32[]{:S(2)}, u32[]{:S(2)}) collective-permute-start(bf16[1120,384]{1,0:T(8,128)(2,1)} %reduce-scatter.14.cloned.1.call-done), channel_id=1, source_target_pairs={{0,16},{16,0},{1,17},{17,1},{2,18},{18,2},{3,19},{19,3},{4,20},{20... | collective-permute-start | bytes 2580488 | tf_op jit(solution)/shard_map/ppermute | solution.py:153
  1379.5 202.5 %collective-permute-start.17 = (f32[192,4480]{1,0:T(8,128)}, f32[192,4480]{1,0:T(8,128)}, u32[]{:S(2)}, u32[]{:S(2)}) collective-permute-start(f32[192,4480]{1,0:T(8,128)} %convert_add_fusion), channel_id=1, source_target_pairs={{0,8},{8,0},{1,9},{9,1},{2,10},{10,2},{3,11},{11,3},{4,12},{12,4},... | collective-permute-start | bytes 10321928 | tf_op jit(solution)/shard_map/ppermute | solution.py:135
  1394.2 182.7 %collective-permute-start.22 = (bf16[1120,768]{1,0:T(8,128)(2,1)}, bf16[1120,768]{1,0:T(8,128)(2,1)}, u32[]{:S(2)}, u32[]{:S(2)}) collective-permute-start(bf16[1120,768]{1,0:T(8,128)(2,1)} %fusion.144), channel_id=1, source_target_pairs={{0,8},{8,0},{1,9},{9,1},{2,10},{10,2},{3,11},{11,3},{4,12},{12,4},... | collective-permute-start | bytes 5160968 | tf_op jit(solution)/shard_map/ppermute | solution.py:135
  1469.9 67.9 %collective-permute-start.13 = (bf16[8,192,384]{2,1,0:T(8,128)(2,1)}, bf16[8,192,384]{2,1,0:T(8,128)(2,1)}, u32[]{:S(2)}, u32[]{:S(2)}) collective-permute-start(bf16[8,192,384]{2,1,0:T(8,128)(2,1)} %reduce-scatter.10.cloned.1.call-done), channel_id=1, source_target_pairs={{0,16},{16,0},{1,17},{17,1},{2,18},{18,2},{3,19},{19,3},{4,20},{20... | collective-permute-start | bytes 3538952 | tf_op jit(solution)/shard_map/ppermute | solution.py:153
  1540.7 46.7 %collective-permute-start.14 = (bf16[8,192,768]{2,1,0:T(8,128)(2,1)S(1)}, bf16[8,192,768]{2,1,0:T(8,128)(2,1)}, u32[]{:S(2)}, u32[]{:S(2)}) collective-permute-start(bf16[8,192,768]{2,1,0:T(8,128)(2,1)S(1)} %fusion.124), channel_id=1, source_target_pairs={{0,8},{8,0},{1,9},{9,1},{2,10},{10,2},{3,11},{11,3},{4,12},{12,4},... | collective-permute-start | bytes 7077896 | tf_op jit(solution)/shard_map/ppermute | solution.py:135
  (201 other events, 3932.3 us)
Sparse Core Ops, SparseCore 0:
  10.8 110.9 all-gather.6
  124.6 50.1 all-gather.8
  177.6 106.7 all-gather.12
  287.0 188.6 all-gather.14
  477.7 63.4 all-gather.10
  759.9 57.5 reduce-scatter.15
  821.2 225.6 reduce-scatter.11
  1071.6 127.8 reduce-scatter.13
  1306.9 162.9 reduce-scatter.9
  1473.6 62.3 reduce-scatter.17
  1538.9 30.7 all-reduce.11
